TPU v7x, 32 devices: a whole 2x2x4 slice. The times are simulated.
32 devices in a mesh: groups: 2 (over y), expert: 4 (over z), tensor: 4 (over x, core).
Axes of the slice: x: 2, y: 2, z: 4, core: 2. Of those that a mesh axis runs over, the one named last changes fastest.
Arguments:
- kv_prefill: bfloat16 [32, 512, 2, 1024], P('groups', 'expert', None, 'tensor'), parts along dimension 0, may hold values from -8 to 8
- slot_of: int32 [32], P('groups'), parts along dimension 0, may hold values from 0 to 15, as said below
- lengths: int32 [32], P('groups'), parts along dimension 0, may hold values from 2 to 512
- query: bfloat16 [32, 4096], P(('groups', 'expert'), 'tensor'), parts along dimension 0, may hold values from -100 to 100
- new_kv: bfloat16 [32, 2, 1024], P(('groups', 'expert'), None, 'tensor'), parts along dimension 0, may hold values from -6 to 6
- wo: bfloat16 [4096, 4096], P('tensor', 'expert'), may hold values from -0.09375 to 0.09375
- resid: bfloat16 [32, 4096], P('groups', 'expert'), parts along dimension 0, may hold values from -60 to 60
- norm_gain: bfloat16 [4096], P('expert'), may hold values from 0.25 to 1.75
- expert_ids: int32 [32, 2], P('groups'), parts along dimension 0, may hold values from 0 to 3, all different within a row; in each aligned block of 16 rows (0 to 15, 16 to 31, ...) at most 12 rows name the same one
- gate_logits: float32 [32, 2], P('groups'), parts along dimension 0, may hold values from -6 to 6
- gate_weight_slabs: bfloat16 [4, 4096, 8192], P('expert', None, 'tensor'), may hold values from -0.09375 to 0.09375
- w_up: bfloat16 [4, 4096, 8192], P('expert', None, 'tensor'), may hold values from -0.09375 to 0.09375
- w_down: bfloat16 [4, 8192, 4096], P('expert', 'tensor'), may hold values from -0.0625 to 0.0625
Outputs:
- attn_out: bfloat16 [32, 4096], P('groups', 'expert'), parts along dimension 0
- moe_out: bfloat16 [32, 4096], P(('groups', 'tensor'), 'expert'), parts along dimension 0
There are 2 independent parts, one for each index of `groups`. A program takes and returns all parts, laid end to end along the dimension named above; an argument that names none is the same for every part. Nothing has to cross between parts.
Inputs may be any that keep to these rules, and one draw needn't show every extreme that they name: `slot_of`: a permutation of 0 to 15. `expert_ids`: each expert is named by at most 12 tokens, one of them by exactly 12; no token names an expert twice.
All inputs are finite; a program needn't handle non-finite values.
Results may differ from a plain program's by a relative error of at most 0.023.
Values may be sent and summed in bfloat16 or wider, within the bound.
No kernel may reach another device: no remote copies, remote signals or barrier semaphores. Data moves between devices by JAX's collectives and lax.ppermute only.
A program may use at most 128 MiB of HBM per device.

v0:
```python
import math

import jax
import jax.numpy as jnp
from jax import lax
from jax.sharding import PartitionSpec as P

D = 4096
HEADS = 32
KVH = 8
HD = 128
EXPERTS = 4


EPSILON = 1e-05
MASKED = -1e30


def cache_partial(query_vectors, key_rows, value_rows, live_mask, logit_scale_factor):
    scores = (
        jnp.einsum("rkqd,rpkd->rkqp", query_vectors, key_rows, preferred_element_type=jnp.float32)
        * logit_scale_factor
    )
    mask_rows = live_mask[:, None, None, :]
    scores = jnp.where(mask_rows, scores, MASKED)
    peak_value = jnp.max(scores, axis=-1)
    exp_weights = jnp.where(mask_rows, jnp.exp(scores - peak_value[..., None]), 0.0)
    denominator = jnp.sum(exp_weights, axis=-1)
    summed = jnp.einsum(
        "rkqp,rpkd->rkqd",
        exp_weights.astype(jnp.bfloat16),
        value_rows,
        preferred_element_type=jnp.float32,
    )
    return (peak_value, denominator, summed)


def combine(earlier, latter):
    peak_value = jnp.maximum(earlier[0], latter[0])
    weight_left = jnp.exp(earlier[0] - peak_value)
    weight_right = jnp.exp(latter[0] - peak_value)
    denominator = earlier[1] * weight_left + latter[1] * weight_right
    summed = earlier[2] * weight_left[..., None] + latter[2] * weight_right[..., None]
    return (peak_value, denominator, summed)


def finish(state, query_vectors, new_rows, logit_scale_factor):
    row_count, kv_local, group_size, head_size = query_vectors.shape
    fresh_key_rows = new_rows[:, 0, :].reshape(row_count, kv_local, head_size)
    new_values = new_rows[:, 1, :].reshape(row_count, kv_local, 1, head_size).astype(jnp.float32)
    self_score_value = (
        jnp.einsum(
            "rkqd,rkd->rkq", query_vectors, fresh_key_rows, preferred_element_type=jnp.float32
        )
        * logit_scale_factor
    )
    own_state = (
        self_score_value,
        jnp.ones_like(self_score_value),
        jnp.broadcast_to(new_values, query_vectors.shape),
    )
    peak_value, denominator, summed = combine(state, own_state)
    return (
        (summed / denominator[..., None])
        .reshape(row_count, kv_local * group_size * head_size)
        .astype(jnp.bfloat16)
    )


def shards(
    kv_prefill,
    slot_of,
    lengths,
    query,
    new_kv,
    wo,
    resid,
    norm_gain,
    expert_ids,
    gate_logits,
    gate_weight_slabs,
    w_up,
    w_down,
):
    axis_count = lax.axis_size("expert")
    my_index = lax.axis_index("expert")
    kv_local = kv_prefill.shape[3] // HD
    group_size = HEADS // KVH
    logit_scale_factor = 1.0 / math.sqrt(HD)
    seq_count = query.shape[0]
    total_rows = lengths.shape[0]
    ordered = jnp.take(kv_prefill, slot_of, axis=0)
    own_cache = lax.all_to_all(ordered, "expert", split_axis=0, concat_axis=1, tiled=True)
    positions = own_cache.shape[1]
    key_rows = own_cache[:, :, 0, :].reshape(seq_count, positions, kv_local, HD)
    value_rows = own_cache[:, :, 1, :].reshape(seq_count, positions, kv_local, HD)
    own_lengths = lax.dynamic_slice_in_dim(lengths, my_index * seq_count, seq_count)
    live_mask = jnp.arange(positions, dtype=jnp.int32)[None, :] < own_lengths[:, None]
    query_vectors = query.reshape(seq_count, kv_local, group_size, HD)
    state = cache_partial(query_vectors, key_rows, value_rows, live_mask, logit_scale_factor)
    context = finish(state, query_vectors, new_kv, logit_scale_factor)
    partial_out = jnp.dot(
        lax.all_gather(context, "expert", axis=0, tiled=True),
        wo,
        preferred_element_type=jnp.float32,
    )
    attention = lax.psum(partial_out.astype(jnp.bfloat16), "tensor")
    hidden_activation = resid.astype(jnp.float32) + attention.astype(jnp.float32)
    squares = lax.psum(jnp.sum(hidden_activation * hidden_activation, axis=1), "expert")
    normed = (
        hidden_activation
        * lax.rsqrt(squares / D + EPSILON)[:, None]
        * norm_gain.astype(jnp.float32)[None, :]
    ).astype(jnp.bfloat16)
    first_share = 1.0 / (1.0 + jnp.exp(gate_logits[:, 1] - gate_logits[:, 0]))
    shares = jnp.stack([first_share, 1.0 - first_share], axis=1)
    sharing = axis_count // EXPERTS
    my_expert = my_index // sharing
    mine_mask = expert_ids == my_expert
    mix_mine = jnp.sum(jnp.where(mine_mask, shares, 0.0), axis=1)
    gate_slab = gate_weight_slabs[0]
    up_slab = w_up[0]
    down_slab = w_down[0]
    capacity = 3 * total_rows // 4
    expert_range = jnp.arange(EXPERTS, dtype=jnp.int32)
    picked = jnp.any(expert_ids[:, :, None] == expert_range[None, None, :], axis=1).astype(
        jnp.int32
    )
    rank_of = jnp.cumsum(picked, axis=0) - 1
    slot_range = jnp.arange(capacity, dtype=jnp.int32)
    slot_hits = (picked[:, :, None] > 0) & (rank_of[:, :, None] == slot_range[None, None, :])
    token_range = jnp.arange(total_rows, dtype=jnp.int32)[:, None, None]
    token_table = jnp.sum(jnp.where(slot_hits, token_range, 0), axis=0)
    token_table = token_table + jnp.where(jnp.any(slot_hits, axis=0), 0, total_rows)
    padded_rows = jnp.concatenate([normed, jnp.zeros((1, normed.shape[1]), jnp.bfloat16)], axis=0)
    blocks = jnp.take(padded_rows, token_table, axis=0)
    outgoing = jnp.repeat(blocks, sharing, axis=0)
    arrived = lax.all_to_all(outgoing, "expert", split_axis=0, concat_axis=2, tiled=True)[0]
    gate_sum = jnp.dot(arrived, gate_slab, preferred_element_type=jnp.float32)
    up_sum = jnp.dot(arrived, up_slab, preferred_element_type=jnp.float32)
    activated = (jax.nn.silu(gate_sum) * up_sum).astype(jnp.bfloat16)
    produced = jnp.dot(activated, down_slab, preferred_element_type=jnp.float32)
    own_picked = jnp.any(mine_mask, axis=1)
    own_rank = jnp.sum(jnp.where(expert_range[None, :] == my_expert, rank_of, 0), axis=1)
    slot_index = jnp.where(own_picked, own_rank, capacity)
    padded_out = jnp.concatenate([produced, jnp.zeros((1, produced.shape[1]), jnp.float32)], axis=0)
    contrib = jnp.take(padded_out, slot_index, axis=0) * mix_mine[:, None]
    column_part = lax.psum_scatter(
        contrib.astype(jnp.bfloat16), "expert", scatter_dimension=1, tiled=True
    )
    summed_out = lax.psum_scatter(column_part, "tensor", scatter_dimension=0, tiled=True).astype(
        jnp.float32
    )
    moe_out = summed_out.astype(jnp.bfloat16)
    return (attention, moe_out)


def solution(mesh):
    return jax.shard_map(
        shards,
        mesh=mesh,
        in_specs=(
            P("groups", "expert", None, "tensor"),
            P("groups"),
            P("groups"),
            P(("groups", "expert"), "tensor"),
            P(("groups", "expert"), None, "tensor"),
            P("tensor", "expert"),
            P("groups", "expert"),
            P("expert"),
            P("groups", None),
            P("groups", None),
            P("expert", None, "tensor"),
            P("expert", None, "tensor"),
            P("expert", "tensor", None),
        ),
        out_specs=(P("groups", "expert"), P(("groups", "tensor"), "expert")),
        check_vma=False,
    )
```

profile of v0, /device:TPU:1, one launch (start us, length us, event | category | flops | bytes accessed | tf_op | source)
XLA Modules:
  0.0 184.4 jit_solution(8807511361082113522)
XLA Ops:
  7.2 0.8 compare_select_fusion.4
  8.0 0.7 compare_and_fusion.2
  8.8 5.9 %gather_fusion = bf16[16,128,2,256]{3,2,1,0:T(2,128)(2,1)} fusion(bf16[16,128,2,256]{3,2,1,0:T(2,128)(2,1)S(1)} %copy-done, s32[1024]{0:T(1024)S(1)} %pad_clamp_fusion.2), kind=kCustom, calls=%fused_computation | custom fusion | bytes 4194368 | tf_op jit(solution)/shard_map/jit(_take)/gather | solution.py:92
  14.7 4.8 %broadcast_select_fusion = bf16[16,128,2,256]{3,2,1,0:T(2,128)(2,1)} fusion(bf16[16,128,2,256]{3,2,1,0:T(2,128)(2,1)} %gather_fusion, pred[16]{0:T(512)(128)(4,1)S(1)} %compare_and_fusion.2), kind=kLoop, calls=%fused_computation.9 | loop fusion | flops 1048576 | bytes 4194320 | tf_op jit(solution)/shard_map/jit(_take)/select_n | solution.py:92
  19.5 5.6 %all-to-all-start = ((bf16[16,128,2,256]{3,2,1,0:T(2,128)(2,1)}), bf16[16,128,2,256]{3,2,1,0:T(2,128)(2,1)S(1)}, u32[]{:S(2)}, u32[]{:S(2)}) async-start(bf16[16,128,2,256]{3,2,1,0:T(2,128)(2,1)} %broadcast_select_fusion), calls=%async_computation | async-start | bytes 4194304 | tf_op jit(solution)/shard_map/all_to_all | solution.py:93
  26.9 46.0 %all-to-all-done = bf16[16,128,2,256]{3,2,1,0:T(2,128)(2,1)S(1)} async-done(((bf16[16,128,2,256]{3,2,1,0:T(2,128)(2,1)}), bf16[16,128,2,256]{3,2,1,0:T(2,128)(2,1)S(1)}, u32[]{:S(2)}, u32[]{:S(2)}) %all-to-all-start) | async-done | bytes 2097184 | tf_op jit(solution)/shard_map/all_to_all | solution.py:93
  73.4 1.1 fusion.45
  74.5 1.5 copy.53
  77.5 10.3 %all-gather = bf16[4,4,1024]{2,1,0:T(4,128)(2,1)S(1)} all-gather(bf16[1,4,1024]{2,1,0:T(4,128)(2,1)S(1)} %reshape.151), channel_id=1, replica_groups=mesh['groups'=2,'expert'=4,'tensor'=4] {'expert'}, dimensions={0}, use_global_device_ids=true | all-gather | bytes 40960 | tf_op jit(solution)/shard_map/all_gather | solution.py:103
  87.8 2.0 %convolution_convert_fusion = bf16[16,1024]{1,0:T(8,128)(2,1)S(1)} fusion(bf16[16,1024]{1,0:T(8,128)(2,1)S(1)} %reshape.152, bf16[1024,1024]{1,0:T(8,128)(2,1)} %param.18), kind=kOutput, calls=%fused_computation.15 | convolution fusion | flops 33570816 | bytes 2162688 | tf_op jit(solution)/shard_map/dot_general | solution.py:102
  89.8 14.2 %psum.14 = bf16[16,1024]{1,0:T(8,128)(2,1)S(1)} all-reduce(bf16[16,1024]{1,0:T(8,128)(2,1)S(1)} %convolution_convert_fusion), channel_id=1, replica_groups=mesh['groups'=2,'expert'=4,'tensor'=4] {'tensor'}, use_global_device_ids=true, to_apply=%region_2.3 | all-reduce | flops 16384 | bytes 65536 | tf_op jit(solution)/shard_map/psum | solution.py:107
  104.1 7.8 %psum.15 = f32[16]{0:T(128)S(1)} all-reduce(f32[16]{0:T(128)S(1)} %multiply_reduce_fusion), channel_id=1, replica_groups=mesh['groups'=2,'expert'=4,'tensor'=4] {'expert'}, use_global_device_ids=true, to_apply=%region_10.11 | all-reduce | flops 16 | bytes 128 | tf_op jit(solution)/shard_map/psum | solution.py:109
  112.0 0.7 gather_fusion.1
  112.7 0.7 broadcast_select_fusion.1
  113.4 3.3 %all-to-all-start.1 = ((bf16[4,12,1024]{2,1,0:T(8,128)(2,1)}), bf16[4,12,1024]{2,1,0:T(8,128)(2,1)S(1)}, u32[]{:S(2)}, u32[]{:S(2)}) async-start(bf16[4,12,1024]{2,1,0:T(8,128)(2,1)} %broadcast_select_fusion.1), calls=%async_computation.1 | async-start | bytes 262144 | tf_op jit(solution)/shard_map/all_to_all | solution.py:138
  117.0 4.5 %all-to-all-done.1 = bf16[4,12,1024]{2,1,0:T(8,128)(2,1)S(1)} async-done(((bf16[4,12,1024]{2,1,0:T(8,128)(2,1)}), bf16[4,12,1024]{2,1,0:T(8,128)(2,1)S(1)}, u32[]{:S(2)}, u32[]{:S(2)}) %all-to-all-start.1) | async-done | bytes 98336 | tf_op jit(solution)/shard_map/all_to_all | solution.py:138
  121.7 8.0 %fusion.4 = f32[12,2048]{1,0:T(8,128)S(1)} fusion(bf16[12,4096]{1,0:T(8,128)(2,1)S(1)} %bitcast.60, bf16[1,4096,2048]{2,1,0:T(8,128)(2,1)} %param.23), kind=kOutput, calls=%fused_computation.7 | convolution fusion | flops 201326592 | bytes 16973824 | tf_op jit(solution)/shard_map/dot_general | solution.py:139
  129.7 13.0 %fusion = f32[12,4096]{1,0:T(8,128)S(1)} fusion(bf16[1,2048,4096]{2,1,0:T(8,128)(2,1)} %param.25, bf16[12,4096]{1,0:T(8,128)(2,1)S(1)} %bitcast.61, bf16[1,4096,2048]{2,1,0:T(8,128)(2,1)} %param.24, f32[12,2048]{1,0:T(8,128)S(1)} %fusion.4), kind=kOutput, calls=%fused_computation.3 | convolution fusion | flops 402800640 | bytes 33947648 | tf_op jit(solution)/shard_map/dot_general | solution.py:142
  142.7 0.6 gather_fusion.2
  143.4 0.7 multiply_convert_fusion
  144.2 0.6 dynamic-slice
  145.4 18.1 %reduce-scatter.2.cloned.1.call-done = bf16[16,1024]{1,0:T(8,128)(2,1)} async-done(((bf16[16,4096]{1,0:T(8,128)(2,1)}), bf16[16,1024]{1,0:T(8,128)(2,1)}) %reduce-scatter.2.cloned.1.call-update) | async-done | bytes 32784 | tf_op jit(solution)/shard_map/reduce_scatter | solution.py:148
  163.5 13.5 %all-reduce.2 = bf16[16,1024]{1,0:T(8,128)(2,1)S(1)} all-reduce(bf16[16,1024]{1,0:T(8,128)(2,1)} %reduce-scatter.2.cloned.1.call-done), channel_id=3, replica_groups=mesh['groups'=2,'expert'=4,'tensor'=4] {'tensor'}, use_global_device_ids=true, to_apply=%region_13.14.clone | all-reduce | flops 16384 | bytes 65536
  177.0 0.6 constant_dynamic-slice_fusion
  (72 shorter events, 4.6 us)
Async XLA Ops:
  7.2 1.6 copy-start
  19.5 5.6 %copy-start.5 = (bf16[4,1024]{1,0:T(4,128)(2,1)S(1)}, bf16[4,1024]{1,0:T(4,128)(2,1)}, u32[]{:S(2)}) copy-start(bf16[4,1024]{1,0:T(4,128)(2,1)} %param.16) | copy-start | bytes 24580
  19.5 5.6 %copy-start.4 = (bf16[4,2,256]{2,1,0:T(2,128)(2,1)S(1)}, bf16[4,2,256]{2,1,0:T(2,128)(2,1)}, u32[]{:S(2)}) copy-start(bf16[4,2,256]{2,1,0:T(2,128)(2,1)} %param.17) | copy-start | bytes 12292
  19.5 5.6 %copy-start.7 = (bf16[1024]{0:T(1024)(128)(2,1)S(1)}, bf16[1024]{0:T(1024)(128)(2,1)}, u32[]{:S(2)}) copy-start(bf16[1024]{0:T(1024)(128)(2,1)} %param.20) | copy-start | bytes 6148
  19.5 5.7 %copy-start.6 = (s32[16,2]{0,1:T(2,128)S(1)}, s32[16,2]{0,1:T(2,128)}, u32[]{:S(2)}) copy-start(s32[16,2]{0,1:T(2,128)} %param.21) | copy-start | bytes 388
  19.5 7.0 %copy-start.9 = (s32[16]{0:T(128)S(1)}, s32[16]{0:T(128)}, u32[]{:S(2)}) copy-start(s32[16]{0:T(128)} %param.15) | copy-start | bytes 196
  19.5 7.1 %copy-start.8 = (f32[16,2]{0,1:T(2,128)S(1)}, f32[16,2]{0,1:T(2,128)}, u32[]{:S(2)}) copy-start(f32[16,2]{0,1:T(2,128)} %param.22) | copy-start | bytes 388
  19.5 53.3 %all-to-all-start = ((bf16[16,128,2,256]{3,2,1,0:T(2,128)(2,1)}), bf16[16,128,2,256]{3,2,1,0:T(2,128)(2,1)S(1)}, u32[]{:S(2)}, u32[]{:S(2)}) async-start(bf16[16,128,2,256]{3,2,1,0:T(2,128)(2,1)} %broadcast_select_fusion), calls=%async_computation | async-start | bytes 4194304 | tf_op jit(solution)/shard_map/all_to_all | solution.py:93
  76.9 27.1 %copy-start.3 = (bf16[16,1024]{1,0:T(8,128)(2,1)S(1)}, bf16[16,1024]{1,0:T(8,128)(2,1)}, u32[]{:S(2)}) copy-start(bf16[16,1024]{1,0:T(8,128)(2,1)} %param.19) | copy-start | bytes 98308
  103.9 25.8 %copy-start.2 = (bf16[16,1024]{1,0:T(8,128)(2,1)}, bf16[16,1024]{1,0:T(8,128)(2,1)S(1)}, u32[]{:S(2)}) copy-start(bf16[16,1024]{1,0:T(8,128)(2,1)S(1)} %psum.14) | copy-start | bytes 98308
  113.4 8.1 %all-to-all-start.1 = ((bf16[4,12,1024]{2,1,0:T(8,128)(2,1)}), bf16[4,12,1024]{2,1,0:T(8,128)(2,1)S(1)}, u32[]{:S(2)}, u32[]{:S(2)}) async-start(bf16[4,12,1024]{2,1,0:T(8,128)(2,1)} %broadcast_select_fusion.1), calls=%async_computation.1 | async-start | bytes 262144 | tf_op jit(solution)/shard_map/all_to_all | solution.py:138
  116.7 46.7 %reduce-scatter.2.cloned.1.call-start = ((), (), s32[]{:S(2)}) async-start(), calls=%async_computation.3 | async-start | bytes 163840 | tf_op jit(solution)/shard_map/reduce_scatter | solution.py:148
  129.7 47.9 %copy-start.1 = (bf16[16,128,2,256]{3,2,1,0:T(2,128)(2,1)S(1)}, bf16[16,128,2,256]{3,2,1,0:T(2,128)(2,1)}, u32[]{:S(2)}) copy-start(bf16[16,128,2,256]{3,2,1,0:T(2,128)(2,1)} %param.13) | copy-start | bytes 6291460
  142.7 1.4 copy-start.10
Sparse Core Ops, SparseCore 0:
  144.3 19.1 reduce-scatter.1
where the time goes:
time: 185 us; the launch traced here: 184 us
  waiting for transfers between devices  68.5 us (37%)
  blocking collectives  45.7 us (25%)
  matrix products  23.9 us (13%)
  between operations  15 us (8%)
  local copies, waits for them, and re-layouts  13.1 us (7%)
  other arithmetic  9.12 us (5%)
  starting transfers between devices  9.1 us (5%)
    all_to_all x1, waiting for transfers between devices, shards(): lax.all_to_all(ordered, 'expert', split_axis=0, concat_axis=1, tiled=True)  46 us
    reduce_scatter x1, waiting for transfers between devices, shards(): lax.psum_scatter(contrib.astype(jnp.bfloat16), 'expert', scatter_dimensio...  18.1 us
    psum x1, blocking collectives, shards(): attention = lax.psum(partial_out.astype(jnp.bfloat16), 'tensor')  14.2 us
    unnamed x1, blocking collectives  13.5 us
    dot_general x1, matrix products, shards(): produced = jnp.dot(activated, down_slab, preferred_element_type=jnp.float32)  13 us
    all_gather x1, blocking collectives, shards(): lax.all_gather(context, 'expert', axis=0, tiled=True)  10.3 us
    dot_general x1, matrix products, shards(): gate_sum = jnp.dot(arrived, gate_slab, preferred_element_type=jnp.float32)  8.04 us
    psum x1, blocking collectives, shards(): lax.psum(jnp.sum(hidden_activation * hidden_activation, axis=1), 'expert')  7.8 us
  transfers between devices with their start and end apart: 3, of which 3 were waited for; matrix products, arithmetic and copies ran while one was open for 1% of the time, Pallas kernels for 0%

commit v1 on v0

v1 whole, which is shorter than its diff:
```python
import functools
import math

import jax
import jax.numpy as jnp
from jax import lax
from jax.experimental import pallas as pl
from jax.experimental.pallas import tpu as pltpu
from jax.sharding import PartitionSpec as P

HEADS = 32
KVH = 8
HD = 128
EXPERTS = 4
EPSILON = 1e-05
MASKED = -1e30
LIVE = -1e29
LANES = 128
STATS = 16
MOST_PERMUTES = 4

BF = jnp.bfloat16
F32 = jnp.float32
VMEM = pl.BlockSpec(memory_space=pltpu.VMEM)
SMEM = pl.BlockSpec(memory_space=pltpu.SMEM)
HBM = pl.BlockSpec(memory_space=pltpu.HBM)


def gather(value, axis):
    count = lax.axis_size(axis)
    if count > MOST_PERMUTES:
        return [lax.all_gather(value, axis)]
    out = [value]
    for shift in range(1, count):
        out.append(lax.ppermute(value, axis, [(i, (i + shift) % count) for i in range(count)]))
    return out


def exchange(values, axis):
    count = lax.axis_size(axis)
    if count > MOST_PERMUTES:
        return [lax.all_to_all(values[0], axis, 0, 0, tiled=True)]
    out = [values[0]]
    for shift in range(1, count):
        out.append(
            lax.ppermute(values[shift], axis, [(i, (i + shift) % count) for i in range(count)])
        )
    return out


def piece(refs, count, shift):
    return refs[shift][...] if len(refs) == count else refs[0][shift]


def source(refs, count, me, shift):
    return lax.rem(me - shift + count, count) if len(refs) == count else shift


def target(stacked, count, me, shift):
    return shift if stacked else lax.rem(me + shift, count)


def grouped(count):
    return 1 if count > MOST_PERMUTES else count


def attend_kernel(count, own_rows, kv_heads, group, positions, *refs):
    taken = grouped(count)
    slot_ref, length_ref = refs[0], refs[1]
    query_refs = refs[2 : 2 + taken]
    new_ref, cache_ref, out_ref = refs[2 + taken : 5 + taken]
    q_rows, score, acc, fresh = refs[5 + taken :]
    me = lax.axis_index("expert")
    heads = kv_heads * group
    total = count * own_rows
    rows = total * heads
    width = 2 * positions
    scale = 1.0 / math.sqrt(HD)
    for shift in range(count):
        block = piece(query_refs, count, shift).astype(F32)
        where_to = source(query_refs, count, me, shift)
        for head in range(heads):
            q_rows[where_to, pl.ds(head, own_rows, stride=heads), :] = block[
                :, head * HD : (head + 1) * HD
            ]
    head_of_row = lax.broadcasted_iota(jnp.int32, (heads, HD), 0) // group
    lane = lax.broadcasted_iota(jnp.int32, (heads, width), 1)
    position = me * positions + lane // 2
    is_key = lax.rem(lane, 2) == 0

    def diagonal(parts):
        return sum(jnp.where(head_of_row == g, parts(g), 0.0) for g in range(kv_heads))

    def scores(b):
        owner, within = b // own_rows, lax.rem(b, own_rows)
        vectors = q_rows[owner, pl.ds(pl.multiple_of(within * heads, heads), heads), :]
        spread = jnp.concatenate(
            [jnp.where(head_of_row == g, vectors, 0.0) for g in range(kv_heads)], axis=1
        ).astype(BF)
        both = cache_ref[slot_ref[b]]
        found = (
            lax.dot_general(
                spread, both, (((1,), (1,)), ((), ())), preferred_element_type=F32
            )
            * scale
        )
        live = is_key & (position < length_ref[b])
        score[pl.ds(pl.multiple_of(b * heads, heads), heads), :] = jnp.where(live, found, MASKED)

    def values(b):
        at = pl.ds(pl.multiple_of(b * heads, heads), heads)
        both = cache_ref[slot_ref[b]]
        summed = jnp.dot(score[at, :].astype(BF), both, preferred_element_type=F32)
        acc[at, :] = diagonal(lambda g: summed[:, g * HD : (g + 1) * HD])

    def sweep(step):
        if total <= 16:
            for b in range(total):
                step(b)
        else:
            pl.loop(0, total)(step)

    sweep(scores)
    own = own_rows * heads
    new = new_ref[...].astype(F32)
    for b in range(own_rows):
        for g in range(kv_heads):
            at = b * heads + g * group
            for which in range(2):
                fresh[which, at : at + group, :] = jnp.broadcast_to(
                    new[b, which : which + 1, g * HD : (g + 1) * HD], (group, HD)
                )
    own_score = jnp.sum(q_rows[me] * fresh[0], axis=1, keepdims=True) * scale
    row = lax.broadcasted_iota(jnp.int32, (rows, 1), 0)
    at_home = (row >= me * own) & (row < (me + 1) * own)
    own_all = jnp.concatenate([own_score] * count, axis=0)
    own_all = jnp.where(at_home, own_all, MASKED)
    raw = score[...]
    peak = jnp.maximum(jnp.max(raw, axis=1, keepdims=True), own_all).astype(BF).astype(F32)
    weights = jnp.where(raw > LIVE, jnp.exp(raw - peak), 0.0)
    own_weight = jnp.where(at_home, jnp.exp(own_all - peak), 0.0)
    weight_sum = jnp.sum(weights, axis=1, keepdims=True) + own_weight
    score[...] = pltpu.roll(weights, 1, 1)
    sweep(values)
    fresh_all = jnp.concatenate([fresh[1]] * count, axis=0)
    out_ref[0:rows, :] = (acc[...] + own_weight * fresh_all).astype(BF)
    high = weight_sum.astype(BF).astype(F32)
    low = weight_sum - high
    column = lax.broadcasted_iota(jnp.int32, (rows, LANES), 1)
    table = jnp.where(
        column == 0, peak, jnp.where(column == 1, high, jnp.where(column == 2, low, 0.0))
    )
    for part in range(rows // LANES):
        turned = table[part * LANES : (part + 1) * LANES, :].T
        out_ref[rows + part * STATS : rows + (part + 1) * STATS, :] = turned[0:STATS, :].astype(BF)


def attend(slot_of, lengths, queries, new_kv, cache, count):
    own_rows, _, kv_width = new_kv.shape
    kv_heads = kv_width // HD
    group = HEADS // KVH
    heads = kv_heads * group
    positions = cache.shape[1] // 2
    rows = count * own_rows * heads
    return pl.pallas_call(
        functools.partial(attend_kernel, count, own_rows, kv_heads, group, positions),
        name="attend",
        out_shape=jax.ShapeDtypeStruct((rows + STATS * (rows // LANES), LANES), BF),
        in_specs=[SMEM, SMEM] + [VMEM] * (len(queries) + 2),
        out_specs=VMEM,
        scratch_shapes=[
            pltpu.VMEM((count, own_rows * heads, HD), F32),
            pltpu.VMEM((rows, 2 * positions), F32),
            pltpu.VMEM((rows, HD), F32),
            pltpu.VMEM((2, own_rows * heads, HD), F32),
        ],
        compiler_params=pltpu.CompilerParams(vmem_limit_bytes=12 << 20),
        cost_estimate=pl.CostEstimate(flops=10**9, bytes_accessed=4 << 20, transcendentals=0),
    )(slot_of, lengths, *queries, new_kv, cache)


def project_kernel(count, rows, heads, *refs):
    taken = grouped(count)
    part_refs = refs[:taken]
    wo_ref, out_ref, joined, context = refs[taken:]
    parts = [piece(part_refs, count, s) for s in range(count)]

    def stats(part):
        tables = []
        for block in range(rows // LANES):
            at = rows + block * STATS
            table = part[at : at + STATS, :].astype(F32)
            tall = jnp.concatenate([table, jnp.zeros((LANES - STATS, LANES), F32)], axis=0)
            tables.append(tall.T)
        table = jnp.concatenate(tables, axis=0)
        return table[:, 0:1], table[:, 1:2] + table[:, 2:3]

    found = [stats(part) for part in parts]
    peak = functools.reduce(jnp.maximum, [m for m, _ in found])
    weights = [jnp.exp(m - peak) for m, _ in found]
    denominator = sum(w * l for w, (_, l) in zip(weights, found))
    numerator = sum(w * part[0:rows, :].astype(F32) for w, part in zip(weights, parts))
    joined[...] = numerator / denominator
    total = rows // heads
    for head in range(heads):
        context[:, head * HD : (head + 1) * HD] = joined[
            pl.ds(head, total, stride=heads), :
        ].astype(BF)
    out_ref[...] = jnp.dot(context[...], wo_ref[...], preferred_element_type=F32).astype(BF)


def project(parts, wo, count, total):
    heads = wo.shape[0] // HD
    rows = total * heads
    return pl.pallas_call(
        functools.partial(project_kernel, count, rows, heads),
        name="project",
        out_shape=jax.ShapeDtypeStruct((total, wo.shape[1]), BF),
        in_specs=[VMEM] * (len(parts) + 1),
        out_specs=VMEM,
        scratch_shapes=[
            pltpu.VMEM((rows, HD), F32),
            pltpu.VMEM((total, wo.shape[0]), BF),
        ],
        compiler_params=pltpu.CompilerParams(vmem_limit_bytes=(12 if len(parts) == count else 48) << 20),
        cost_estimate=pl.CostEstimate(flops=10**9, bytes_accessed=4 << 20, transcendentals=0),
    )(*parts, wo)


def residual_kernel(count, *refs):
    taken = grouped(count)
    part_refs = refs[:taken]
    resid_ref, gain_ref, attn_ref, out_ref, ordered = refs[taken:]
    me = lax.axis_index("tensor")
    for shift in range(count):
        ordered[source(part_refs, count, me, shift)] = piece(part_refs, count, shift)
    attention = sum(ordered[i].astype(F32) for i in range(count)).astype(BF)
    attn_ref[...] = attention
    hidden = resid_ref[...].astype(F32) + attention.astype(F32)
    squares = jnp.sum(hidden * hidden, axis=1, keepdims=True)
    width = hidden.shape[1]
    out_ref[:, 0:width] = (hidden * gain_ref[...].astype(F32)).astype(BF)
    high = squares.astype(BF).astype(F32)
    middle = (squares - high).astype(BF).astype(F32)
    low = squares - high - middle
    column = lax.broadcasted_iota(jnp.int32, (hidden.shape[0], LANES), 1)
    out_ref[:, width:] = jnp.where(
        column == 0, high, jnp.where(column == 1, middle, jnp.where(column == 2, low, 0.0))
    ).astype(BF)


def residual(parts, resid, gain, count):
    rows, width = resid.shape
    return pl.pallas_call(
        functools.partial(residual_kernel, count),
        name="residual",
        out_shape=(
            jax.ShapeDtypeStruct((rows, width), BF),
            jax.ShapeDtypeStruct((rows, width + LANES), BF),
        ),
        in_specs=[VMEM] * (len(parts) + 2),
        out_specs=(VMEM, VMEM),
        scratch_shapes=[pltpu.VMEM((count, rows, width), BF)],
        compiler_params=pltpu.CompilerParams(vmem_limit_bytes=8 << 20),
        cost_estimate=pl.CostEstimate(flops=10**8, bytes_accessed=1 << 20, transcendentals=0),
    )(*parts, resid, gain.reshape(1, width))


def experts_kernel(count, sharing, chunks, *refs):
    taken = grouped(count)
    part_refs = refs[:taken]
    ids_ref, logits_ref, gate_hbm, up_hbm, down_hbm = refs[taken : taken + 5]
    out_refs = refs[taken + 5 : 2 * taken + 5]
    spread, gate_buf, up_buf, down_buf, act, gate_sem, up_sem, down_sem = refs[2 * taken + 5 :]
    me = lax.axis_index("expert")
    depth, hidden_units = gate_buf.shape
    step = depth // chunks
    down_step = hidden_units // chunks
    copies = []
    for c in range(chunks):
        at = pl.ds(c * step, step)
        copies.append(
            (
                pltpu.make_async_copy(gate_hbm.at[at, :], gate_buf.at[at, :], gate_sem.at[c]),
                pltpu.make_async_copy(up_hbm.at[at, :], up_buf.at[at, :], up_sem.at[c]),
            )
        )
    down_copies = []
    for c in range(chunks):
        at = pl.ds(c * down_step, down_step)
        down_copies.append(
            pltpu.make_async_copy(down_hbm.at[at, :], down_buf.at[at, :], down_sem.at[c])
        )
    for pair in copies:
        pair[0].start()
        pair[1].start()
    for copy in down_copies:
        copy.start()
    rows = spread.shape[0]
    width = depth // count
    squares = jnp.zeros((rows, 1), F32)
    for shift in range(count):
        block = piece(part_refs, count, shift)
        at = source(part_refs, count, me, shift)
        spread[:, pl.ds(pl.multiple_of(at * width, width), width)] = block[:, 0:width]
        tail = block[:, width:].astype(F32)
        squares = squares + (tail[:, 0:1] + tail[:, 1:2] + tail[:, 2:3])
    inverse = lax.rsqrt(squares / depth + EPSILON)
    mine = me // sharing
    logits = logits_ref[...]
    first = 1.0 / (1.0 + jnp.exp(logits[1:2, :] - logits[0:1, :]))
    ids = ids_ref[...]
    mix_row = jnp.where(ids[0:1, :] == mine, first, 0.0) + jnp.where(
        ids[1:2, :] == mine, 1.0 - first, 0.0
    )
    eye = lax.broadcasted_iota(jnp.int32, (rows, rows), 0) == lax.broadcasted_iota(
        jnp.int32, (rows, rows), 1
    )
    mix = jnp.sum(jnp.where(eye, mix_row, 0.0), axis=1, keepdims=True)
    gate_sum = jnp.zeros((rows, hidden_units), F32)
    up_sum = jnp.zeros((rows, hidden_units), F32)
    for c in range(chunks):
        at = pl.ds(c * step, step)
        block = spread[:, at]
        copies[c][0].wait()
        gate_sum += jnp.dot(block, gate_buf[at, :], preferred_element_type=F32)
        copies[c][1].wait()
        up_sum += jnp.dot(block, up_buf[at, :], preferred_element_type=F32)
    gate_sum = gate_sum * inverse
    act[...] = (gate_sum / (1.0 + jnp.exp(-gate_sum)) * (up_sum * inverse)).astype(BF)
    for copy in down_copies:
        copy.wait()
    stacked = taken == 1
    for shift in range(count):
        at = target(stacked, count, me, shift)
        columns = pl.ds(pl.multiple_of(at * width, width), width)
        made = jnp.dot(act[...], down_buf[:, columns], preferred_element_type=F32)
        made = (made * mix).astype(BF)
        if stacked:
            out_refs[0][shift] = made
        else:
            out_refs[shift][...] = made


def experts(parts, ids, logits, gate, up, down, count):
    depth, hidden_units = gate.shape
    rows = ids.shape[0]
    width = depth // count
    stacked = len(parts) != count
    one = jax.ShapeDtypeStruct((rows, width), BF)
    out_shape = (
        (jax.ShapeDtypeStruct((count, rows, width), BF),) if stacked else tuple([one] * count)
    )
    chunks = 4
    hbm = lambda w: pltpu.with_memory_space_constraint(w, pltpu.HBM)
    return pl.pallas_call(
        functools.partial(experts_kernel, count, count // EXPERTS, chunks),
        name="experts",
        out_shape=out_shape,
        in_specs=[VMEM] * (len(parts) + 2) + [HBM] * 3,
        out_specs=tuple([VMEM] * len(out_shape)),
        scratch_shapes=[
            pltpu.VMEM((rows, depth), BF),
            pltpu.VMEM((depth, hidden_units), BF),
            pltpu.VMEM((depth, hidden_units), BF),
            pltpu.VMEM((hidden_units, depth), BF),
            pltpu.VMEM((rows, hidden_units), BF),
            pltpu.SemaphoreType.DMA((chunks,)),
            pltpu.SemaphoreType.DMA((chunks,)),
            pltpu.SemaphoreType.DMA((chunks,)),
        ],
        compiler_params=pltpu.CompilerParams(vmem_limit_bytes=58 << 20),
        cost_estimate=pl.CostEstimate(flops=10**10, bytes_accessed=50 << 20, transcendentals=0),
    )(*parts, ids.T, logits.T, hbm(gate), hbm(up), hbm(down))


def first_sum_kernel(count, other, *refs):
    taken = grouped(count)
    part_refs, out_refs = refs[:taken], refs[taken:]
    me = lax.axis_index("tensor")
    total = sum(piece(part_refs, count, s).astype(F32) for s in range(count))
    rows = total.shape[0] // other
    blocks = [total[i * rows : (i + 1) * rows, :] for i in range(other)]
    for shift in range(other):
        if grouped(other) == 1:
            out_refs[0][shift] = blocks[shift].astype(BF)
        else:
            at = target(False, other, me, shift)
            chosen = sum(jnp.where(at == i, blocks[i], 0.0) for i in range(other))
            out_refs[shift][...] = chosen.astype(BF)


def last_sum_kernel(count, *refs):
    taken = grouped(count)
    part_refs, out_ref = refs[:taken], refs[taken]
    out_ref[...] = sum(piece(part_refs, count, s).astype(F32) for s in range(count)).astype(BF)


def first_sum(parts, count, other, rows, width):
    one = (rows // other, width)
    if grouped(other) == 1:
        out_shape = (jax.ShapeDtypeStruct((other,) + one, BF),)
    else:
        out_shape = tuple([jax.ShapeDtypeStruct(one, BF)] * other)
    return pl.pallas_call(
        functools.partial(first_sum_kernel, count, other),
        name="first_sum",
        out_shape=out_shape,
        in_specs=[VMEM] * len(parts),
        out_specs=tuple([VMEM] * len(out_shape)),
        compiler_params=pltpu.CompilerParams(vmem_limit_bytes=8 << 20),
    )(*parts)


def last_sum(parts, count, shape):
    return pl.pallas_call(
        functools.partial(last_sum_kernel, count),
        name="last_sum",
        out_shape=jax.ShapeDtypeStruct(shape, BF),
        in_specs=[VMEM] * len(parts),
        out_specs=VMEM,
        compiler_params=pltpu.CompilerParams(vmem_limit_bytes=8 << 20),
    )(*parts)


def shards(
    kv_prefill,
    slot_of,
    lengths,
    query,
    new_kv,
    wo,
    resid,
    norm_gain,
    expert_ids,
    gate_logits,
    gate_weight_slabs,
    w_up,
    w_down,
):
    expert_count = lax.axis_size("expert")
    tensor_count = lax.axis_size("tensor")
    total, width = resid.shape
    slots, positions, _, kv_width = kv_prefill.shape
    queries = gather(query, "expert")
    cache = kv_prefill.reshape(slots, 2 * positions, kv_width)
    part = attend(slot_of, lengths, queries, new_kv, cache, expert_count)
    projected = project(gather(part, "expert"), wo, expert_count, total)
    attention, scaled = residual(gather(projected, "tensor"), resid, norm_gain, tensor_count)
    outgoing = experts(
        gather(scaled, "expert"),
        expert_ids,
        gate_logits,
        gate_weight_slabs[0],
        w_up[0],
        w_down[0],
        expert_count,
    )
    column_parts = first_sum(
        exchange(outgoing, "expert"), expert_count, tensor_count, total, width
    )
    moe_out = last_sum(
        exchange(column_parts, "tensor"), tensor_count, (total // tensor_count, width)
    )
    return (attention, moe_out)


def solution(mesh):
    return jax.shard_map(
        shards,
        mesh=mesh,
        in_specs=(
            P("groups", "expert", None, "tensor"),
            P("groups"),
            P("groups"),
            P(("groups", "expert"), "tensor"),
            P(("groups", "expert"), None, "tensor"),
            P("tensor", "expert"),
            P("groups", "expert"),
            P("expert"),
            P("groups", None),
            P("groups", None),
            P("expert", None, "tensor"),
            P("expert", None, "tensor"),
            P("expert", "tensor", None),
        ),
        out_specs=(P("groups", "expert"), P(("groups", "tensor"), "expert")),
        check_vma=False,
    )
```

time: 185 us -> 72.6 us (0.39)
  waiting for transfers between devices: 68.5 us -> 13.8 us
  blocking collectives: 45.7 us -> 0 us
  matrix products: 23.9 us -> 0 us
  Pallas kernels: 0 us -> 23.1 us
  starting transfers between devices: 9.1 us -> 24.7 us
  between operations: 15 us -> 0.72 us
  other arithmetic: 9.12 us -> 0 us
  local copies, waits for them, and re-layouts: 13.1 us -> 9.84 us
    all_to_all x2 -> x0, waiting for transfers between devices: 50.4 us -> none  [the longest x1 46 us: shards(): lax.all_to_all(ordered, 'expert', split_axis=0, concat_axis=1, tiled=True)]
    ppermute x0 -> x18, starting transfers between devices: none -> 24.7 us  [the longest x12 17 us: gather(): lax.ppermute(value, axis, [(i, (i + shift) % count) for i in range(count)])]
    dot_general x6 -> x0, matrix products: 23.9 us -> none  [the longest x1 13 us: shards(): produced = jnp.dot(activated, down_slab, preferred_element_type=jnp.float32)]
    pallas_call x0 -> x6, Pallas kernels: none -> 23.1 us  [the longest x1 19.2 us: experts(): pl.pallas_call(functools.partial(experts_kernel, count, count // EXPERTS,...]
    psum x2 -> x0, blocking collectives: 22 us -> none  [the longest x1 14.2 us: shards(): attention = lax.psum(partial_out.astype(jnp.bfloat16), 'tensor')]
    reduce_scatter x1 -> x0, waiting for transfers between devices: 18.1 us -> none  [shards(): lax.psum_scatter(contrib.astype(jnp.bfloat16), 'expert', scatter_dimensio...]
    ppermute x0 -> x18, waiting for transfers between devices: none -> 13.8 us  [the longest x12 8.83 us: gather(): lax.ppermute(value, axis, [(i, (i + shift) % count) for i in range(count)])]
    unnamed x1 -> x0, blocking collectives: 13.5 us -> none
  transfers between devices with their start and end apart: 3 -> 18, of which waited for: 3 -> 11; matrix products, arithmetic and copies ran while one was open for 1% -> 5% of each run, Pallas kernels for 0% -> 0%
where the time goes in v1:
time: 72.6 us; the launch traced here: 72.1 us
  starting transfers between devices  24.7 us (34%)
  Pallas kernels  23.1 us (32%)
  waiting for transfers between devices  13.8 us (19%)
  local copies, waits for them, and re-layouts  9.84 us (14%)
    pallas_call x1, Pallas kernels, experts(): pl.pallas_call(functools.partial(experts_kernel, count, count // EXPERTS,...  19.2 us
    ppermute x12, starting transfers between devices, gather(): lax.ppermute(value, axis, [(i, (i + shift) % count) for i in range(count)])  17 us
    ppermute x12, waiting for transfers between devices, gather(): lax.ppermute(value, axis, [(i, (i + shift) % count) for i in range(count)])  8.83 us
    ppermute x6, starting transfers between devices, exchange(): lax.ppermute(values[shift], axis, [(i, (i + shift) % count) for i in rang...  7.66 us
    unnamed x22, local copies, waits for them, and re-layouts  6.41 us
    ppermute x6, waiting for transfers between devices, exchange(): lax.ppermute(values[shift], axis, [(i, (i + shift) % count) for i in rang...  4.93 us
    reshape x1, local copies, waits for them, and re-layouts, shards(): cache = kv_prefill.reshape(slots, 2 * positions, kv_width)  2.75 us
    pallas_call x1, Pallas kernels, attend(): pl.pallas_call(functools.partial(attend_kernel, count, own_rows, kv_heads...  1.7 us
  transfers between devices with their start and end apart: 18, of which 11 were waited for; matrix products, arithmetic and copies ran while one was open for 5% of the time, Pallas kernels for 0%

profile of v1, /device:TPU:1, one launch (start us, length us, event | category | flops | bytes accessed | tf_op | source)
XLA Modules:
  0.0 72.1 jit_solution(125455834284093484)
XLA Ops:
  0.6 2.2 %collective-permute-start = (bf16[4,1024]{1,0:T(4,128)(2,1)}, bf16[4,1024]{1,0:T(4,128)(2,1)S(1)}, u32[]{:S(2)}, u32[]{:S(2)}) collective-permute-start(bf16[4,1024]{1,0:T(4,128)(2,1)} %refs_2_.1), channel_id=1, source_target_pairs={{0,4},{4,8},{8,12},{12,0},{1,5},{5,9},{9,13},{13,1},{2,6},{6,10},{... | collective-permute-start | bytes 24584 | tf_op jit(solution)/shard_map/ppermute | solution.py:35
  2.8 2.3 %collective-permute-start.1 = (bf16[4,1024]{1,0:T(4,128)(2,1)}, bf16[4,1024]{1,0:T(4,128)(2,1)S(1)}, u32[]{:S(2)}, u32[]{:S(2)}) collective-permute-start(bf16[4,1024]{1,0:T(4,128)(2,1)} %refs_2_.1), channel_id=1, source_target_pairs={{0,8},{4,12},{8,0},{12,4},{1,9},{5,13},{9,1},{13,5},{2,10},{6,14},... | collective-permute-start | bytes 24584 | tf_op jit(solution)/shard_map/ppermute | solution.py:35
  5.1 1.1 %collective-permute-start.2 = (bf16[4,1024]{1,0:T(4,128)(2,1)}, bf16[4,1024]{1,0:T(4,128)(2,1)S(1)}, u32[]{:S(2)}, u32[]{:S(2)}) collective-permute-start(bf16[4,1024]{1,0:T(4,128)(2,1)} %refs_2_.1), channel_id=1, source_target_pairs={{0,12},{4,0},{8,4},{12,8},{1,13},{5,1},{9,5},{13,9},{2,14},{6,2},{... | collective-permute-start | bytes 24584 | tf_op jit(solution)/shard_map/ppermute | solution.py:35
  6.2 2.7 %reshape.10.refs_7_ = bf16[16,256,256]{2,1,0:T(8,128)(2,1)S(1)} reshape(bf16[16,128,2,256]{3,2,1,0:T(2,128)(2,1)} %param.13) | data formatting | bytes 4194304 | tf_op jit(solution)/shard_map/reshape | solution.py:446
  11.7 1.7 %attend.1.refs_0_ = bf16[144,128]{1,0:T(8,128)(2,1)S(1)} custom-call(s32[16]{0:T(128)S(1)} %copy-done.6, s32[16]{0:T(128)S(1)} %copy-done.7, bf16[4,1024]{1,0:T(4,128)(2,1)S(1)} %copy-done.4, bf16[4,1024]{1,0:T(4,128)(2,1)S(1)} %collective-permute-done.refs_3_, bf16[4,1024]{1,0:T(4,128)(2,1)S(1)} %collective-permute-done.1.refs_4_, ...), custom_call_target="tpu_custom_call" | custom-call | flops 1000000000 | bytes 4194304 | tf_op jit(solution)/shard_map/attend/pallas_call | solution.py:165
  13.8 1.6 %collective-permute-start.4 = (bf16[144,128]{1,0:T(8,128)(2,1)S(1)}, bf16[144,128]{1,0:T(8,128)(2,1)S(1)}, u32[]{:S(2)}, u32[]{:S(2)}) collective-permute-start(bf16[144,128]{1,0:T(8,128)(2,1)S(1)} %attend.1.refs_0_), channel_id=1, source_target_pairs={{0,8},{4,12},{8,0},{12,4},{1,9},{5,13},{9,1},{13,5},{2,10},{6,14},... | collective-permute-start | bytes 110600 | tf_op jit(solution)/shard_map/ppermute | solution.py:35
  15.4 1.3 %collective-permute-start.5 = (bf16[144,128]{1,0:T(8,128)(2,1)S(1)}, bf16[144,128]{1,0:T(8,128)(2,1)S(1)}, u32[]{:S(2)}, u32[]{:S(2)}) collective-permute-start(bf16[144,128]{1,0:T(8,128)(2,1)S(1)} %attend.1.refs_0_), channel_id=1, source_target_pairs={{0,12},{4,0},{8,4},{12,8},{1,13},{5,1},{9,5},{13,9},{2,14},{6,2},{... | collective-permute-start | bytes 110600 | tf_op jit(solution)/shard_map/ppermute | solution.py:35
  16.7 1.3 %collective-permute-done.3.refs_1_ = bf16[144,128]{1,0:T(8,128)(2,1)S(1)} collective-permute-done((bf16[144,128]{1,0:T(8,128)(2,1)S(1)}, bf16[144,128]{1,0:T(8,128)(2,1)S(1)}, u32[]{:S(2)}, u32[]{:S(2)}) %collective-permute-start.3) | collective-permute-done | bytes 36896 | tf_op jit(solution)/shard_map/ppermute | solution.py:35
  18.4 1.6 %copy-done.2 = bf16[1024,1024]{1,0:T(8,128)(2,1)S(1)} copy-done((bf16[1024,1024]{1,0:T(8,128)(2,1)S(1)}, bf16[1024,1024]{1,0:T(8,128)(2,1)}, u32[]{:S(2)}) %copy-start.2) | copy-done | bytes 2097176
  20.0 0.8 %project.1.refs_0_ = bf16[16,1024]{1,0:T(8,128)(2,1)S(1)} custom-call(bf16[144,128]{1,0:T(8,128)(2,1)S(1)} %attend.1.refs_0_, bf16[144,128]{1,0:T(8,128)(2,1)S(1)} %collective-permute-done.3.refs_1_, bf16[144,128]{1,0:T(8,128)(2,1)S(1)} %collective-permute-done.4.refs_2_, bf16[144,128]{1,0:T(8,128)(2,1)S(1)} %collective-permute-done.5.refs_3_, ...), custom_call_target="tpu_custom_call" | custom-call | flops 1000000000 | bytes 4194304 | tf_op jit(solution)/shard_map/project/pallas_call | solution.py:215
  20.8 5.0 %collective-permute-start.6 = (bf16[16,1024]{1,0:T(8,128)(2,1)S(1)}, bf16[16,1024]{1,0:T(8,128)(2,1)S(1)}, u32[]{:S(2)}, u32[]{:S(2)}) collective-permute-start(bf16[16,1024]{1,0:T(8,128)(2,1)S(1)} %project.1.refs_0_), channel_id=1, source_target_pairs={{0,1},{1,2},{2,3},{3,0},{4,5},{5,6},{6,7},{7,4},{8,9},{9,10},{10,1... | collective-permute-start | bytes 98312 | tf_op jit(solution)/shard_map/ppermute | solution.py:35
  26.9 1.7 %collective-permute-done.7.refs_2_ = bf16[16,1024]{1,0:T(8,128)(2,1)S(1)} collective-permute-done((bf16[16,1024]{1,0:T(8,128)(2,1)S(1)}, bf16[16,1024]{1,0:T(8,128)(2,1)S(1)}, u32[]{:S(2)}, u32[]{:S(2)}) %collective-permute-start.7) | collective-permute-done | bytes 32800 | tf_op jit(solution)/shard_map/ppermute | solution.py:35
  28.6 0.8 %collective-permute-done.8.refs_3_ = bf16[16,1024]{1,0:T(8,128)(2,1)S(1)} collective-permute-done((bf16[16,1024]{1,0:T(8,128)(2,1)S(1)}, bf16[16,1024]{1,0:T(8,128)(2,1)S(1)}, u32[]{:S(2)}, u32[]{:S(2)}) %collective-permute-start.8) | collective-permute-done | bytes 32800 | tf_op jit(solution)/shard_map/ppermute | solution.py:35
  29.4 0.8 %copy-done.3 = bf16[16,1024]{1,0:T(8,128)(2,1)S(1)} copy-done((bf16[16,1024]{1,0:T(8,128)(2,1)S(1)}, bf16[16,1024]{1,0:T(8,128)(2,1)}, u32[]{:S(2)}) %copy-start.3) | copy-done | bytes 32792
  31.4 2.1 %collective-permute-start.11 = (bf16[16,1152]{1,0:T(8,128)(2,1)S(1)}, bf16[16,1152]{1,0:T(8,128)(2,1)S(1)}, u32[]{:S(2)}, u32[]{:S(2)}) collective-permute-start(bf16[16,1152]{1,0:T(8,128)(2,1)S(1)} %get-tuple-element.13.refs_0_), channel_id=1, source_target_pairs={{0,12},{4,0},{8,4},{12,8},{1,13},{5,1},{9,5},{13,9},{2,14},{6,2},{... | collective-permute-start | bytes 110600 | tf_op jit(solution)/shard_map/ppermute | solution.py:35
  33.6 1.3 %collective-permute-done.10.refs_2_ = bf16[16,1152]{1,0:T(8,128)(2,1)S(1)} collective-permute-done((bf16[16,1152]{1,0:T(8,128)(2,1)S(1)}, bf16[16,1152]{1,0:T(8,128)(2,1)S(1)}, u32[]{:S(2)}, u32[]{:S(2)}) %collective-permute-start.10) | collective-permute-done | bytes 36896 | tf_op jit(solution)/shard_map/ppermute | solution.py:35
  35.3 2.9 %collective-permute-done.9.refs_1_ = bf16[16,1152]{1,0:T(8,128)(2,1)S(1)} collective-permute-done((bf16[16,1152]{1,0:T(8,128)(2,1)S(1)}, bf16[16,1152]{1,0:T(8,128)(2,1)S(1)}, u32[]{:S(2)}, u32[]{:S(2)}) %collective-permute-start.9) | collective-permute-done | bytes 36896 | tf_op jit(solution)/shard_map/ppermute | solution.py:35
  38.8 19.2 %experts.1 = (bf16[16,1024]{1,0:T(8,128)(2,1)}, bf16[16,1024]{1,0:T(8,128)(2,1)}, bf16[16,1024]{1,0:T(8,128)(2,1)}, bf16[16,1024]{1,0:T(8,128)(2,1)}) custom-call(bf16[16,1152]{1,0:T(8,128)(2,1)} %copy-done, bf16[16,1152]{1,0:T(8,128)(2,1)} %copy-done.10, bf16[16,1152]{1,0:T(8,128)(2,1)} %copy-done.8, bf16[16,1152]{1,0:T(8,128)(2,1)} %copy-done.9, ...), custom_call_target="tpu_custom_call" | custom-call | flops 10000000000 | bytes 52428800 | tf_op jit(solution)/shard_map/experts/pallas_call | solution.py:356
  58.5 2.8 %collective-permute-start.14 = (bf16[16,1024]{1,0:T(8,128)(2,1)}, bf16[16,1024]{1,0:T(8,128)(2,1)S(1)}, u32[]{:S(2)}, u32[]{:S(2)}) collective-permute-start(bf16[16,1024]{1,0:T(8,128)(2,1)} %get-tuple-element.17), channel_id=1, source_target_pairs={{0,12},{4,0},{8,4},{12,8},{1,13},{5,1},{9,5},{13,9},{2,14},{6,2},{... | collective-permute-start | bytes 98312 | tf_op jit(solution)/shard_map/ppermute | solution.py:46
  61.3 1.5 %collective-permute-done.12.refs_1_ = bf16[16,1024]{1,0:T(8,128)(2,1)S(1)} collective-permute-done((bf16[16,1024]{1,0:T(8,128)(2,1)}, bf16[16,1024]{1,0:T(8,128)(2,1)S(1)}, u32[]{:S(2)}, u32[]{:S(2)}) %collective-permute-start.12) | collective-permute-done | bytes 32800 | tf_op jit(solution)/shard_map/ppermute | solution.py:46
  63.2 0.8 %copy-done.1 = bf16[16,1024]{1,0:T(8,128)(2,1)S(1)} copy-done((bf16[16,1024]{1,0:T(8,128)(2,1)S(1)}, bf16[16,1024]{1,0:T(8,128)(2,1)}, u32[]{:S(2)}) %copy-start.1) | copy-done | bytes 32792
  64.0 3.6 %collective-permute-start.15 = (bf16[4,1024]{1,0:T(4,128)(2,1)S(1)}, bf16[4,1024]{1,0:T(4,128)(2,1)S(1)}, u32[]{:S(2)}, u32[]{:S(2)}) collective-permute-start(bf16[4,1024]{1,0:T(4,128)(2,1)S(1)} %get-tuple-element.19), channel_id=1, source_target_pairs={{0,1},{1,2},{2,3},{3,0},{4,5},{5,6},{6,7},{7,4},{8,9},{9,10},{10,1... | collective-permute-start | bytes 24584 | tf_op jit(solution)/shard_map/ppermute | solution.py:46
  68.4 1.9 %collective-permute-done.16.refs_2_ = bf16[4,1024]{1,0:T(4,128)(2,1)S(1)} collective-permute-done((bf16[4,1024]{1,0:T(4,128)(2,1)S(1)}, bf16[4,1024]{1,0:T(4,128)(2,1)S(1)}, u32[]{:S(2)}, u32[]{:S(2)}) %collective-permute-start.16) | collective-permute-done | bytes 8224 | tf_op jit(solution)/shard_map/ppermute | solution.py:46
  70.4 1.1 %collective-permute-done.17.refs_3_ = bf16[4,1024]{1,0:T(4,128)(2,1)S(1)} collective-permute-done((bf16[4,1024]{1,0:T(4,128)(2,1)S(1)}, bf16[4,1024]{1,0:T(4,128)(2,1)S(1)}, u32[]{:S(2)}, u32[]{:S(2)}) %collective-permute-start.17) | collective-permute-done | bytes 8224 | tf_op jit(solution)/shard_map/ppermute | solution.py:46
  (42 shorter events, 9.2 us)
Async XLA Ops:
  0.6 8.3 %collective-permute-start = (bf16[4,1024]{1,0:T(4,128)(2,1)}, bf16[4,1024]{1,0:T(4,128)(2,1)S(1)}, u32[]{:S(2)}, u32[]{:S(2)}) collective-permute-start(bf16[4,1024]{1,0:T(4,128)(2,1)} %refs_2_.1), channel_id=1, source_target_pairs={{0,4},{4,8},{8,12},{12,0},{1,5},{5,9},{9,13},{13,1},{2,6},{6,10},{... | collective-permute-start | bytes 24584 | tf_op jit(solution)/shard_map/ppermute | solution.py:35
  2.8 6.1 %collective-permute-start.1 = (bf16[4,1024]{1,0:T(4,128)(2,1)}, bf16[4,1024]{1,0:T(4,128)(2,1)S(1)}, u32[]{:S(2)}, u32[]{:S(2)}) collective-permute-start(bf16[4,1024]{1,0:T(4,128)(2,1)} %refs_2_.1), channel_id=1, source_target_pairs={{0,8},{4,12},{8,0},{12,4},{1,9},{5,13},{9,1},{13,5},{2,10},{6,14},... | collective-permute-start | bytes 24584 | tf_op jit(solution)/shard_map/ppermute | solution.py:35
  5.1 3.8 %collective-permute-start.2 = (bf16[4,1024]{1,0:T(4,128)(2,1)}, bf16[4,1024]{1,0:T(4,128)(2,1)S(1)}, u32[]{:S(2)}, u32[]{:S(2)}) collective-permute-start(bf16[4,1024]{1,0:T(4,128)(2,1)} %refs_2_.1), channel_id=1, source_target_pairs={{0,12},{4,0},{8,4},{12,8},{1,13},{5,1},{9,5},{13,9},{2,14},{6,2},{... | collective-permute-start | bytes 24584 | tf_op jit(solution)/shard_map/ppermute | solution.py:35
  13.4 4.7 %collective-permute-start.3 = (bf16[144,128]{1,0:T(8,128)(2,1)S(1)}, bf16[144,128]{1,0:T(8,128)(2,1)S(1)}, u32[]{:S(2)}, u32[]{:S(2)}) collective-permute-start(bf16[144,128]{1,0:T(8,128)(2,1)S(1)} %attend.1.refs_0_), channel_id=1, source_target_pairs={{0,4},{4,8},{8,12},{12,0},{1,5},{5,9},{9,13},{13,1},{2,6},{6,10},{... | collective-permute-start | bytes 110600 | tf_op jit(solution)/shard_map/ppermute | solution.py:35
  13.8 4.2 %collective-permute-start.4 = (bf16[144,128]{1,0:T(8,128)(2,1)S(1)}, bf16[144,128]{1,0:T(8,128)(2,1)S(1)}, u32[]{:S(2)}, u32[]{:S(2)}) collective-permute-start(bf16[144,128]{1,0:T(8,128)(2,1)S(1)} %attend.1.refs_0_), channel_id=1, source_target_pairs={{0,8},{4,12},{8,0},{12,4},{1,9},{5,13},{9,1},{13,5},{2,10},{6,14},... | collective-permute-start | bytes 110600 | tf_op jit(solution)/shard_map/ppermute | solution.py:35
  15.4 3.0 %collective-permute-start.5 = (bf16[144,128]{1,0:T(8,128)(2,1)S(1)}, bf16[144,128]{1,0:T(8,128)(2,1)S(1)}, u32[]{:S(2)}, u32[]{:S(2)}) collective-permute-start(bf16[144,128]{1,0:T(8,128)(2,1)S(1)} %attend.1.refs_0_), channel_id=1, source_target_pairs={{0,12},{4,0},{8,4},{12,8},{1,13},{5,1},{9,5},{13,9},{2,14},{6,2},{... | collective-permute-start | bytes 110600 | tf_op jit(solution)/shard_map/ppermute | solution.py:35
  18.4 1.6 %copy-start.2 = (bf16[1024,1024]{1,0:T(8,128)(2,1)S(1)}, bf16[1024,1024]{1,0:T(8,128)(2,1)}, u32[]{:S(2)}) copy-start(bf16[1024,1024]{1,0:T(8,128)(2,1)} %refs_4_.2) | copy-start | bytes 6291460
  20.8 6.1 %collective-permute-start.6 = (bf16[16,1024]{1,0:T(8,128)(2,1)S(1)}, bf16[16,1024]{1,0:T(8,128)(2,1)S(1)}, u32[]{:S(2)}, u32[]{:S(2)}) collective-permute-start(bf16[16,1024]{1,0:T(8,128)(2,1)S(1)} %project.1.refs_0_), channel_id=1, source_target_pairs={{0,1},{1,2},{2,3},{3,0},{4,5},{5,6},{6,7},{7,4},{8,9},{9,10},{10,1... | collective-permute-start | bytes 98312 | tf_op jit(solution)/shard_map/ppermute | solution.py:35
  25.8 2.8 %collective-permute-start.7 = (bf16[16,1024]{1,0:T(8,128)(2,1)S(1)}, bf16[16,1024]{1,0:T(8,128)(2,1)S(1)}, u32[]{:S(2)}, u32[]{:S(2)}) collective-permute-start(bf16[16,1024]{1,0:T(8,128)(2,1)S(1)} %project.1.refs_0_), channel_id=1, source_target_pairs={{0,2},{1,3},{2,0},{3,1},{4,6},{5,7},{6,4},{7,5},{8,10},{9,11},{10,... | collective-permute-start | bytes 98312 | tf_op jit(solution)/shard_map/ppermute | solution.py:35
  26.0 3.3 %collective-permute-start.8 = (bf16[16,1024]{1,0:T(8,128)(2,1)S(1)}, bf16[16,1024]{1,0:T(8,128)(2,1)S(1)}, u32[]{:S(2)}, u32[]{:S(2)}) collective-permute-start(bf16[16,1024]{1,0:T(8,128)(2,1)S(1)} %project.1.refs_0_), channel_id=1, source_target_pairs={{0,3},{1,0},{2,1},{3,2},{4,7},{5,4},{6,5},{7,6},{8,11},{9,8},{10,9... | collective-permute-start | bytes 98312 | tf_op jit(solution)/shard_map/ppermute | solution.py:35
  29.4 0.8 %copy-start.3 = (bf16[16,1024]{1,0:T(8,128)(2,1)S(1)}, bf16[16,1024]{1,0:T(8,128)(2,1)}, u32[]{:S(2)}) copy-start(bf16[16,1024]{1,0:T(8,128)(2,1)} %refs_4_.3) | copy-start | bytes 98308
  30.8 7.4 %copy-start = (bf16[16,1152]{1,0:T(8,128)(2,1)}, bf16[16,1152]{1,0:T(8,128)(2,1)S(1)}, u32[]{:S(2)}) copy-start(bf16[16,1152]{1,0:T(8,128)(2,1)S(1)} %get-tuple-element.13.refs_0_) | copy-start | bytes 110596
  30.8 4.1 %collective-permute-start.10 = (bf16[16,1152]{1,0:T(8,128)(2,1)S(1)}, bf16[16,1152]{1,0:T(8,128)(2,1)S(1)}, u32[]{:S(2)}, u32[]{:S(2)}) collective-permute-start(bf16[16,1152]{1,0:T(8,128)(2,1)S(1)} %get-tuple-element.13.refs_0_), channel_id=1, source_target_pairs={{0,8},{4,12},{8,0},{12,4},{1,9},{5,13},{9,1},{13,5},{2,10},{6,14},... | collective-permute-start | bytes 110600 | tf_op jit(solution)/shard_map/ppermute | solution.py:35
  31.4 3.8 %collective-permute-start.11 = (bf16[16,1152]{1,0:T(8,128)(2,1)S(1)}, bf16[16,1152]{1,0:T(8,128)(2,1)S(1)}, u32[]{:S(2)}, u32[]{:S(2)}) collective-permute-start(bf16[16,1152]{1,0:T(8,128)(2,1)S(1)} %get-tuple-element.13.refs_0_), channel_id=1, source_target_pairs={{0,12},{4,0},{8,4},{12,8},{1,13},{5,1},{9,5},{13,9},{2,14},{6,2},{... | collective-permute-start | bytes 110600 | tf_op jit(solution)/shard_map/ppermute | solution.py:35
  33.6 4.6 %collective-permute-start.9 = (bf16[16,1152]{1,0:T(8,128)(2,1)S(1)}, bf16[16,1152]{1,0:T(8,128)(2,1)S(1)}, u32[]{:S(2)}, u32[]{:S(2)}) collective-permute-start(bf16[16,1152]{1,0:T(8,128)(2,1)S(1)} %get-tuple-element.13.refs_0_), channel_id=1, source_target_pairs={{0,4},{4,8},{8,12},{12,0},{1,5},{5,9},{9,13},{13,1},{2,6},{6,10},{... | collective-permute-start | bytes 110600 | tf_op jit(solution)/shard_map/ppermute | solution.py:35
  34.9 3.3 %copy-start.8 = (bf16[16,1152]{1,0:T(8,128)(2,1)}, bf16[16,1152]{1,0:T(8,128)(2,1)S(1)}, u32[]{:S(2)}) copy-start(bf16[16,1152]{1,0:T(8,128)(2,1)S(1)} %collective-permute-done.10.refs_2_) | copy-start | bytes 110596
  35.3 2.9 %copy-start.9 = (bf16[16,1152]{1,0:T(8,128)(2,1)}, bf16[16,1152]{1,0:T(8,128)(2,1)S(1)}, u32[]{:S(2)}) copy-start(bf16[16,1152]{1,0:T(8,128)(2,1)S(1)} %collective-permute-done.11.refs_3_) | copy-start | bytes 110596
  58.0 4.8 %collective-permute-start.12 = (bf16[16,1024]{1,0:T(8,128)(2,1)}, bf16[16,1024]{1,0:T(8,128)(2,1)S(1)}, u32[]{:S(2)}, u32[]{:S(2)}) collective-permute-start(bf16[16,1024]{1,0:T(8,128)(2,1)} %get-tuple-element.15), channel_id=1, source_target_pairs={{0,4},{4,8},{8,12},{12,0},{1,5},{5,9},{9,13},{13,1},{2,6},{6,10},{... | collective-permute-start | bytes 98312 | tf_op jit(solution)/shard_map/ppermute | solution.py:46
  58.1 4.8 %collective-permute-start.13 = (bf16[16,1024]{1,0:T(8,128)(2,1)}, bf16[16,1024]{1,0:T(8,128)(2,1)S(1)}, u32[]{:S(2)}, u32[]{:S(2)}) collective-permute-start(bf16[16,1024]{1,0:T(8,128)(2,1)} %get-tuple-element.16), channel_id=1, source_target_pairs={{0,8},{4,12},{8,0},{12,4},{1,9},{5,13},{9,1},{13,5},{2,10},{6,14},... | collective-permute-start | bytes 98312 | tf_op jit(solution)/shard_map/ppermute | solution.py:46
  58.5 4.7 %collective-permute-start.14 = (bf16[16,1024]{1,0:T(8,128)(2,1)}, bf16[16,1024]{1,0:T(8,128)(2,1)S(1)}, u32[]{:S(2)}, u32[]{:S(2)}) collective-permute-start(bf16[16,1024]{1,0:T(8,128)(2,1)} %get-tuple-element.17), channel_id=1, source_target_pairs={{0,12},{4,0},{8,4},{12,8},{1,13},{5,1},{9,5},{13,9},{2,14},{6,2},{... | collective-permute-start | bytes 98312 | tf_op jit(solution)/shard_map/ppermute | solution.py:46
  63.2 0.8 %copy-start.1 = (bf16[16,1024]{1,0:T(8,128)(2,1)S(1)}, bf16[16,1024]{1,0:T(8,128)(2,1)}, u32[]{:S(2)}) copy-start(bf16[16,1024]{1,0:T(8,128)(2,1)} %get-tuple-element.14.refs_0_) | copy-start | bytes 98308
  64.0 4.4 %collective-permute-start.15 = (bf16[4,1024]{1,0:T(4,128)(2,1)S(1)}, bf16[4,1024]{1,0:T(4,128)(2,1)S(1)}, u32[]{:S(2)}, u32[]{:S(2)}) collective-permute-start(bf16[4,1024]{1,0:T(4,128)(2,1)S(1)} %get-tuple-element.19), channel_id=1, source_target_pairs={{0,1},{1,2},{2,3},{3,0},{4,5},{5,6},{6,7},{7,4},{8,9},{9,10},{10,1... | collective-permute-start | bytes 24584 | tf_op jit(solution)/shard_map/ppermute | solution.py:46
  67.6 2.7 %collective-permute-start.16 = (bf16[4,1024]{1,0:T(4,128)(2,1)S(1)}, bf16[4,1024]{1,0:T(4,128)(2,1)S(1)}, u32[]{:S(2)}, u32[]{:S(2)}) collective-permute-start(bf16[4,1024]{1,0:T(4,128)(2,1)S(1)} %get-tuple-element.20), channel_id=1, source_target_pairs={{0,2},{1,3},{2,0},{3,1},{4,6},{5,7},{6,4},{7,5},{8,10},{9,11},{10,... | collective-permute-start | bytes 24584 | tf_op jit(solution)/shard_map/ppermute | solution.py:46
  68.4 3.1 %collective-permute-start.17 = (bf16[4,1024]{1,0:T(4,128)(2,1)S(1)}, bf16[4,1024]{1,0:T(4,128)(2,1)S(1)}, u32[]{:S(2)}, u32[]{:S(2)}) collective-permute-start(bf16[4,1024]{1,0:T(4,128)(2,1)S(1)} %get-tuple-element.21), channel_id=1, source_target_pairs={{0,3},{1,0},{2,1},{3,2},{4,7},{5,4},{6,5},{7,6},{8,11},{9,8},{10,9... | collective-permute-start | bytes 24584 | tf_op jit(solution)/shard_map/ppermute | solution.py:46
  (5 other events, 3.3 us)

commit v2 on v1

--- a/solution.py
+++ b/solution.py
@@ -64,12 +64,50 @@
     return 1 if count > MOST_PERMUTES else count
 
 
+def load_kernel(cuts, waits, *refs):
+    count = len(cuts)
+    sources, outs, sems = refs[:count], refs[count + waits : -1], refs[-1]
+    copies = []
+    for i, cut in enumerate(cuts):
+        view = sources[i] if cut is None else sources[i].at[cut]
+        copies.append(pltpu.make_async_copy(view, outs[i], sems.at[i]))
+    for copy in copies:
+        copy.start()
+    for copy in copies:
+        copy.wait()
+
+
+def load(items, waits=()):
+    hbm = lambda w: pltpu.with_memory_space_constraint(w, pltpu.HBM)
+    size = sum(math.prod(shape) * array.dtype.itemsize for array, _, shape in items)
+    return pl.pallas_call(
+        functools.partial(load_kernel, [cut for _, cut, _ in items], len(waits)),
+        name="load",
+        out_shape=tuple(pltpu.VMEM(shape, array.dtype) for array, _, shape in items),
+        in_specs=[HBM] * len(items) + [pl.BlockSpec(memory_space=pl.ANY)] * len(waits),
+        out_specs=tuple([VMEM] * len(items)),
+        scratch_shapes=[pltpu.SemaphoreType.DMA((len(items),))],
+        compiler_params=pltpu.CompilerParams(vmem_limit_bytes=1 << 20),
+        cost_estimate=pl.CostEstimate(flops=10**8, bytes_accessed=2 * size, transcendentals=0),
+    )(*[hbm(array) for array, _, _ in items], *waits)
+
+
+def whole(array):
+    return (array, None, array.shape)
+
+
+def rows_of(array, part, parts):
+    step = array.shape[0] // parts
+    return (array, (pl.ds(part * step, step), slice(None)), (step, array.shape[1]))
+
+
 def attend_kernel(count, own_rows, kv_heads, group, positions, *refs):
     taken = grouped(count)
     slot_ref, length_ref = refs[0], refs[1]
     query_refs = refs[2 : 2 + taken]
-    new_ref, cache_ref, out_ref = refs[2 + taken : 5 + taken]
-    q_rows, score, acc, fresh = refs[5 + taken :]
+    new_ref = refs[2 + taken]
+    cache_refs = refs[3 + taken : 3 + taken + kv_heads]
+    out_ref, q_rows, score, acc, fresh = refs[3 + taken + kv_heads :]
     me = lax.axis_index("expert")
     heads = kv_heads * group
     total = count * own_rows
@@ -88,6 +126,10 @@
     position = me * positions + lane // 2
     is_key = lax.rem(lane, 2) == 0
 
+    def cached(b):
+        at = slot_ref[b]
+        return jnp.concatenate([ref[at] for ref in cache_refs], axis=1)
+
     def diagonal(parts):
         return sum(jnp.where(head_of_row == g, parts(g), 0.0) for g in range(kv_heads))
 
@@ -97,7 +139,7 @@
         spread = jnp.concatenate(
             [jnp.where(head_of_row == g, vectors, 0.0) for g in range(kv_heads)], axis=1
         ).astype(BF)
-        both = cache_ref[slot_ref[b]]
+        both = cached(b)
         found = (
             lax.dot_general(
                 spread, both, (((1,), (1,)), ((), ())), preferred_element_type=F32
@@ -109,7 +151,7 @@
 
     def values(b):
         at = pl.ds(pl.multiple_of(b * heads, heads), heads)
-        both = cache_ref[slot_ref[b]]
+        both = cached(b)
         summed = jnp.dot(score[at, :].astype(BF), both, preferred_element_type=F32)
         acc[at, :] = diagonal(lambda g: summed[:, g * HD : (g + 1) * HD])
 
@@ -155,18 +197,18 @@
         out_ref[rows + part * STATS : rows + (part + 1) * STATS, :] = turned[0:STATS, :].astype(BF)
 
 
-def attend(slot_of, lengths, queries, new_kv, cache, count):
+def attend(slot_of, lengths, queries, new_kv, caches, count):
     own_rows, _, kv_width = new_kv.shape
     kv_heads = kv_width // HD
     group = HEADS // KVH
     heads = kv_heads * group
-    positions = cache.shape[1] // 2
+    positions = caches[0].shape[1] // 2
     rows = count * own_rows * heads
     return pl.pallas_call(
         functools.partial(attend_kernel, count, own_rows, kv_heads, group, positions),
         name="attend",
         out_shape=jax.ShapeDtypeStruct((rows + STATS * (rows // LANES), LANES), BF),
-        in_specs=[SMEM, SMEM] + [VMEM] * (len(queries) + 2),
+        in_specs=[SMEM, SMEM] + [VMEM] * (len(queries) + 1 + kv_heads),
         out_specs=VMEM,
         scratch_shapes=[
             pltpu.VMEM((count, own_rows * heads, HD), F32),
@@ -176,7 +218,7 @@
         ],
         compiler_params=pltpu.CompilerParams(vmem_limit_bytes=12 << 20),
         cost_estimate=pl.CostEstimate(flops=10**9, bytes_accessed=4 << 20, transcendentals=0),
-    )(slot_of, lengths, *queries, new_kv, cache)
+    )(slot_of, lengths, *queries, new_kv, *caches)
 
 
 def project_kernel(count, rows, heads, *refs):
@@ -239,7 +281,8 @@
     hidden = resid_ref[...].astype(F32) + attention.astype(F32)
     squares = jnp.sum(hidden * hidden, axis=1, keepdims=True)
     width = hidden.shape[1]
-    out_ref[:, 0:width] = (hidden * gain_ref[...].astype(F32)).astype(BF)
+    gain = gain_ref[...].astype(F32).reshape(1, width)
+    out_ref[:, 0:width] = (hidden * gain).astype(BF)
     high = squares.astype(BF).astype(F32)
     middle = (squares - high).astype(BF).astype(F32)
     low = squares - high - middle
@@ -263,37 +306,27 @@
         scratch_shapes=[pltpu.VMEM((count, rows, width), BF)],
         compiler_params=pltpu.CompilerParams(vmem_limit_bytes=8 << 20),
         cost_estimate=pl.CostEstimate(flops=10**8, bytes_accessed=1 << 20, transcendentals=0),
-    )(*parts, resid, gain.reshape(1, width))
+    )(*parts, resid, gain)
 
 
 def experts_kernel(count, sharing, chunks, *refs):
     taken = grouped(count)
-    part_refs = refs[:taken]
-    ids_ref, logits_ref, gate_hbm, up_hbm, down_hbm = refs[taken : taken + 5]
-    out_refs = refs[taken + 5 : 2 * taken + 5]
-    spread, gate_buf, up_buf, down_buf, act, gate_sem, up_sem, down_sem = refs[2 * taken + 5 :]
+    part_refs, refs = refs[:taken], refs[taken:]
+    ids_ref, logits_ref, refs = refs[0], refs[1], refs[2:]
+    gate_refs, up_refs, refs = refs[:chunks], refs[chunks : 2 * chunks], refs[2 * chunks :]
+    down_hbm, refs = refs[0], refs[1:]
+    out_refs, refs = refs[:taken], refs[taken:]
+    spread, down_buf, act, down_sem = refs
     me = lax.axis_index("expert")
-    depth, hidden_units = gate_buf.shape
+    hidden_units, depth = down_buf.shape
     step = depth // chunks
     down_step = hidden_units // chunks
-    copies = []
-    for c in range(chunks):
-        at = pl.ds(c * step, step)
-        copies.append(
-            (
-                pltpu.make_async_copy(gate_hbm.at[at, :], gate_buf.at[at, :], gate_sem.at[c]),
-                pltpu.make_async_copy(up_hbm.at[at, :], up_buf.at[at, :], up_sem.at[c]),
-            )
-        )
     down_copies = []
     for c in range(chunks):
         at = pl.ds(c * down_step, down_step)
         down_copies.append(
             pltpu.make_async_copy(down_hbm.at[at, :], down_buf.at[at, :], down_sem.at[c])
         )
-    for pair in copies:
-        pair[0].start()
-        pair[1].start()
     for copy in down_copies:
         copy.start()
     rows = spread.shape[0]
@@ -320,12 +353,9 @@
     gate_sum = jnp.zeros((rows, hidden_units), F32)
     up_sum = jnp.zeros((rows, hidden_units), F32)
     for c in range(chunks):
-        at = pl.ds(c * step, step)
-        block = spread[:, at]
-        copies[c][0].wait()
-        gate_sum += jnp.dot(block, gate_buf[at, :], preferred_element_type=F32)
-        copies[c][1].wait()
-        up_sum += jnp.dot(block, up_buf[at, :], preferred_element_type=F32)
+        block = spread[:, c * step : (c + 1) * step]
+        gate_sum += jnp.dot(block, gate_refs[c][...], preferred_element_type=F32)
+        up_sum += jnp.dot(block, up_refs[c][...], preferred_element_type=F32)
     gate_sum = gate_sum * inverse
     act[...] = (gate_sum / (1.0 + jnp.exp(-gate_sum)) * (up_sum * inverse)).astype(BF)
     for copy in down_copies:
@@ -342,36 +372,35 @@
             out_refs[shift][...] = made
 
 
-def experts(parts, ids, logits, gate, up, down, count):
-    depth, hidden_units = gate.shape
-    rows = ids.shape[0]
+def experts(parts, ids, logits, gates, ups, down, count):
+    hidden_units, depth = down.shape
+    rows = ids.shape[1]
     width = depth // count
+    chunks = len(gates)
     stacked = len(parts) != count
-    one = jax.ShapeDtypeStruct((rows, width), BF)
-    out_shape = (
-        (jax.ShapeDtypeStruct((count, rows, width), BF),) if stacked else tuple([one] * count)
-    )
-    chunks = 4
-    hbm = lambda w: pltpu.with_memory_space_constraint(w, pltpu.HBM)
+    one = pltpu.VMEM((rows, width), BF)
+    out_shape = (pltpu.VMEM((count, rows, width), BF),) if stacked else tuple([one] * count)
     return pl.pallas_call(
         functools.partial(experts_kernel, count, count // EXPERTS, chunks),
         name="experts",
         out_shape=out_shape,
-        in_specs=[VMEM] * (len(parts) + 2) + [HBM] * 3,
+        in_specs=[VMEM] * (len(parts) + 2 + 2 * chunks) + [HBM],
         out_specs=tuple([VMEM] * len(out_shape)),
         scratch_shapes=[
             pltpu.VMEM((rows, depth), BF),
-            pltpu.VMEM((depth, hidden_units), BF),
-            pltpu.VMEM((depth, hidden_units), BF),
             pltpu.VMEM((hidden_units, depth), BF),
             pltpu.VMEM((rows, hidden_units), BF),
             pltpu.SemaphoreType.DMA((chunks,)),
-            pltpu.SemaphoreType.DMA((chunks,)),
-            pltpu.SemaphoreType.DMA((chunks,)),
         ],
-        compiler_params=pltpu.CompilerParams(vmem_limit_bytes=58 << 20),
+        compiler_params=pltpu.CompilerParams(vmem_limit_bytes=19 << 20),
         cost_estimate=pl.CostEstimate(flops=10**10, bytes_accessed=50 << 20, transcendentals=0),
-    )(*parts, ids.T, logits.T, hbm(gate), hbm(up), hbm(down))
+    )(
+        *[
+            pltpu.with_memory_space_constraint(w, pltpu.VMEM)
+            for w in (*parts, ids, logits, *gates, *ups)
+        ],
+        pltpu.with_memory_space_constraint(down, pltpu.HBM),
+    )
 
 
 def first_sum_kernel(count, other, *refs):
@@ -442,18 +471,49 @@
     tensor_count = lax.axis_size("tensor")
     total, width = resid.shape
     slots, positions, _, kv_width = kv_prefill.shape
+    gate, up, down = gate_weight_slabs[0], w_up[0], w_down[0]
+    chunks = 4
+    part_of = lambda w, c: rows_of(w, c, chunks)
+    kv_heads = kv_width // HD
     queries = gather(query, "expert")
-    cache = kv_prefill.reshape(slots, 2 * positions, kv_width)
-    part = attend(slot_of, lengths, queries, new_kv, cache, expert_count)
-    projected = project(gather(part, "expert"), wo, expert_count, total)
-    attention, scaled = residual(gather(projected, "tensor"), resid, norm_gain, tensor_count)
+    head_shape = (slots, positions, 2, HD)
+    heads = [
+        (kv_prefill, (slice(None), slice(None), slice(None), pl.ds(g * HD, HD)), head_shape)
+        for g in range(kv_heads)
+    ]
+    loaded = load([whole(query), whole(new_kv), *heads, part_of(gate, 0)])
+    if len(queries) == expert_count:
+        queries[0] = loaded[0]
+    fresh, caches, gate_0 = loaded[1], loaded[2:-1], loaded[-1]
+    caches = [cache.reshape(slots, 2 * positions, HD) for cache in caches]
+    part = attend(slot_of, lengths, queries, fresh, caches, expert_count)
+    parts = gather(part, "expert")
+    wo_here, resid_here, gain_here, ids, logits, gate_1, up_0, up_1 = load(
+        [
+            whole(wo),
+            whole(resid),
+            whole(norm_gain),
+            whole(expert_ids.T),
+            whole(gate_logits.T),
+            part_of(gate, 1),
+            part_of(up, 0),
+            part_of(up, 1),
+        ],
+        [part],
+    )
+    projected = project(parts, wo_here, expert_count, total)
+    attention, scaled = residual(gather(projected, "tensor"), resid_here, gain_here, tensor_count)
+    blocks = gather(scaled, "expert")
+    gate_2, up_2, gate_3, up_3 = load(
+        [part_of(gate, 2), part_of(up, 2), part_of(gate, 3), part_of(up, 3)], [scaled]
+    )
     outgoing = experts(
-        gather(scaled, "expert"),
-        expert_ids,
-        gate_logits,
-        gate_weight_slabs[0],
-        w_up[0],
-        w_down[0],
+        blocks,
+        ids,
+        logits,
+        [gate_0, gate_1, gate_2, gate_3],
+        [up_0, up_1, up_2, up_3],
+        down,
         expert_count,
     )
     column_parts = first_sum(

time: 72.6 us -> 63.1 us (0.87)
  local copies, waits for them, and re-layouts: 9.84 us -> 0.01 us
  Pallas kernels: 23.1 us -> 30.5 us
  waiting for transfers between devices: 13.8 us -> 6.93 us
    pallas_call x0 -> x3, Pallas kernels: none -> 14.2 us  [load(): pl.pallas_call(functools.partial(load_kernel, [cut for _, cut, _ in items...]
    ppermute x12, waiting for transfers between devices: 8.83 us -> 1.76 us  [gather(): lax.ppermute(value, axis, [(i, (i + shift) % count) for i in range(count)])]
    pallas_call x1, Pallas kernels: 19.2 us -> 12.5 us  [experts(): pl.pallas_call(functools.partial(experts_kernel, count, count // EXPERTS,...]
    unnamed x22 -> x4, local copies, waits for them, and re-layouts: 6.41 us -> 0.01 us
    reshape x2 -> x0, local copies, waits for them, and re-layouts: 3.43 us -> none  [the longest x1 2.75 us: shards(): cache = kv_prefill.reshape(slots, 2 * positions, kv_width)]
    ppermute x6, starting transfers between devices: 7.66 us -> 9.65 us  [exchange(): lax.ppermute(values[shift], axis, [(i, (i + shift) % count) for i in rang...]
    ppermute x12, starting transfers between devices: 17 us -> 15.1 us  [gather(): lax.ppermute(value, axis, [(i, (i + shift) % count) for i in range(count)])]
  transfers between devices with their start and end apart: 18 -> 18, of which waited for: 11 -> 7; matrix products, arithmetic and copies ran while one was open for 5% -> 0% of each run, Pallas kernels for 0% -> 23%
where the time goes in v2:
time: 63.1 us; the launch traced here: 62.9 us
  Pallas kernels  30.5 us (48%)
  starting transfers between devices  24.7 us (39%)
  waiting for transfers between devices  6.93 us (11%)
  between operations  0.75 us (1%)
    ppermute x12, starting transfers between devices, gather(): lax.ppermute(value, axis, [(i, (i + shift) % count) for i in range(count)])  15.1 us
    pallas_call x3, Pallas kernels, load(): pl.pallas_call(functools.partial(load_kernel, [cut for _, cut, _ in items...  14.2 us
    pallas_call x1, Pallas kernels, experts(): pl.pallas_call(functools.partial(experts_kernel, count, count // EXPERTS,...  12.5 us
    ppermute x6, starting transfers between devices, exchange(): lax.ppermute(values[shift], axis, [(i, (i + shift) % count) for i in rang...  9.65 us
    ppermute x6, waiting for transfers between devices, exchange(): lax.ppermute(values[shift], axis, [(i, (i + shift) % count) for i in rang...  5.17 us
    ppermute x12, waiting for transfers between devices, gather(): lax.ppermute(value, axis, [(i, (i + shift) % count) for i in range(count)])  1.76 us
    pallas_call x1, Pallas kernels, attend(): pl.pallas_call(functools.partial(attend_kernel, count, own_rows, kv_heads...  1.7 us
  transfers between devices with their start and end apart: 18, of which 7 were waited for; matrix products, arithmetic and copies ran while one was open for 0% of the time, Pallas kernels for 23%

profile of v2, /device:TPU:1, one launch (start us, length us, event | category | flops | bytes accessed | tf_op | source)
XLA Modules:
  0.0 62.9 jit_solution(6336662410402311997)
XLA Ops:
  0.6 2.2 %collective-permute-start = (bf16[4,1024]{1,0:T(4,128)(2,1)}, bf16[4,1024]{1,0:T(4,128)(2,1)S(1)}, u32[]{:S(2)}, u32[]{:S(2)}) collective-permute-start(bf16[4,1024]{1,0:T(4,128)(2,1)} %refs_0_.3), channel_id=1, source_target_pairs={{0,4},{4,8},{8,12},{12,0},{1,5},{5,9},{9,13},{13,1},{2,6},{6,10},{... | collective-permute-start | bytes 24584 | tf_op jit(solution)/shard_map/ppermute | solution.py:35
  2.8 2.1 %collective-permute-start.2 = (bf16[4,1024]{1,0:T(4,128)(2,1)}, bf16[4,1024]{1,0:T(4,128)(2,1)S(1)}, u32[]{:S(2)}, u32[]{:S(2)}) collective-permute-start(bf16[4,1024]{1,0:T(4,128)(2,1)} %refs_0_.3), channel_id=1, source_target_pairs={{0,12},{4,0},{8,4},{12,8},{1,13},{5,1},{9,5},{13,9},{2,14},{6,2},{... | collective-permute-start | bytes 24584 | tf_op jit(solution)/shard_map/ppermute | solution.py:35
  5.3 2.9 %load.3 = (bf16[4,1024]{1,0:T(4,128)(2,1)S(1)}, bf16[4,2,256]{2,1,0:T(2,128)(2,1)S(1)}, bf16[16,128,2,128]{3,2,1,0:T(2,128)(2,1)S(1)}, bf16[16,128,2,128]{3,2,1,0:T(2,128)(2,1)S(1)}, bf16[1024,2048]{1,0:T(8,128)(2,1)S(1)}) custom-call(bf16[4,1024]{1,0:T(4,128)(2,1)} %refs_0_.3, bf16[4,2,256]{2,1,0:T(2,128)(2,1)} %refs_1_.3, ...), custom_call_target="tpu_custom_call" | custom-call | flops 100000000 | bytes 12607488 | tf_op jit(solution)/shard_map/load/pallas_call | solution.py:83
  8.5 1.7 %attend.1.refs_8_.refs_0_ = bf16[144,128]{1,0:T(8,128)(2,1)S(1)} custom-call(s32[16]{0:T(128)S(1)} %copy-done, s32[16]{0:T(128)S(1)} %copy-done.1, bf16[4,1024]{1,0:T(4,128)(2,1)S(1)} %get-tuple-element.29.refs_2_, bf16[4,1024]{1,0:T(4,128)(2,1)S(1)} %collective-permute-done.refs_3_, bf16[4,1024]{1,0:T(4,128)(2,1)S(1)} %collective-permute-done.1.refs_4_, ...), custom_call_target="tpu_custom_call" | custom-call | flops 1000000000 | bytes 4194304 | tf_op jit(solution)/shard_map/attend/pallas_call | solution.py:207
  10.2 1.4 %collective-permute-start.5 = (bf16[144,128]{1,0:T(8,128)(2,1)S(1)}, bf16[144,128]{1,0:T(8,128)(2,1)S(1)}, u32[]{:S(2)}, u32[]{:S(2)}) collective-permute-start(bf16[144,128]{1,0:T(8,128)(2,1)S(1)} %attend.1.refs_8_.refs_0_), channel_id=1, source_target_pairs={{0,12},{4,0},{8,4},{12,8},{1,13},{5,1},{9,5},{13,9},{2,14},{6,2},{... | collective-permute-start | bytes 110600 | tf_op jit(solution)/shard_map/ppermute | solution.py:35
  11.7 0.8 %collective-permute-start.4 = (bf16[144,128]{1,0:T(8,128)(2,1)S(1)}, bf16[144,128]{1,0:T(8,128)(2,1)S(1)}, u32[]{:S(2)}, u32[]{:S(2)}) collective-permute-start(bf16[144,128]{1,0:T(8,128)(2,1)S(1)} %attend.1.refs_8_.refs_0_), channel_id=1, source_target_pairs={{0,8},{4,12},{8,0},{12,4},{1,9},{5,13},{9,1},{13,5},{2,10},{6,14},... | collective-permute-start | bytes 110600 | tf_op jit(solution)/shard_map/ppermute | solution.py:35
  12.5 1.0 %collective-permute-start.3 = (bf16[144,128]{1,0:T(8,128)(2,1)S(1)}, bf16[144,128]{1,0:T(8,128)(2,1)S(1)}, u32[]{:S(2)}, u32[]{:S(2)}) collective-permute-start(bf16[144,128]{1,0:T(8,128)(2,1)S(1)} %attend.1.refs_8_.refs_0_), channel_id=1, source_target_pairs={{0,4},{4,8},{8,12},{12,0},{1,5},{5,9},{9,13},{13,1},{2,6},{6,10},{... | collective-permute-start | bytes 110600 | tf_op jit(solution)/shard_map/ppermute | solution.py:35
  13.5 5.4 %load.4 = (bf16[1024,1024]{1,0:T(8,128)(2,1)S(1)}, bf16[16,1024]{1,0:T(8,128)(2,1)S(1)}, bf16[1024]{0:T(1024)(128)(2,1)S(1)}, s32[2,16]{1,0:T(2,128)S(1)}, f32[2...) custom-call(bf16[1024,1024]{1,0:T(8,128)(2,1)} %refs_0_.5, ...), custom_call_target="tpu_custom_call" | custom-call | flops 100000000 | bytes 29430272 | tf_op jit(solution)/shard_map/load/pallas_call | solution.py:83
  18.9 0.8 %project.1.refs_0_ = bf16[16,1024]{1,0:T(8,128)(2,1)S(1)} custom-call(bf16[144,128]{1,0:T(8,128)(2,1)S(1)} %attend.1.refs_8_.refs_0_, bf16[144,128]{1,0:T(8,128)(2,1)S(1)} %collective-permute-done.3.refs_1_, bf16[144,128]{1,0:T(8,128)(2,1)S(1)} %collective-permute-done.4.refs_2_, bf16[144,128]{1,0:T(8,128)(2,1)S(1)} %collective-permute-done.5.refs_3_, ...), custom_call_target="tpu_custom_call" | custom-call | flops 1000000000 | bytes 4194304 | tf_op jit(solution)/shard_map/project/pallas_call | solution.py:257
  19.6 2.1 %collective-permute-start.8 = (bf16[16,1024]{1,0:T(8,128)(2,1)S(1)}, bf16[16,1024]{1,0:T(8,128)(2,1)S(1)}, u32[]{:S(2)}, u32[]{:S(2)}) collective-permute-start(bf16[16,1024]{1,0:T(8,128)(2,1)S(1)} %project.1.refs_0_), channel_id=1, source_target_pairs={{0,3},{1,0},{2,1},{3,2},{4,7},{5,4},{6,5},{7,6},{8,11},{9,8},{10,9... | collective-permute-start | bytes 98312 | tf_op jit(solution)/shard_map/ppermute | solution.py:35
  21.7 1.4 %collective-permute-start.7 = (bf16[16,1024]{1,0:T(8,128)(2,1)S(1)}, bf16[16,1024]{1,0:T(8,128)(2,1)S(1)}, u32[]{:S(2)}, u32[]{:S(2)}) collective-permute-start(bf16[16,1024]{1,0:T(8,128)(2,1)S(1)} %project.1.refs_0_), channel_id=1, source_target_pairs={{0,2},{1,3},{2,0},{3,1},{4,6},{5,7},{6,4},{7,5},{8,10},{9,11},{10,... | collective-permute-start | bytes 98312 | tf_op jit(solution)/shard_map/ppermute | solution.py:35
  23.4 1.5 %collective-permute-done.8.refs_3_ = bf16[16,1024]{1,0:T(8,128)(2,1)S(1)} collective-permute-done((bf16[16,1024]{1,0:T(8,128)(2,1)S(1)}, bf16[16,1024]{1,0:T(8,128)(2,1)S(1)}, u32[]{:S(2)}, u32[]{:S(2)}) %collective-permute-start.8) | collective-permute-done | bytes 32800 | tf_op jit(solution)/shard_map/ppermute | solution.py:35
  24.8 0.7 %residual.1 = (bf16[16,1024]{1,0:T(8,128)(2,1)}, bf16[16,1152]{1,0:T(8,128)(2,1)S(1)}) custom-call(bf16[16,1024]{1,0:T(8,128)(2,1)S(1)} %project.1.refs_0_, bf16[16,1024]{1,0:T(8,128)(2,1)S(1)} %collective-permute-done.6.refs_1_, bf16[16,1024]{1,0:T(8,128)(2,1)S(1)} %collective-permute-done.7.refs_2_, bf16[16,1024]{1,0:T(8,128)(2,1)S(1)} %collective-permute-done.8.refs_3_, ...), custom_call_target="tpu_custom_call" | custom-call | flops 100000000 | bytes 1048576 | tf_op jit(solution)/shard_map/residual/pallas_call | solution.py:297
  25.5 2.9 %collective-permute-start.11 = (bf16[16,1152]{1,0:T(8,128)(2,1)S(1)}, bf16[16,1152]{1,0:T(8,128)(2,1)S(1)}, u32[]{:S(2)}, u32[]{:S(2)}) collective-permute-start(bf16[16,1152]{1,0:T(8,128)(2,1)S(1)} %get-tuple-element.37.refs_4_.refs_0_), channel_id=1, source_target_pairs={{0,12},{4,0},{8,4},{12,8},{1,13},{5,1},{9,5},{13,9},{2,14},{6,2},{... | collective-permute-start | bytes 110600 | tf_op jit(solution)/shard_map/ppermute | solution.py:35
  29.0 5.9 %load.5 = (bf16[1024,2048]{1,0:T(8,128)(2,1)S(1)}, bf16[1024,2048]{1,0:T(8,128)(2,1)S(1)}, bf16[1024,2048]{1,0:T(8,128)(2,1)S(1)}, bf16[1024,2048]{1,0:T(8,128)(2,1)S(1)}) custom-call(bf16[4096,2048]{1,0:T(8,128)(2,1)} %bitcast.11, bf16[4096,2048]{1,0:T(8,128)(2,1)} %bitcast.15, bf16[4096,2048]{1,0:T(8,128)(2,1)} %bitcast.12, bf16[4096,2048]{1,0:T(8,128)(2,1)} %bitcast.16, ...), custom_call_target="tpu_custom_call" | custom-call | flops 100000000 | bytes 33554432 | tf_op jit(solution)/shard_map/load/pallas_call | solution.py:83
  34.9 12.5 %experts.1 = (bf16[16,1024]{1,0:T(8,128)(2,1)S(1)}, bf16[16,1024]{1,0:T(8,128)(2,1)S(1)}, bf16[16,1024]{1,0:T(8,128)(2,1)S(1)}, bf16[16,1024]{1,0:T(8,128)(2,1)S(1)}) custom-call(bf16[16,1152]{1,0:T(8,128)(2,1)S(1)} %get-tuple-element.37.refs_4_.refs_0_, bf16[16,1152]{1,0:T(8,128)(2,1)S(1)} %collective-permute-done.9.refs_1_, ...), custom_call_target="tpu_custom_call" | custom-call | flops 10000000000 | bytes 52428800 | tf_op jit(solution)/shard_map/experts/pallas_call | solution.py:383
  47.4 2.1 %collective-permute-start.12 = (bf16[16,1024]{1,0:T(8,128)(2,1)S(1)}, bf16[16,1024]{1,0:T(8,128)(2,1)S(1)}, u32[]{:S(2)}, u32[]{:S(2)}) collective-permute-start(bf16[16,1024]{1,0:T(8,128)(2,1)S(1)} %get-tuple-element.49), channel_id=1, source_target_pairs={{0,4},{4,8},{8,12},{12,0},{1,5},{5,9},{9,13},{13,1},{2,6},{6,10},{... | collective-permute-start | bytes 98312 | tf_op jit(solution)/shard_map/ppermute | solution.py:46
  49.5 1.5 %collective-permute-start.13 = (bf16[16,1024]{1,0:T(8,128)(2,1)S(1)}, bf16[16,1024]{1,0:T(8,128)(2,1)S(1)}, u32[]{:S(2)}, u32[]{:S(2)}) collective-permute-start(bf16[16,1024]{1,0:T(8,128)(2,1)S(1)} %get-tuple-element.50), channel_id=1, source_target_pairs={{0,8},{4,12},{8,0},{12,4},{1,9},{5,13},{9,1},{13,5},{2,10},{6,14},... | collective-permute-start | bytes 98312 | tf_op jit(solution)/shard_map/ppermute | solution.py:46
  51.0 0.7 %collective-permute-start.14 = (bf16[16,1024]{1,0:T(8,128)(2,1)S(1)}, bf16[16,1024]{1,0:T(8,128)(2,1)S(1)}, u32[]{:S(2)}, u32[]{:S(2)}) collective-permute-start(bf16[16,1024]{1,0:T(8,128)(2,1)S(1)} %get-tuple-element.51), channel_id=1, source_target_pairs={{0,12},{4,0},{8,4},{12,8},{1,13},{5,1},{9,5},{13,9},{2,14},{6,2},{... | collective-permute-start | bytes 98312 | tf_op jit(solution)/shard_map/ppermute | solution.py:46
  52.0 1.3 %collective-permute-done.13.refs_2_ = bf16[16,1024]{1,0:T(8,128)(2,1)S(1)} collective-permute-done((bf16[16,1024]{1,0:T(8,128)(2,1)S(1)}, bf16[16,1024]{1,0:T(8,128)(2,1)S(1)}, u32[]{:S(2)}, u32[]{:S(2)}) %collective-permute-start.13) | collective-permute-done | bytes 32800 | tf_op jit(solution)/shard_map/ppermute | solution.py:46
  53.8 4.5 %collective-permute-start.15 = (bf16[4,1024]{1,0:T(4,128)(2,1)S(1)}, bf16[4,1024]{1,0:T(4,128)(2,1)S(1)}, u32[]{:S(2)}, u32[]{:S(2)}) collective-permute-start(bf16[4,1024]{1,0:T(4,128)(2,1)S(1)} %get-tuple-element.53), channel_id=1, source_target_pairs={{0,1},{1,2},{2,3},{3,0},{4,5},{5,6},{6,7},{7,4},{8,9},{9,10},{10,1... | collective-permute-start | bytes 24584 | tf_op jit(solution)/shard_map/ppermute | solution.py:46
  58.4 0.9 %collective-permute-start.16 = (bf16[4,1024]{1,0:T(4,128)(2,1)S(1)}, bf16[4,1024]{1,0:T(4,128)(2,1)S(1)}, u32[]{:S(2)}, u32[]{:S(2)}) collective-permute-start(bf16[4,1024]{1,0:T(4,128)(2,1)S(1)} %get-tuple-element.54), channel_id=1, source_target_pairs={{0,2},{1,3},{2,0},{3,1},{4,6},{5,7},{6,4},{7,5},{8,10},{9,11},{10,... | collective-permute-start | bytes 24584 | tf_op jit(solution)/shard_map/ppermute | solution.py:46
  59.2 2.0 %collective-permute-done.16.refs_2_ = bf16[4,1024]{1,0:T(4,128)(2,1)S(1)} collective-permute-done((bf16[4,1024]{1,0:T(4,128)(2,1)S(1)}, bf16[4,1024]{1,0:T(4,128)(2,1)S(1)}, u32[]{:S(2)}, u32[]{:S(2)}) %collective-permute-start.16) | collective-permute-done | bytes 8224 | tf_op jit(solution)/shard_map/ppermute | solution.py:46
  61.2 1.1 %collective-permute-done.17.refs_3_ = bf16[4,1024]{1,0:T(4,128)(2,1)S(1)} collective-permute-done((bf16[4,1024]{1,0:T(4,128)(2,1)S(1)}, bf16[4,1024]{1,0:T(4,128)(2,1)S(1)}, u32[]{:S(2)}, u32[]{:S(2)}) %collective-permute-start.17) | collective-permute-done | bytes 8224 | tf_op jit(solution)/shard_map/ppermute | solution.py:46
  (25 shorter events, 3.1 us)
Async XLA Ops:
  0.6 7.6 %collective-permute-start = (bf16[4,1024]{1,0:T(4,128)(2,1)}, bf16[4,1024]{1,0:T(4,128)(2,1)S(1)}, u32[]{:S(2)}, u32[]{:S(2)}) collective-permute-start(bf16[4,1024]{1,0:T(4,128)(2,1)} %refs_0_.3), channel_id=1, source_target_pairs={{0,4},{4,8},{8,12},{12,0},{1,5},{5,9},{9,13},{13,1},{2,6},{6,10},{... | collective-permute-start | bytes 24584 | tf_op jit(solution)/shard_map/ppermute | solution.py:35
  2.8 5.4 %collective-permute-start.2 = (bf16[4,1024]{1,0:T(4,128)(2,1)}, bf16[4,1024]{1,0:T(4,128)(2,1)S(1)}, u32[]{:S(2)}, u32[]{:S(2)}) collective-permute-start(bf16[4,1024]{1,0:T(4,128)(2,1)} %refs_0_.3), channel_id=1, source_target_pairs={{0,12},{4,0},{8,4},{12,8},{1,13},{5,1},{9,5},{13,9},{2,14},{6,2},{... | collective-permute-start | bytes 24584 | tf_op jit(solution)/shard_map/ppermute | solution.py:35
  4.9 3.6 %collective-permute-start.1 = (bf16[4,1024]{1,0:T(4,128)(2,1)}, bf16[4,1024]{1,0:T(4,128)(2,1)S(1)}, u32[]{:S(2)}, u32[]{:S(2)}) collective-permute-start(bf16[4,1024]{1,0:T(4,128)(2,1)} %refs_0_.3), channel_id=1, source_target_pairs={{0,8},{4,12},{8,0},{12,4},{1,9},{5,13},{9,1},{13,5},{2,10},{6,14},... | collective-permute-start | bytes 24584 | tf_op jit(solution)/shard_map/ppermute | solution.py:35
  5.3 3.2 %copy-start = (s32[16]{0:T(128)S(1)}, s32[16]{0:T(128)}, u32[]{:S(2)}) copy-start(s32[16]{0:T(128)} %refs_0_.4) | copy-start | bytes 196
  5.3 3.2 %copy-start.1 = (s32[16]{0:T(128)S(1)}, s32[16]{0:T(128)}, u32[]{:S(2)}) copy-start(s32[16]{0:T(128)} %refs_1_.4) | copy-start | bytes 196
  10.2 8.6 %collective-permute-start.5 = (bf16[144,128]{1,0:T(8,128)(2,1)S(1)}, bf16[144,128]{1,0:T(8,128)(2,1)S(1)}, u32[]{:S(2)}, u32[]{:S(2)}) collective-permute-start(bf16[144,128]{1,0:T(8,128)(2,1)S(1)} %attend.1.refs_8_.refs_0_), channel_id=1, source_target_pairs={{0,12},{4,0},{8,4},{12,8},{1,13},{5,1},{9,5},{13,9},{2,14},{6,2},{... | collective-permute-start | bytes 110600 | tf_op jit(solution)/shard_map/ppermute | solution.py:35
  11.7 7.2 %collective-permute-start.4 = (bf16[144,128]{1,0:T(8,128)(2,1)S(1)}, bf16[144,128]{1,0:T(8,128)(2,1)S(1)}, u32[]{:S(2)}, u32[]{:S(2)}) collective-permute-start(bf16[144,128]{1,0:T(8,128)(2,1)S(1)} %attend.1.refs_8_.refs_0_), channel_id=1, source_target_pairs={{0,8},{4,12},{8,0},{12,4},{1,9},{5,13},{9,1},{13,5},{2,10},{6,14},... | collective-permute-start | bytes 110600 | tf_op jit(solution)/shard_map/ppermute | solution.py:35
  12.5 6.4 %collective-permute-start.3 = (bf16[144,128]{1,0:T(8,128)(2,1)S(1)}, bf16[144,128]{1,0:T(8,128)(2,1)S(1)}, u32[]{:S(2)}, u32[]{:S(2)}) collective-permute-start(bf16[144,128]{1,0:T(8,128)(2,1)S(1)} %attend.1.refs_8_.refs_0_), channel_id=1, source_target_pairs={{0,4},{4,8},{8,12},{12,0},{1,5},{5,9},{9,13},{13,1},{2,6},{6,10},{... | collective-permute-start | bytes 110600 | tf_op jit(solution)/shard_map/ppermute | solution.py:35
  19.6 5.2 %collective-permute-start.8 = (bf16[16,1024]{1,0:T(8,128)(2,1)S(1)}, bf16[16,1024]{1,0:T(8,128)(2,1)S(1)}, u32[]{:S(2)}, u32[]{:S(2)}) collective-permute-start(bf16[16,1024]{1,0:T(8,128)(2,1)S(1)} %project.1.refs_0_), channel_id=1, source_target_pairs={{0,3},{1,0},{2,1},{3,2},{4,7},{5,4},{6,5},{7,6},{8,11},{9,8},{10,9... | collective-permute-start | bytes 98312 | tf_op jit(solution)/shard_map/ppermute | solution.py:35
  21.7 3.1 %collective-permute-start.7 = (bf16[16,1024]{1,0:T(8,128)(2,1)S(1)}, bf16[16,1024]{1,0:T(8,128)(2,1)S(1)}, u32[]{:S(2)}, u32[]{:S(2)}) collective-permute-start(bf16[16,1024]{1,0:T(8,128)(2,1)S(1)} %project.1.refs_0_), channel_id=1, source_target_pairs={{0,2},{1,3},{2,0},{3,1},{4,6},{5,7},{6,4},{7,5},{8,10},{9,11},{10,... | collective-permute-start | bytes 98312 | tf_op jit(solution)/shard_map/ppermute | solution.py:35
  23.1 1.8 %collective-permute-start.6 = (bf16[16,1024]{1,0:T(8,128)(2,1)S(1)}, bf16[16,1024]{1,0:T(8,128)(2,1)S(1)}, u32[]{:S(2)}, u32[]{:S(2)}) collective-permute-start(bf16[16,1024]{1,0:T(8,128)(2,1)S(1)} %project.1.refs_0_), channel_id=1, source_target_pairs={{0,1},{1,2},{2,3},{3,0},{4,5},{5,6},{6,7},{7,4},{8,9},{9,10},{10,1... | collective-permute-start | bytes 98312 | tf_op jit(solution)/shard_map/ppermute | solution.py:35
  25.5 9.4 %collective-permute-start.11 = (bf16[16,1152]{1,0:T(8,128)(2,1)S(1)}, bf16[16,1152]{1,0:T(8,128)(2,1)S(1)}, u32[]{:S(2)}, u32[]{:S(2)}) collective-permute-start(bf16[16,1152]{1,0:T(8,128)(2,1)S(1)} %get-tuple-element.37.refs_4_.refs_0_), channel_id=1, source_target_pairs={{0,12},{4,0},{8,4},{12,8},{1,13},{5,1},{9,5},{13,9},{2,14},{6,2},{... | collective-permute-start | bytes 110600 | tf_op jit(solution)/shard_map/ppermute | solution.py:35
  28.4 6.5 %collective-permute-start.10 = (bf16[16,1152]{1,0:T(8,128)(2,1)S(1)}, bf16[16,1152]{1,0:T(8,128)(2,1)S(1)}, u32[]{:S(2)}, u32[]{:S(2)}) collective-permute-start(bf16[16,1152]{1,0:T(8,128)(2,1)S(1)} %get-tuple-element.37.refs_4_.refs_0_), channel_id=1, source_target_pairs={{0,8},{4,12},{8,0},{12,4},{1,9},{5,13},{9,1},{13,5},{2,10},{6,14},... | collective-permute-start | bytes 110600 | tf_op jit(solution)/shard_map/ppermute | solution.py:35
  29.0 5.9 %collective-permute-start.9 = (bf16[16,1152]{1,0:T(8,128)(2,1)S(1)}, bf16[16,1152]{1,0:T(8,128)(2,1)S(1)}, u32[]{:S(2)}, u32[]{:S(2)}) collective-permute-start(bf16[16,1152]{1,0:T(8,128)(2,1)S(1)} %get-tuple-element.37.refs_4_.refs_0_), channel_id=1, source_target_pairs={{0,4},{4,8},{8,12},{12,0},{1,5},{5,9},{9,13},{13,1},{2,6},{6,10},{... | collective-permute-start | bytes 110600 | tf_op jit(solution)/shard_map/ppermute | solution.py:35
  47.4 4.6 %collective-permute-start.12 = (bf16[16,1024]{1,0:T(8,128)(2,1)S(1)}, bf16[16,1024]{1,0:T(8,128)(2,1)S(1)}, u32[]{:S(2)}, u32[]{:S(2)}) collective-permute-start(bf16[16,1024]{1,0:T(8,128)(2,1)S(1)} %get-tuple-element.49), channel_id=1, source_target_pairs={{0,4},{4,8},{8,12},{12,0},{1,5},{5,9},{9,13},{13,1},{2,6},{6,10},{... | collective-permute-start | bytes 98312 | tf_op jit(solution)/shard_map/ppermute | solution.py:46
  49.5 3.8 %collective-permute-start.13 = (bf16[16,1024]{1,0:T(8,128)(2,1)S(1)}, bf16[16,1024]{1,0:T(8,128)(2,1)S(1)}, u32[]{:S(2)}, u32[]{:S(2)}) collective-permute-start(bf16[16,1024]{1,0:T(8,128)(2,1)S(1)} %get-tuple-element.50), channel_id=1, source_target_pairs={{0,8},{4,12},{8,0},{12,4},{1,9},{5,13},{9,1},{13,5},{2,10},{6,14},... | collective-permute-start | bytes 98312 | tf_op jit(solution)/shard_map/ppermute | solution.py:46
  51.0 2.8 %collective-permute-start.14 = (bf16[16,1024]{1,0:T(8,128)(2,1)S(1)}, bf16[16,1024]{1,0:T(8,128)(2,1)S(1)}, u32[]{:S(2)}, u32[]{:S(2)}) collective-permute-start(bf16[16,1024]{1,0:T(8,128)(2,1)S(1)} %get-tuple-element.51), channel_id=1, source_target_pairs={{0,12},{4,0},{8,4},{12,8},{1,13},{5,1},{9,5},{13,9},{2,14},{6,2},{... | collective-permute-start | bytes 98312 | tf_op jit(solution)/shard_map/ppermute | solution.py:46
  53.8 5.4 %collective-permute-start.15 = (bf16[4,1024]{1,0:T(4,128)(2,1)S(1)}, bf16[4,1024]{1,0:T(4,128)(2,1)S(1)}, u32[]{:S(2)}, u32[]{:S(2)}) collective-permute-start(bf16[4,1024]{1,0:T(4,128)(2,1)S(1)} %get-tuple-element.53), channel_id=1, source_target_pairs={{0,1},{1,2},{2,3},{3,0},{4,5},{5,6},{6,7},{7,4},{8,9},{9,10},{10,1... | collective-permute-start | bytes 24584 | tf_op jit(solution)/shard_map/ppermute | solution.py:46
  58.4 2.8 %collective-permute-start.16 = (bf16[4,1024]{1,0:T(4,128)(2,1)S(1)}, bf16[4,1024]{1,0:T(4,128)(2,1)S(1)}, u32[]{:S(2)}, u32[]{:S(2)}) collective-permute-start(bf16[4,1024]{1,0:T(4,128)(2,1)S(1)} %get-tuple-element.54), channel_id=1, source_target_pairs={{0,2},{1,3},{2,0},{3,1},{4,6},{5,7},{6,4},{7,5},{8,10},{9,11},{10,... | collective-permute-start | bytes 24584 | tf_op jit(solution)/shard_map/ppermute | solution.py:46
  59.2 3.1 %collective-permute-start.17 = (bf16[4,1024]{1,0:T(4,128)(2,1)S(1)}, bf16[4,1024]{1,0:T(4,128)(2,1)S(1)}, u32[]{:S(2)}, u32[]{:S(2)}) collective-permute-start(bf16[4,1024]{1,0:T(4,128)(2,1)S(1)} %get-tuple-element.55), channel_id=1, source_target_pairs={{0,3},{1,0},{2,1},{3,2},{4,7},{5,4},{6,5},{7,6},{8,11},{9,8},{10,9... | collective-permute-start | bytes 24584 | tf_op jit(solution)/shard_map/ppermute | solution.py:46

commit v3 on v2

--- a/solution.py
+++ b/solution.py
@@ -18,6 +18,7 @@
 LANES = 128
 STATS = 16
 MOST_PERMUTES = 4
+GATE_PARTS = 4
 
 BF = jnp.bfloat16
 F32 = jnp.float32
@@ -77,9 +78,8 @@
         copy.wait()
 
 
-def load(items, waits=()):
+def load(items, waits=(), flops=10**8):
     hbm = lambda w: pltpu.with_memory_space_constraint(w, pltpu.HBM)
-    size = sum(math.prod(shape) * array.dtype.itemsize for array, _, shape in items)
     return pl.pallas_call(
         functools.partial(load_kernel, [cut for _, cut, _ in items], len(waits)),
         name="load",
@@ -88,7 +88,7 @@
         out_specs=tuple([VMEM] * len(items)),
         scratch_shapes=[pltpu.SemaphoreType.DMA((len(items),))],
         compiler_params=pltpu.CompilerParams(vmem_limit_bytes=1 << 20),
-        cost_estimate=pl.CostEstimate(flops=10**8, bytes_accessed=2 * size, transcendentals=0),
+        cost_estimate=pl.CostEstimate(flops=flops, bytes_accessed=1000, transcendentals=0),
     )(*[hbm(array) for array, _, _ in items], *waits)
 
 
@@ -216,8 +216,8 @@
             pltpu.VMEM((rows, HD), F32),
             pltpu.VMEM((2, own_rows * heads, HD), F32),
         ],
-        compiler_params=pltpu.CompilerParams(vmem_limit_bytes=12 << 20),
-        cost_estimate=pl.CostEstimate(flops=10**9, bytes_accessed=4 << 20, transcendentals=0),
+        compiler_params=pltpu.CompilerParams(vmem_limit_bytes=6 << 20),
+        cost_estimate=pl.CostEstimate(flops=10**8, bytes_accessed=1000, transcendentals=0),
     )(slot_of, lengths, *queries, new_kv, *caches)
 
 
@@ -264,8 +264,8 @@
             pltpu.VMEM((rows, HD), F32),
             pltpu.VMEM((total, wo.shape[0]), BF),
         ],
-        compiler_params=pltpu.CompilerParams(vmem_limit_bytes=(12 if len(parts) == count else 48) << 20),
-        cost_estimate=pl.CostEstimate(flops=10**9, bytes_accessed=4 << 20, transcendentals=0),
+        compiler_params=pltpu.CompilerParams(vmem_limit_bytes=(4 if len(parts) == count else 48) << 20),
+        cost_estimate=pl.CostEstimate(flops=10**11, bytes_accessed=1000, transcendentals=0),
     )(*parts, wo)
 
 
@@ -304,31 +304,21 @@
         in_specs=[VMEM] * (len(parts) + 2),
         out_specs=(VMEM, VMEM),
         scratch_shapes=[pltpu.VMEM((count, rows, width), BF)],
-        compiler_params=pltpu.CompilerParams(vmem_limit_bytes=8 << 20),
-        cost_estimate=pl.CostEstimate(flops=10**8, bytes_accessed=1 << 20, transcendentals=0),
+        compiler_params=pltpu.CompilerParams(vmem_limit_bytes=4 << 20),
+        cost_estimate=pl.CostEstimate(flops=10**8, bytes_accessed=1000, transcendentals=0),
     )(*parts, resid, gain)
 
 
-def experts_kernel(count, sharing, chunks, *refs):
+def experts_kernel(count, sharing, gates, *refs):
     taken = grouped(count)
     part_refs, refs = refs[:taken], refs[taken:]
     ids_ref, logits_ref, refs = refs[0], refs[1], refs[2:]
-    gate_refs, up_refs, refs = refs[:chunks], refs[chunks : 2 * chunks], refs[2 * chunks :]
-    down_hbm, refs = refs[0], refs[1:]
+    up_ref, down_ref, refs = *refs[:2], refs[2:]
+    gate_refs, refs = refs[:gates], refs[gates:]
     out_refs, refs = refs[:taken], refs[taken:]
-    spread, down_buf, act, down_sem = refs
+    spread, act = refs
     me = lax.axis_index("expert")
-    hidden_units, depth = down_buf.shape
-    step = depth // chunks
-    down_step = hidden_units // chunks
-    down_copies = []
-    for c in range(chunks):
-        at = pl.ds(c * down_step, down_step)
-        down_copies.append(
-            pltpu.make_async_copy(down_hbm.at[at, :], down_buf.at[at, :], down_sem.at[c])
-        )
-    for copy in down_copies:
-        copy.start()
+    depth = up_ref.shape[0]
     rows = spread.shape[0]
     width = depth // count
     squares = jnp.zeros((rows, 1), F32)
@@ -350,21 +340,19 @@
         jnp.int32, (rows, rows), 1
     )
     mix = jnp.sum(jnp.where(eye, mix_row, 0.0), axis=1, keepdims=True)
-    gate_sum = jnp.zeros((rows, hidden_units), F32)
-    up_sum = jnp.zeros((rows, hidden_units), F32)
-    for c in range(chunks):
-        block = spread[:, c * step : (c + 1) * step]
-        gate_sum += jnp.dot(block, gate_refs[c][...], preferred_element_type=F32)
-        up_sum += jnp.dot(block, up_refs[c][...], preferred_element_type=F32)
+    step = depth // gates
+    gate_sum = sum(
+        jnp.dot(spread[:, i * step : (i + 1) * step], ref[...], preferred_element_type=F32)
+        for i, ref in enumerate(gate_refs)
+    )
+    up_sum = jnp.dot(spread[...], up_ref[...], preferred_element_type=F32)
     gate_sum = gate_sum * inverse
     act[...] = (gate_sum / (1.0 + jnp.exp(-gate_sum)) * (up_sum * inverse)).astype(BF)
-    for copy in down_copies:
-        copy.wait()
     stacked = taken == 1
     for shift in range(count):
         at = target(stacked, count, me, shift)
         columns = pl.ds(pl.multiple_of(at * width, width), width)
-        made = jnp.dot(act[...], down_buf[:, columns], preferred_element_type=F32)
+        made = jnp.dot(act[...], down_ref[:, columns], preferred_element_type=F32)
         made = (made * mix).astype(BF)
         if stacked:
             out_refs[0][shift] = made
@@ -372,35 +360,26 @@
             out_refs[shift][...] = made
 
 
-def experts(parts, ids, logits, gates, ups, down, count):
+def experts(parts, ids, logits, gates, up, down, count):
     hidden_units, depth = down.shape
     rows = ids.shape[1]
     width = depth // count
-    chunks = len(gates)
     stacked = len(parts) != count
     one = pltpu.VMEM((rows, width), BF)
     out_shape = (pltpu.VMEM((count, rows, width), BF),) if stacked else tuple([one] * count)
     return pl.pallas_call(
-        functools.partial(experts_kernel, count, count // EXPERTS, chunks),
+        functools.partial(experts_kernel, count, count // EXPERTS, len(gates)),
         name="experts",
         out_shape=out_shape,
-        in_specs=[VMEM] * (len(parts) + 2 + 2 * chunks) + [HBM],
+        in_specs=[VMEM] * (len(parts) + 4 + len(gates)),
         out_specs=tuple([VMEM] * len(out_shape)),
         scratch_shapes=[
             pltpu.VMEM((rows, depth), BF),
-            pltpu.VMEM((hidden_units, depth), BF),
             pltpu.VMEM((rows, hidden_units), BF),
-            pltpu.SemaphoreType.DMA((chunks,)),
         ],
-        compiler_params=pltpu.CompilerParams(vmem_limit_bytes=19 << 20),
-        cost_estimate=pl.CostEstimate(flops=10**10, bytes_accessed=50 << 20, transcendentals=0),
-    )(
-        *[
-            pltpu.with_memory_space_constraint(w, pltpu.VMEM)
-            for w in (*parts, ids, logits, *gates, *ups)
-        ],
-        pltpu.with_memory_space_constraint(down, pltpu.HBM),
-    )
+        compiler_params=pltpu.CompilerParams(vmem_limit_bytes=(16 if stacked else 4) << 20),
+        cost_estimate=pl.CostEstimate(flops=10**8, bytes_accessed=1000, transcendentals=0),
+    )(*parts, ids, logits, up, down, *gates)
 
 
 def first_sum_kernel(count, other, *refs):
@@ -437,7 +416,7 @@
         out_shape=out_shape,
         in_specs=[VMEM] * len(parts),
         out_specs=tuple([VMEM] * len(out_shape)),
-        compiler_params=pltpu.CompilerParams(vmem_limit_bytes=8 << 20),
+        compiler_params=pltpu.CompilerParams(vmem_limit_bytes=4 << 20),
     )(*parts)
 
 
@@ -448,7 +427,7 @@
         out_shape=jax.ShapeDtypeStruct(shape, BF),
         in_specs=[VMEM] * len(parts),
         out_specs=VMEM,
-        compiler_params=pltpu.CompilerParams(vmem_limit_bytes=8 << 20),
+        compiler_params=pltpu.CompilerParams(vmem_limit_bytes=4 << 20),
     )(*parts)
 
 
@@ -471,9 +450,6 @@
     tensor_count = lax.axis_size("tensor")
     total, width = resid.shape
     slots, positions, _, kv_width = kv_prefill.shape
-    gate, up, down = gate_weight_slabs[0], w_up[0], w_down[0]
-    chunks = 4
-    part_of = lambda w, c: rows_of(w, c, chunks)
     kv_heads = kv_width // HD
     queries = gather(query, "expert")
     head_shape = (slots, positions, 2, HD)
@@ -481,39 +457,28 @@
         (kv_prefill, (slice(None), slice(None), slice(None), pl.ds(g * HD, HD)), head_shape)
         for g in range(kv_heads)
     ]
-    loaded = load([whole(query), whole(new_kv), *heads, part_of(gate, 0)])
+    gate = gate_weight_slabs[0]
+    loaded = load([whole(query), whole(new_kv), *heads, rows_of(gate, 0, GATE_PARTS), rows_of(gate, 1, GATE_PARTS)])
     if len(queries) == expert_count:
         queries[0] = loaded[0]
-    fresh, caches, gate_0 = loaded[1], loaded[2:-1], loaded[-1]
+    fresh, caches = loaded[1], loaded[2 : 2 + kv_heads]
+    gate_0 = loaded[2 + kv_heads]
+    gate_1 = loaded[3 + kv_heads]
     caches = [cache.reshape(slots, 2 * positions, HD) for cache in caches]
     part = attend(slot_of, lengths, queries, fresh, caches, expert_count)
     parts = gather(part, "expert")
-    wo_here, resid_here, gain_here, ids, logits, gate_1, up_0, up_1 = load(
-        [
-            whole(wo),
-            whole(resid),
-            whole(norm_gain),
-            whole(expert_ids.T),
-            whole(gate_logits.T),
-            part_of(gate, 1),
-            part_of(up, 0),
-            part_of(up, 1),
-        ],
-        [part],
-    )
+    wo_here, resid_here, gain_here, gate_2, gate_3 = load([whole(wo), whole(resid), whole(norm_gain), rows_of(gate, 2, GATE_PARTS), rows_of(gate, 3, GATE_PARTS)], [part])
     projected = project(parts, wo_here, expert_count, total)
-    attention, scaled = residual(gather(projected, "tensor"), resid_here, gain_here, tensor_count)
+    partials = gather(projected, "tensor")
+    attention, scaled = residual(partials, resid_here, gain_here, tensor_count)
     blocks = gather(scaled, "expert")
-    gate_2, up_2, gate_3, up_3 = load(
-        [part_of(gate, 2), part_of(up, 2), part_of(gate, 3), part_of(up, 3)], [scaled]
-    )
     outgoing = experts(
         blocks,
-        ids,
-        logits,
-        [gate_0, gate_1, gate_2, gate_3],
-        [up_0, up_1, up_2, up_3],
-        down,
+        expert_ids.T,
+        gate_logits.T,
+        (gate_0, gate_1, gate_2, gate_3),
+        w_up[0],
+        w_down[0],
         expert_count,
     )
     column_parts = first_sum(

time: 63.1 us -> 54.3 us (0.86)
  Pallas kernels: 30.5 us -> 18.7 us
  waiting for transfers between devices: 6.93 us -> 10.8 us
  starting transfers between devices: 24.7 us -> 23.6 us
    pallas_call x3 -> x2, Pallas kernels: 14.2 us -> 8.26 us  [load(): pl.pallas_call(functools.partial(load_kernel, [cut for _, cut, _ in items...]
    pallas_call x1, Pallas kernels: 12.5 us -> 6.62 us  [experts(): pl.pallas_call(functools.partial(experts_kernel, count, count // EXPERTS,...]
    ppermute x12, waiting for transfers between devices: 1.76 us -> 6.1 us  [gather(): lax.ppermute(value, axis, [(i, (i + shift) % count) for i in range(count)])]
    ppermute x6, starting transfers between devices: 9.65 us -> 8.91 us  [exchange(): lax.ppermute(values[shift], axis, [(i, (i + shift) % count) for i in rang...]
  transfers between devices with their start and end apart: 18 -> 18, of which waited for: 7 -> 9; matrix products, arithmetic and copies ran while one was open for 0% -> 0% of each run, Pallas kernels for 23% -> 15%
where the time goes in v3:
time: 54.3 us; the launch traced here: 54.1 us
  starting transfers between devices  23.6 us (43%)
  Pallas kernels  18.7 us (34%)
  waiting for transfers between devices  10.8 us (20%)
  between operations  0.89 us (2%)
    ppermute x12, starting transfers between devices, gather(): lax.ppermute(value, axis, [(i, (i + shift) % count) for i in range(count)])  14.7 us
    ppermute x6, starting transfers between devices, exchange(): lax.ppermute(values[shift], axis, [(i, (i + shift) % count) for i in rang...  8.91 us
    pallas_call x2, Pallas kernels, load(): pl.pallas_call(functools.partial(load_kernel, [cut for _, cut, _ in items...  8.26 us
    pallas_call x1, Pallas kernels, experts(): pl.pallas_call(functools.partial(experts_kernel, count, count // EXPERTS,...  6.62 us
    ppermute x12, waiting for transfers between devices, gather(): lax.ppermute(value, axis, [(i, (i + shift) % count) for i in range(count)])  6.1 us
    ppermute x6, waiting for transfers between devices, exchange(): lax.ppermute(values[shift], axis, [(i, (i + shift) % count) for i in rang...  4.72 us
    pallas_call x1, Pallas kernels, attend(): pl.pallas_call(functools.partial(attend_kernel, count, own_rows, kv_heads...  1.71 us
  transfers between devices with their start and end apart: 18, of which 9 were waited for; matrix products, arithmetic and copies ran while one was open for 0% of the time, Pallas kernels for 15%

profile of v3, /device:TPU:1, one launch (start us, length us, event | category | flops | bytes accessed | tf_op | source)
XLA Modules:
  0.0 54.1 jit_solution(16405875397728758632)
XLA Ops:
  0.6 2.2 %collective-permute-start = (bf16[4,1024]{1,0:T(4,128)(2,1)}, bf16[4,1024]{1,0:T(4,128)(2,1)S(1)}, u32[]{:S(2)}, u32[]{:S(2)}) collective-permute-start(bf16[4,1024]{1,0:T(4,128)(2,1)} %refs_0_.3), channel_id=1, source_target_pairs={{0,4},{4,8},{8,12},{12,0},{1,5},{5,9},{9,13},{13,1},{2,6},{6,10},{... | collective-permute-start | bytes 24584 | tf_op jit(solution)/shard_map/ppermute | solution.py:36
  2.8 2.1 %collective-permute-start.2 = (bf16[4,1024]{1,0:T(4,128)(2,1)}, bf16[4,1024]{1,0:T(4,128)(2,1)S(1)}, u32[]{:S(2)}, u32[]{:S(2)}) collective-permute-start(bf16[4,1024]{1,0:T(4,128)(2,1)} %refs_0_.3), channel_id=1, source_target_pairs={{0,12},{4,0},{8,4},{12,8},{1,13},{5,1},{9,5},{13,9},{2,14},{6,2},{... | collective-permute-start | bytes 24584 | tf_op jit(solution)/shard_map/ppermute | solution.py:36
  5.3 4.1 %load.2 = (bf16[4,1024]{1,0:T(4,128)(2,1)S(1)}, bf16[4,2,256]{2,1,0:T(2,128)(2,1)S(1)}, bf16[16,128,2,128]{3,2,1,0:T(2,128)(2,1)S(1)}, bf16[16,128,2,128]{3,2,1,...) custom-call(bf16[4,1024]{1,0:T(4,128)(2,1)} %refs_0_.3, bf16[4,2,256]{2,1,0:T(2,128)(2,1)} %refs_1_.3, ...), custom_call_target="tpu_custom_call" | custom-call | flops 100000000 | bytes 1000 | tf_op jit(solution)/shard_map/load/pallas_call | solution.py:83
  9.5 1.7 %attend.1.refs_5_.refs_0_ = bf16[144,128]{1,0:T(8,128)(2,1)S(1)} custom-call(s32[16]{0:T(128)S(1)} %copy-done.2, s32[16]{0:T(128)S(1)} %copy-done.3, bf16[4,1024]{1,0:T(4,128)(2,1)S(1)} %get-tuple-element.23.refs_2_, bf16[4,1024]{1,0:T(4,128)(2,1)S(1)} %collective-permute-done.refs_3_, bf16[4,1024]{1,0:T(4,128)(2,1)S(1)} %collective-permute-done.1.refs_4_, ...), custom_call_target="tpu_custom_call" | custom-call | flops 100000000 | bytes 1000 | tf_op jit(solution)/shard_map/attend/pallas_call | solution.py:207
  11.2 1.1 %collective-permute-start.5 = (bf16[144,128]{1,0:T(8,128)(2,1)S(1)}, bf16[144,128]{1,0:T(8,128)(2,1)S(1)}, u32[]{:S(2)}, u32[]{:S(2)}) collective-permute-start(bf16[144,128]{1,0:T(8,128)(2,1)S(1)} %attend.1.refs_5_.refs_0_), channel_id=1, source_target_pairs={{0,12},{4,0},{8,4},{12,8},{1,13},{5,1},{9,5},{13,9},{2,14},{6,2},{... | collective-permute-start | bytes 110600 | tf_op jit(solution)/shard_map/ppermute | solution.py:36
  12.3 1.4 %collective-permute-start.4 = (bf16[144,128]{1,0:T(8,128)(2,1)S(1)}, bf16[144,128]{1,0:T(8,128)(2,1)S(1)}, u32[]{:S(2)}, u32[]{:S(2)}) collective-permute-start(bf16[144,128]{1,0:T(8,128)(2,1)S(1)} %attend.1.refs_5_.refs_0_), channel_id=1, source_target_pairs={{0,8},{4,12},{8,0},{12,4},{1,9},{5,13},{9,1},{13,5},{2,10},{6,14},... | collective-permute-start | bytes 110600 | tf_op jit(solution)/shard_map/ppermute | solution.py:36
  13.7 1.0 %collective-permute-start.3 = (bf16[144,128]{1,0:T(8,128)(2,1)S(1)}, bf16[144,128]{1,0:T(8,128)(2,1)S(1)}, u32[]{:S(2)}, u32[]{:S(2)}) collective-permute-start(bf16[144,128]{1,0:T(8,128)(2,1)S(1)} %attend.1.refs_5_.refs_0_), channel_id=1, source_target_pairs={{0,4},{4,8},{8,12},{12,0},{1,5},{5,9},{9,13},{13,1},{2,6},{6,10},{... | collective-permute-start | bytes 110600 | tf_op jit(solution)/shard_map/ppermute | solution.py:36
  14.7 4.1 %load.3 = (bf16[1024,1024]{1,0:T(8,128)(2,1)S(1)}, bf16[16,1024]{1,0:T(8,128)(2,1)S(1)}, bf16[1024]{0:T(1024)(128)(2,1)S(1)}, bf16[1024,2048]{1,0:T(8,128)(2,1)S(1)}, bf16[1024,2048]{1,0:T(8,128)(2,1)S(1)}) custom-call(bf16[1024,1024]{1,0:T(8,128)(2,1)} %refs_0_.5, bf16[16,1024]{1,0:T(8,128)(2,1)} %refs_1_.5, bf16[1024]{0:T(1024)(128)(2,1)} %refs_2_.3, ...), custom_call_target="tpu_custom_call" | custom-call | flops 100000000 | bytes 1000 | tf_op jit(solution)/shard_map/load/pallas_call | solution.py:83
  18.9 0.8 %project.1.refs_0_ = bf16[16,1024]{1,0:T(8,128)(2,1)S(1)} custom-call(bf16[144,128]{1,0:T(8,128)(2,1)S(1)} %attend.1.refs_5_.refs_0_, bf16[144,128]{1,0:T(8,128)(2,1)S(1)} %collective-permute-done.3.refs_1_, bf16[144,128]{1,0:T(8,128)(2,1)S(1)} %collective-permute-done.4.refs_2_, bf16[144,128]{1,0:T(8,128)(2,1)S(1)} %collective-permute-done.5.refs_3_, ...), custom_call_target="tpu_custom_call" | custom-call | flops 99999997952 | bytes 1000 | tf_op jit(solution)/shard_map/project/pallas_call | solution.py:257
  19.7 2.7 %collective-permute-start.8 = (bf16[16,1024]{1,0:T(8,128)(2,1)S(1)}, bf16[16,1024]{1,0:T(8,128)(2,1)S(1)}, u32[]{:S(2)}, u32[]{:S(2)}) collective-permute-start(bf16[16,1024]{1,0:T(8,128)(2,1)S(1)} %project.1.refs_0_), channel_id=1, source_target_pairs={{0,3},{1,0},{2,1},{3,2},{4,7},{5,4},{6,5},{7,6},{8,11},{9,8},{10,9... | collective-permute-start | bytes 98312 | tf_op jit(solution)/shard_map/ppermute | solution.py:36
  22.4 1.2 %collective-permute-start.7 = (bf16[16,1024]{1,0:T(8,128)(2,1)S(1)}, bf16[16,1024]{1,0:T(8,128)(2,1)S(1)}, u32[]{:S(2)}, u32[]{:S(2)}) collective-permute-start(bf16[16,1024]{1,0:T(8,128)(2,1)S(1)} %project.1.refs_0_), channel_id=1, source_target_pairs={{0,2},{1,3},{2,0},{3,1},{4,6},{5,7},{6,4},{7,5},{8,10},{9,11},{10,... | collective-permute-start | bytes 98312 | tf_op jit(solution)/shard_map/ppermute | solution.py:36
  24.1 1.3 %collective-permute-done.8.refs_3_ = bf16[16,1024]{1,0:T(8,128)(2,1)S(1)} collective-permute-done((bf16[16,1024]{1,0:T(8,128)(2,1)S(1)}, bf16[16,1024]{1,0:T(8,128)(2,1)S(1)}, u32[]{:S(2)}, u32[]{:S(2)}) %collective-permute-start.8) | collective-permute-done | bytes 32800 | tf_op jit(solution)/shard_map/ppermute | solution.py:36
  26.5 2.0 %collective-permute-start.11 = (bf16[16,1152]{1,0:T(8,128)(2,1)S(1)}, bf16[16,1152]{1,0:T(8,128)(2,1)S(1)}, u32[]{:S(2)}, u32[]{:S(2)}) collective-permute-start(bf16[16,1152]{1,0:T(8,128)(2,1)S(1)} %get-tuple-element.31.refs_0_), channel_id=1, source_target_pairs={{0,12},{4,0},{8,4},{12,8},{1,13},{5,1},{9,5},{13,9},{2,14},{6,2},{... | collective-permute-start | bytes 110600 | tf_op jit(solution)/shard_map/ppermute | solution.py:36
  28.7 0.8 %collective-permute-done.11.refs_3_ = bf16[16,1152]{1,0:T(8,128)(2,1)S(1)} collective-permute-done((bf16[16,1152]{1,0:T(8,128)(2,1)S(1)}, bf16[16,1152]{1,0:T(8,128)(2,1)S(1)}, u32[]{:S(2)}, u32[]{:S(2)}) %collective-permute-start.11) | collective-permute-done | bytes 36896 | tf_op jit(solution)/shard_map/ppermute | solution.py:36
  29.5 2.6 %collective-permute-done.10.refs_2_ = bf16[16,1152]{1,0:T(8,128)(2,1)S(1)} collective-permute-done((bf16[16,1152]{1,0:T(8,128)(2,1)S(1)}, bf16[16,1152]{1,0:T(8,128)(2,1)S(1)}, u32[]{:S(2)}, u32[]{:S(2)}) %collective-permute-start.10) | collective-permute-done | bytes 36896 | tf_op jit(solution)/shard_map/ppermute | solution.py:36
  32.2 0.9 %collective-permute-done.9.refs_1_ = bf16[16,1152]{1,0:T(8,128)(2,1)S(1)} collective-permute-done((bf16[16,1152]{1,0:T(8,128)(2,1)S(1)}, bf16[16,1152]{1,0:T(8,128)(2,1)S(1)}, u32[]{:S(2)}, u32[]{:S(2)}) %collective-permute-start.9) | collective-permute-done | bytes 36896 | tf_op jit(solution)/shard_map/ppermute | solution.py:36
  33.2 6.6 %experts.1 = (bf16[16,1024]{1,0:T(8,128)(2,1)S(1)}, bf16[16,1024]{1,0:T(8,128)(2,1)S(1)}, bf16[16,1024]{1,0:T(8,128)(2,1)S(1)}, bf16[16,1024]{1,0:T(8,128)(2,1)S(1)}) custom-call(bf16[16,1152]{1,0:T(8,128)(2,1)S(1)} %get-tuple-element.31.refs_0_, bf16[16,1152]{1,0:T(8,128)(2,1)S(1)} %collective-permute-done.9.refs_1_, ...), custom_call_target="tpu_custom_call" | custom-call | flops 100000000 | bytes 1000 | tf_op jit(solution)/shard_map/experts/pallas_call | solution.py:370
  39.8 0.7 %collective-permute-start.13 = (bf16[16,1024]{1,0:T(8,128)(2,1)S(1)}, bf16[16,1024]{1,0:T(8,128)(2,1)S(1)}, u32[]{:S(2)}, u32[]{:S(2)}) collective-permute-start(bf16[16,1024]{1,0:T(8,128)(2,1)S(1)} %get-tuple-element.38), channel_id=1, source_target_pairs={{0,8},{4,12},{8,0},{12,4},{1,9},{5,13},{9,1},{13,5},{2,10},{6,14},... | collective-permute-start | bytes 98312 | tf_op jit(solution)/shard_map/ppermute | solution.py:47
  40.5 2.6 %collective-permute-start.14 = (bf16[16,1024]{1,0:T(8,128)(2,1)S(1)}, bf16[16,1024]{1,0:T(8,128)(2,1)S(1)}, u32[]{:S(2)}, u32[]{:S(2)}) collective-permute-start(bf16[16,1024]{1,0:T(8,128)(2,1)S(1)} %get-tuple-element.39), channel_id=1, source_target_pairs={{0,12},{4,0},{8,4},{12,8},{1,13},{5,1},{9,5},{13,9},{2,14},{6,2},{... | collective-permute-start | bytes 98312 | tf_op jit(solution)/shard_map/ppermute | solution.py:47
  43.1 1.3 %collective-permute-done.12.refs_1_ = bf16[16,1024]{1,0:T(8,128)(2,1)S(1)} collective-permute-done((bf16[16,1024]{1,0:T(8,128)(2,1)S(1)}, bf16[16,1024]{1,0:T(8,128)(2,1)S(1)}, u32[]{:S(2)}, u32[]{:S(2)}) %collective-permute-start.12) | collective-permute-done | bytes 32800 | tf_op jit(solution)/shard_map/ppermute | solution.py:47
  44.8 4.8 %collective-permute-start.15 = (bf16[4,1024]{1,0:T(4,128)(2,1)S(1)}, bf16[4,1024]{1,0:T(4,128)(2,1)S(1)}, u32[]{:S(2)}, u32[]{:S(2)}) collective-permute-start(bf16[4,1024]{1,0:T(4,128)(2,1)S(1)} %get-tuple-element.41), channel_id=1, source_target_pairs={{0,1},{1,2},{2,3},{3,0},{4,5},{5,6},{6,7},{7,4},{8,9},{9,10},{10,1... | collective-permute-start | bytes 24584 | tf_op jit(solution)/shard_map/ppermute | solution.py:47
  49.6 0.9 %collective-permute-start.16 = (bf16[4,1024]{1,0:T(4,128)(2,1)S(1)}, bf16[4,1024]{1,0:T(4,128)(2,1)S(1)}, u32[]{:S(2)}, u32[]{:S(2)}) collective-permute-start(bf16[4,1024]{1,0:T(4,128)(2,1)S(1)} %get-tuple-element.42), channel_id=1, source_target_pairs={{0,2},{1,3},{2,0},{3,1},{4,6},{5,7},{6,4},{7,5},{8,10},{9,11},{10,... | collective-permute-start | bytes 24584 | tf_op jit(solution)/shard_map/ppermute | solution.py:47
  50.4 2.0 %collective-permute-done.16.refs_2_ = bf16[4,1024]{1,0:T(4,128)(2,1)S(1)} collective-permute-done((bf16[4,1024]{1,0:T(4,128)(2,1)S(1)}, bf16[4,1024]{1,0:T(4,128)(2,1)S(1)}, u32[]{:S(2)}, u32[]{:S(2)}) %collective-permute-start.16) | collective-permute-done | bytes 8224 | tf_op jit(solution)/shard_map/ppermute | solution.py:47
  52.4 1.1 %collective-permute-done.17.refs_3_ = bf16[4,1024]{1,0:T(4,128)(2,1)S(1)} collective-permute-done((bf16[4,1024]{1,0:T(4,128)(2,1)S(1)}, bf16[4,1024]{1,0:T(4,128)(2,1)S(1)}, u32[]{:S(2)}, u32[]{:S(2)}) %collective-permute-start.17) | collective-permute-done | bytes 8224 | tf_op jit(solution)/shard_map/ppermute | solution.py:47
  (46 shorter events, 3.3 us)
Async XLA Ops:
  0.6 8.8 %collective-permute-start = (bf16[4,1024]{1,0:T(4,128)(2,1)}, bf16[4,1024]{1,0:T(4,128)(2,1)S(1)}, u32[]{:S(2)}, u32[]{:S(2)}) collective-permute-start(bf16[4,1024]{1,0:T(4,128)(2,1)} %refs_0_.3), channel_id=1, source_target_pairs={{0,4},{4,8},{8,12},{12,0},{1,5},{5,9},{9,13},{13,1},{2,6},{6,10},{... | collective-permute-start | bytes 24584 | tf_op jit(solution)/shard_map/ppermute | solution.py:36
  2.8 6.7 %collective-permute-start.2 = (bf16[4,1024]{1,0:T(4,128)(2,1)}, bf16[4,1024]{1,0:T(4,128)(2,1)S(1)}, u32[]{:S(2)}, u32[]{:S(2)}) collective-permute-start(bf16[4,1024]{1,0:T(4,128)(2,1)} %refs_0_.3), channel_id=1, source_target_pairs={{0,12},{4,0},{8,4},{12,8},{1,13},{5,1},{9,5},{13,9},{2,14},{6,2},{... | collective-permute-start | bytes 24584 | tf_op jit(solution)/shard_map/ppermute | solution.py:36
  4.9 4.6 %collective-permute-start.1 = (bf16[4,1024]{1,0:T(4,128)(2,1)}, bf16[4,1024]{1,0:T(4,128)(2,1)S(1)}, u32[]{:S(2)}, u32[]{:S(2)}) collective-permute-start(bf16[4,1024]{1,0:T(4,128)(2,1)} %refs_0_.3), channel_id=1, source_target_pairs={{0,8},{4,12},{8,0},{12,4},{1,9},{5,13},{9,1},{13,5},{2,10},{6,14},... | collective-permute-start | bytes 24584 | tf_op jit(solution)/shard_map/ppermute | solution.py:36
  11.2 7.6 %collective-permute-start.5 = (bf16[144,128]{1,0:T(8,128)(2,1)S(1)}, bf16[144,128]{1,0:T(8,128)(2,1)S(1)}, u32[]{:S(2)}, u32[]{:S(2)}) collective-permute-start(bf16[144,128]{1,0:T(8,128)(2,1)S(1)} %attend.1.refs_5_.refs_0_), channel_id=1, source_target_pairs={{0,12},{4,0},{8,4},{12,8},{1,13},{5,1},{9,5},{13,9},{2,14},{6,2},{... | collective-permute-start | bytes 110600 | tf_op jit(solution)/shard_map/ppermute | solution.py:36
  12.3 6.5 %collective-permute-start.4 = (bf16[144,128]{1,0:T(8,128)(2,1)S(1)}, bf16[144,128]{1,0:T(8,128)(2,1)S(1)}, u32[]{:S(2)}, u32[]{:S(2)}) collective-permute-start(bf16[144,128]{1,0:T(8,128)(2,1)S(1)} %attend.1.refs_5_.refs_0_), channel_id=1, source_target_pairs={{0,8},{4,12},{8,0},{12,4},{1,9},{5,13},{9,1},{13,5},{2,10},{6,14},... | collective-permute-start | bytes 110600 | tf_op jit(solution)/shard_map/ppermute | solution.py:36
  13.7 5.1 %collective-permute-start.3 = (bf16[144,128]{1,0:T(8,128)(2,1)S(1)}, bf16[144,128]{1,0:T(8,128)(2,1)S(1)}, u32[]{:S(2)}, u32[]{:S(2)}) collective-permute-start(bf16[144,128]{1,0:T(8,128)(2,1)S(1)} %attend.1.refs_5_.refs_0_), channel_id=1, source_target_pairs={{0,4},{4,8},{8,12},{12,0},{1,5},{5,9},{9,13},{13,1},{2,6},{6,10},{... | collective-permute-start | bytes 110600 | tf_op jit(solution)/shard_map/ppermute | solution.py:36
  18.8 14.2 %slice-start = ((s8[16777216]{0:T(1024)(128)(4,1)}), s8[4194304]{0:T(1024)(128)(4,1)S(1)}, s32[]{:S(2)}) async-start(s8[16777216]{0:T(1024)(128)(4,1)} %bitcast.7), calls=%async_computation | async-start | bytes 8388608
  18.8 14.2 %slice-start.4 = ((s8[16777216]{0:T(1024)(128)(4,1)}), s8[4194304]{0:T(1024)(128)(4,1)S(1)}, s32[]{:S(2)}) async-start(s8[16777216]{0:T(1024)(128)(4,1)} %bitcast.10), calls=%async_computation.4 | async-start | bytes 8388608
  18.9 14.2 %slice-start.1 = ((s8[16777216]{0:T(1024)(128)(4,1)}), s8[4194304]{0:T(1024)(128)(4,1)S(1)}, s32[]{:S(2)}) async-start(s8[16777216]{0:T(1024)(128)(4,1)} %bitcast.7), calls=%async_computation.1 | async-start | bytes 8388608
  18.9 14.2 %slice-start.2 = ((s8[16777216]{0:T(1024)(128)(4,1)}), s8[4194304]{0:T(1024)(128)(4,1)S(1)}, s32[]{:S(2)}) async-start(s8[16777216]{0:T(1024)(128)(4,1)} %bitcast.7), calls=%async_computation.2 | async-start | bytes 8388608
  18.9 14.2 %slice-start.3 = ((s8[16777216]{0:T(1024)(128)(4,1)}), s8[4194304]{0:T(1024)(128)(4,1)S(1)}, s32[]{:S(2)}) async-start(s8[16777216]{0:T(1024)(128)(4,1)} %bitcast.7), calls=%async_computation.3 | async-start | bytes 8388608
  18.9 14.2 %slice-start.5 = ((s8[16777216]{0:T(1024)(128)(4,1)}), s8[4194304]{0:T(1024)(128)(4,1)S(1)}, s32[]{:S(2)}) async-start(s8[16777216]{0:T(1024)(128)(4,1)} %bitcast.10), calls=%async_computation.5 | async-start | bytes 8388608
  19.7 5.7 %collective-permute-start.8 = (bf16[16,1024]{1,0:T(8,128)(2,1)S(1)}, bf16[16,1024]{1,0:T(8,128)(2,1)S(1)}, u32[]{:S(2)}, u32[]{:S(2)}) collective-permute-start(bf16[16,1024]{1,0:T(8,128)(2,1)S(1)} %project.1.refs_0_), channel_id=1, source_target_pairs={{0,3},{1,0},{2,1},{3,2},{4,7},{5,4},{6,5},{7,6},{8,11},{9,8},{10,9... | collective-permute-start | bytes 98312 | tf_op jit(solution)/shard_map/ppermute | solution.py:36
  22.4 3.4 %collective-permute-start.7 = (bf16[16,1024]{1,0:T(8,128)(2,1)S(1)}, bf16[16,1024]{1,0:T(8,128)(2,1)S(1)}, u32[]{:S(2)}, u32[]{:S(2)}) collective-permute-start(bf16[16,1024]{1,0:T(8,128)(2,1)S(1)} %project.1.refs_0_), channel_id=1, source_target_pairs={{0,2},{1,3},{2,0},{3,1},{4,6},{5,7},{6,4},{7,5},{8,10},{9,11},{10,... | collective-permute-start | bytes 98312 | tf_op jit(solution)/shard_map/ppermute | solution.py:36
  23.6 2.2 %collective-permute-start.6 = (bf16[16,1024]{1,0:T(8,128)(2,1)S(1)}, bf16[16,1024]{1,0:T(8,128)(2,1)S(1)}, u32[]{:S(2)}, u32[]{:S(2)}) collective-permute-start(bf16[16,1024]{1,0:T(8,128)(2,1)S(1)} %project.1.refs_0_), channel_id=1, source_target_pairs={{0,1},{1,2},{2,3},{3,0},{4,5},{5,6},{6,7},{7,4},{8,9},{9,10},{10,1... | collective-permute-start | bytes 98312 | tf_op jit(solution)/shard_map/ppermute | solution.py:36
  26.5 3.0 %collective-permute-start.11 = (bf16[16,1152]{1,0:T(8,128)(2,1)S(1)}, bf16[16,1152]{1,0:T(8,128)(2,1)S(1)}, u32[]{:S(2)}, u32[]{:S(2)}) collective-permute-start(bf16[16,1152]{1,0:T(8,128)(2,1)S(1)} %get-tuple-element.31.refs_0_), channel_id=1, source_target_pairs={{0,12},{4,0},{8,4},{12,8},{1,13},{5,1},{9,5},{13,9},{2,14},{6,2},{... | collective-permute-start | bytes 110600 | tf_op jit(solution)/shard_map/ppermute | solution.py:36
  28.5 3.7 %collective-permute-start.10 = (bf16[16,1152]{1,0:T(8,128)(2,1)S(1)}, bf16[16,1152]{1,0:T(8,128)(2,1)S(1)}, u32[]{:S(2)}, u32[]{:S(2)}) collective-permute-start(bf16[16,1152]{1,0:T(8,128)(2,1)S(1)} %get-tuple-element.31.refs_0_), channel_id=1, source_target_pairs={{0,8},{4,12},{8,0},{12,4},{1,9},{5,13},{9,1},{13,5},{2,10},{6,14},... | collective-permute-start | bytes 110600 | tf_op jit(solution)/shard_map/ppermute | solution.py:36
  28.5 4.6 %collective-permute-start.9 = (bf16[16,1152]{1,0:T(8,128)(2,1)S(1)}, bf16[16,1152]{1,0:T(8,128)(2,1)S(1)}, u32[]{:S(2)}, u32[]{:S(2)}) collective-permute-start(bf16[16,1152]{1,0:T(8,128)(2,1)S(1)} %get-tuple-element.31.refs_0_), channel_id=1, source_target_pairs={{0,4},{4,8},{8,12},{12,0},{1,5},{5,9},{9,13},{13,1},{2,6},{6,10},{... | collective-permute-start | bytes 110600 | tf_op jit(solution)/shard_map/ppermute | solution.py:36
  39.8 4.6 %collective-permute-start.12 = (bf16[16,1024]{1,0:T(8,128)(2,1)S(1)}, bf16[16,1024]{1,0:T(8,128)(2,1)S(1)}, u32[]{:S(2)}, u32[]{:S(2)}) collective-permute-start(bf16[16,1024]{1,0:T(8,128)(2,1)S(1)} %get-tuple-element.37), channel_id=1, source_target_pairs={{0,4},{4,8},{8,12},{12,0},{1,5},{5,9},{9,13},{13,1},{2,6},{6,10},{... | collective-permute-start | bytes 98312 | tf_op jit(solution)/shard_map/ppermute | solution.py:47
  39.8 4.6 %collective-permute-start.13 = (bf16[16,1024]{1,0:T(8,128)(2,1)S(1)}, bf16[16,1024]{1,0:T(8,128)(2,1)S(1)}, u32[]{:S(2)}, u32[]{:S(2)}) collective-permute-start(bf16[16,1024]{1,0:T(8,128)(2,1)S(1)} %get-tuple-element.38), channel_id=1, source_target_pairs={{0,8},{4,12},{8,0},{12,4},{1,9},{5,13},{9,1},{13,5},{2,10},{6,14},... | collective-permute-start | bytes 98312 | tf_op jit(solution)/shard_map/ppermute | solution.py:47
  40.5 4.2 %collective-permute-start.14 = (bf16[16,1024]{1,0:T(8,128)(2,1)S(1)}, bf16[16,1024]{1,0:T(8,128)(2,1)S(1)}, u32[]{:S(2)}, u32[]{:S(2)}) collective-permute-start(bf16[16,1024]{1,0:T(8,128)(2,1)S(1)} %get-tuple-element.39), channel_id=1, source_target_pairs={{0,12},{4,0},{8,4},{12,8},{1,13},{5,1},{9,5},{13,9},{2,14},{6,2},{... | collective-permute-start | bytes 98312 | tf_op jit(solution)/shard_map/ppermute | solution.py:47
  44.8 5.6 %collective-permute-start.15 = (bf16[4,1024]{1,0:T(4,128)(2,1)S(1)}, bf16[4,1024]{1,0:T(4,128)(2,1)S(1)}, u32[]{:S(2)}, u32[]{:S(2)}) collective-permute-start(bf16[4,1024]{1,0:T(4,128)(2,1)S(1)} %get-tuple-element.41), channel_id=1, source_target_pairs={{0,1},{1,2},{2,3},{3,0},{4,5},{5,6},{6,7},{7,4},{8,9},{9,10},{10,1... | collective-permute-start | bytes 24584 | tf_op jit(solution)/shard_map/ppermute | solution.py:47
  49.6 2.8 %collective-permute-start.16 = (bf16[4,1024]{1,0:T(4,128)(2,1)S(1)}, bf16[4,1024]{1,0:T(4,128)(2,1)S(1)}, u32[]{:S(2)}, u32[]{:S(2)}) collective-permute-start(bf16[4,1024]{1,0:T(4,128)(2,1)S(1)} %get-tuple-element.42), channel_id=1, source_target_pairs={{0,2},{1,3},{2,0},{3,1},{4,6},{5,7},{6,4},{7,5},{8,10},{9,11},{10,... | collective-permute-start | bytes 24584 | tf_op jit(solution)/shard_map/ppermute | solution.py:47
  50.4 3.1 %collective-permute-start.17 = (bf16[4,1024]{1,0:T(4,128)(2,1)S(1)}, bf16[4,1024]{1,0:T(4,128)(2,1)S(1)}, u32[]{:S(2)}, u32[]{:S(2)}) collective-permute-start(bf16[4,1024]{1,0:T(4,128)(2,1)S(1)} %get-tuple-element.43), channel_id=1, source_target_pairs={{0,3},{1,0},{2,1},{3,2},{4,7},{5,4},{6,5},{7,6},{8,11},{9,8},{10,9... | collective-permute-start | bytes 24584 | tf_op jit(solution)/shard_map/ppermute | solution.py:47
  (6 other events, 65.3 us)

commit v4 on v3

--- a/solution.py
+++ b/solution.py
@@ -19,6 +19,7 @@
 STATS = 16
 MOST_PERMUTES = 4
 GATE_PARTS = 4
+EARLY = (0, 3, 2, 1)
 
 BF = jnp.bfloat16
 F32 = jnp.float32
@@ -70,7 +71,7 @@
     sources, outs, sems = refs[:count], refs[count + waits : -1], refs[-1]
     copies = []
     for i, cut in enumerate(cuts):
-        view = sources[i] if cut is None else sources[i].at[cut]
+        view = sources[i] if cut is None else sources[i].at[cut() if callable(cut) else cut]
         copies.append(pltpu.make_async_copy(view, outs[i], sems.at[i]))
     for copy in copies:
         copy.start()
@@ -96,18 +97,30 @@
     return (array, None, array.shape)
 
 
-def rows_of(array, part, parts):
-    step = array.shape[0] // parts
-    return (array, (pl.ds(part * step, step), slice(None)), (step, array.shape[1]))
-
-
-def attend_kernel(count, own_rows, kv_heads, group, positions, *refs):
+def rows_at(part, count, step, relative):
+    if relative:
+        part = lax.rem(lax.axis_index("expert") - part + count, count)
+        return (pl.ds(pl.multiple_of(part * step, step), step), slice(None))
+    return (pl.ds(part * step, step), slice(None))
+
+
+def rows_of(array, part, count, relative):
+    step = array.shape[0] // count
+    cut = functools.partial(rows_at, part, count, step, relative)
+    return (array, cut, (step, array.shape[1]))
+
+
+def attend_kernel(count, own_rows, kv_heads, group, positions, cut, *refs):
     taken = grouped(count)
     slot_ref, length_ref = refs[0], refs[1]
     query_refs = refs[2 : 2 + taken]
     new_ref = refs[2 + taken]
     cache_refs = refs[3 + taken : 3 + taken + kv_heads]
-    out_ref, q_rows, score, acc, fresh = refs[3 + taken + kv_heads :]
+    chunk_hbm, out_ref, chunk_ref, q_rows, score, acc, fresh, chunk_sem = refs[
+        3 + taken + kv_heads :
+    ]
+    chunk_copy = pltpu.make_async_copy(chunk_hbm.at[cut()], chunk_ref, chunk_sem)
+    chunk_copy.start()
     me = lax.axis_index("expert")
     heads = kv_heads * group
     total = count * own_rows
@@ -195,30 +208,43 @@
     for part in range(rows // LANES):
         turned = table[part * LANES : (part + 1) * LANES, :].T
         out_ref[rows + part * STATS : rows + (part + 1) * STATS, :] = turned[0:STATS, :].astype(BF)
-
-
-def attend(slot_of, lengths, queries, new_kv, caches, count):
+    chunk_copy.wait()
+
+
+def attend(slot_of, lengths, queries, new_kv, caches, chunk, count):
     own_rows, _, kv_width = new_kv.shape
     kv_heads = kv_width // HD
     group = HEADS // KVH
     heads = kv_heads * group
     positions = caches[0].shape[1] // 2
     rows = count * own_rows * heads
-    return pl.pallas_call(
-        functools.partial(attend_kernel, count, own_rows, kv_heads, group, positions),
+    source_array, cut, shape = chunk
+    return pl.pallas_call(
+        functools.partial(attend_kernel, count, own_rows, kv_heads, group, positions, cut),
         name="attend",
-        out_shape=jax.ShapeDtypeStruct((rows + STATS * (rows // LANES), LANES), BF),
-        in_specs=[SMEM, SMEM] + [VMEM] * (len(queries) + 1 + kv_heads),
-        out_specs=VMEM,
+        out_shape=(
+            pltpu.VMEM((rows + STATS * (rows // LANES), LANES), BF),
+            pltpu.VMEM(shape, BF),
+        ),
+        in_specs=[SMEM, SMEM] + [VMEM] * (len(queries) + 1 + kv_heads) + [HBM],
+        out_specs=(VMEM, VMEM),
         scratch_shapes=[
             pltpu.VMEM((count, own_rows * heads, HD), F32),
             pltpu.VMEM((rows, 2 * positions), F32),
             pltpu.VMEM((rows, HD), F32),
             pltpu.VMEM((2, own_rows * heads, HD), F32),
+            pltpu.SemaphoreType.DMA,
         ],
         compiler_params=pltpu.CompilerParams(vmem_limit_bytes=6 << 20),
         cost_estimate=pl.CostEstimate(flops=10**8, bytes_accessed=1000, transcendentals=0),
-    )(slot_of, lengths, *queries, new_kv, *caches)
+    )(
+        slot_of,
+        lengths,
+        *queries,
+        new_kv,
+        *caches,
+        pltpu.with_memory_space_constraint(source_array, pltpu.HBM),
+    )
 
 
 def project_kernel(count, rows, heads, *refs):
@@ -298,8 +324,8 @@
         functools.partial(residual_kernel, count),
         name="residual",
         out_shape=(
-            jax.ShapeDtypeStruct((rows, width), BF),
-            jax.ShapeDtypeStruct((rows, width + LANES), BF),
+            pltpu.VMEM((rows, width), BF),
+            pltpu.VMEM((rows, width + LANES), BF),
         ),
         in_specs=[VMEM] * (len(parts) + 2),
         out_specs=(VMEM, VMEM),
@@ -309,14 +335,35 @@
     )(*parts, resid, gain)
 
 
-def experts_kernel(count, sharing, gates, *refs):
+def gate_kernel(*refs):
+    block_ref, gate_ref, out_ref = refs[0], refs[1], refs[-1]
+    block = block_ref[:, 0 : gate_ref.shape[0]]
+    made = jnp.dot(block, gate_ref[...], preferred_element_type=F32)
+    out_ref[...] = made if len(refs) == 3 else made + refs[2][...]
+
+
+def gate_product(block, gate, before=()):
+    return pl.pallas_call(
+        gate_kernel,
+        name="gate_product",
+        out_shape=pltpu.VMEM((block.shape[0], gate.shape[1]), F32),
+        in_specs=[VMEM] * (2 + len(before)),
+        out_specs=VMEM,
+        compiler_params=pltpu.CompilerParams(vmem_limit_bytes=2 << 20),
+        cost_estimate=pl.CostEstimate(flops=10**8, bytes_accessed=1000, transcendentals=0),
+    )(block, gate, *before)
+
+
+def experts_kernel(count, sharing, gates, cut, *refs):
     taken = grouped(count)
+    stacked = taken == 1
     part_refs, refs = refs[:taken], refs[taken:]
-    ids_ref, logits_ref, refs = refs[0], refs[1], refs[2:]
-    up_ref, down_ref, refs = *refs[:2], refs[2:]
-    gate_refs, refs = refs[:gates], refs[gates:]
+    ids_ref, logits_ref, up_ref, down_ref, last_hbm, refs = *refs[:5], refs[5:]
+    before_refs, refs = refs[:gates], refs[gates:]
     out_refs, refs = refs[:taken], refs[taken:]
-    spread, act = refs
+    spread, act, last_gate, last_sem = refs
+    last_copy = pltpu.make_async_copy(last_hbm.at[cut()], last_gate, last_sem)
+    last_copy.start()
     me = lax.axis_index("expert")
     depth = up_ref.shape[0]
     rows = spread.shape[0]
@@ -340,15 +387,23 @@
         jnp.int32, (rows, rows), 1
     )
     mix = jnp.sum(jnp.where(eye, mix_row, 0.0), axis=1, keepdims=True)
-    step = depth // gates
-    gate_sum = sum(
-        jnp.dot(spread[:, i * step : (i + 1) * step], ref[...], preferred_element_type=F32)
-        for i, ref in enumerate(gate_refs)
-    )
     up_sum = jnp.dot(spread[...], up_ref[...], preferred_element_type=F32)
+    last_copy.wait()
+    step = last_gate.shape[0]
+    if stacked:
+        gate_sum = jnp.dot(
+            spread[:, depth - step :], last_gate[...], preferred_element_type=F32
+        )
+        for i, ref in enumerate(before_refs):
+            gate_sum += jnp.dot(
+                spread[:, i * step : (i + 1) * step], ref[...], preferred_element_type=F32
+            )
+    else:
+        gate_sum = before_refs[0][...] + jnp.dot(
+            part_refs[1][:, 0:width], last_gate[...], preferred_element_type=F32
+        )
     gate_sum = gate_sum * inverse
     act[...] = (gate_sum / (1.0 + jnp.exp(-gate_sum)) * (up_sum * inverse)).astype(BF)
-    stacked = taken == 1
     for shift in range(count):
         at = target(stacked, count, me, shift)
         columns = pl.ds(pl.multiple_of(at * width, width), width)
@@ -360,26 +415,37 @@
             out_refs[shift][...] = made
 
 
-def experts(parts, ids, logits, gates, up, down, count):
+def experts(parts, ids, logits, up, down, last, before, count):
     hidden_units, depth = down.shape
     rows = ids.shape[1]
     width = depth // count
     stacked = len(parts) != count
     one = pltpu.VMEM((rows, width), BF)
     out_shape = (pltpu.VMEM((count, rows, width), BF),) if stacked else tuple([one] * count)
-    return pl.pallas_call(
-        functools.partial(experts_kernel, count, count // EXPERTS, len(gates)),
+    gate, cut, shape = last
+    return pl.pallas_call(
+        functools.partial(experts_kernel, count, count // EXPERTS, len(before), cut),
         name="experts",
         out_shape=out_shape,
-        in_specs=[VMEM] * (len(parts) + 4 + len(gates)),
+        in_specs=[VMEM] * (len(parts) + 4) + [HBM] + [VMEM] * len(before),
         out_specs=tuple([VMEM] * len(out_shape)),
         scratch_shapes=[
             pltpu.VMEM((rows, depth), BF),
             pltpu.VMEM((rows, hidden_units), BF),
+            pltpu.VMEM(shape, BF),
+            pltpu.SemaphoreType.DMA,
         ],
-        compiler_params=pltpu.CompilerParams(vmem_limit_bytes=(16 if stacked else 4) << 20),
+        compiler_params=pltpu.CompilerParams(vmem_limit_bytes=(20 if stacked else 7) << 20),
         cost_estimate=pl.CostEstimate(flops=10**8, bytes_accessed=1000, transcendentals=0),
-    )(*parts, ids, logits, up, down, *gates)
+    )(
+        *parts,
+        ids,
+        logits,
+        up,
+        down,
+        pltpu.with_memory_space_constraint(gate, pltpu.HBM),
+        *before,
+    )
 
 
 def first_sum_kernel(count, other, *refs):
@@ -452,33 +518,46 @@
     slots, positions, _, kv_width = kv_prefill.shape
     kv_heads = kv_width // HD
     queries = gather(query, "expert")
+    relative = len(queries) == expert_count
+    chunk_count = expert_count if relative else GATE_PARTS
+    gate = gate_weight_slabs[0]
+    rows = lambda i: rows_of(gate, i, chunk_count, relative)
+    order = EARLY if relative else tuple(range(chunk_count))
     head_shape = (slots, positions, 2, HD)
     heads = [
         (kv_prefill, (slice(None), slice(None), slice(None), pl.ds(g * HD, HD)), head_shape)
         for g in range(kv_heads)
     ]
-    gate = gate_weight_slabs[0]
-    loaded = load([whole(query), whole(new_kv), *heads, rows_of(gate, 0, GATE_PARTS), rows_of(gate, 1, GATE_PARTS)])
-    if len(queries) == expert_count:
+    loaded = load([whole(query), whole(new_kv), *heads, rows(order[0])])
+    if relative:
         queries[0] = loaded[0]
-    fresh, caches = loaded[1], loaded[2 : 2 + kv_heads]
-    gate_0 = loaded[2 + kv_heads]
-    gate_1 = loaded[3 + kv_heads]
+    fresh, caches, gate_0 = loaded[1], loaded[2 : 2 + kv_heads], loaded[2 + kv_heads]
     caches = [cache.reshape(slots, 2 * positions, HD) for cache in caches]
-    part = attend(slot_of, lengths, queries, fresh, caches, expert_count)
+    part, gate_1 = attend(
+        slot_of, lengths, queries, fresh, caches, rows(order[1]), expert_count
+    )
     parts = gather(part, "expert")
-    wo_here, resid_here, gain_here, gate_2, gate_3 = load([whole(wo), whole(resid), whole(norm_gain), rows_of(gate, 2, GATE_PARTS), rows_of(gate, 3, GATE_PARTS)], [part])
+    wo_here, resid_here, gain_here, gate_2 = load(
+        [whole(wo), whole(resid), whole(norm_gain), rows(order[2])], [part]
+    )
     projected = project(parts, wo_here, expert_count, total)
     partials = gather(projected, "tensor")
     attention, scaled = residual(partials, resid_here, gain_here, tensor_count)
     blocks = gather(scaled, "expert")
+    before = [gate_0, gate_1, gate_2]
+    if relative:
+        made = []
+        for shift, chunk in zip(order, before):
+            made = [gate_product(blocks[shift], chunk, made)]
+        before = made
     outgoing = experts(
         blocks,
         expert_ids.T,
         gate_logits.T,
-        (gate_0, gate_1, gate_2, gate_3),
         w_up[0],
         w_down[0],
+        rows(order[3]),
+        before,
         expert_count,
     )
     column_parts = first_sum(

time: 54.3 us -> 54.8 us (level)
  waiting for transfers between devices: 10.8 us -> 8.8 us
  Pallas kernels: 18.7 us -> 20.3 us
  local copies, waits for them, and re-layouts: 0.06 us -> 0.66 us
    pallas_call x2, Pallas kernels: 8.26 us -> 5.96 us  [load(): pl.pallas_call(functools.partial(load_kernel, [cut for _, cut, _ in items...]
    pallas_call x0 -> x3, Pallas kernels: none -> 1.95 us  [gate_product(): pl.pallas_call(gate_kernel, name='gate_product', out_shape=pltpu.VMEM((bl...]
    pallas_call x1, Pallas kernels: 1.71 us -> 3.59 us  [attend(): pl.pallas_call(functools.partial(attend_kernel, count, own_rows, kv_heads...]
    ppermute x12, waiting for transfers between devices: 6.1 us -> 4.7 us  [gather(): lax.ppermute(value, axis, [(i, (i + shift) % count) for i in range(count)])]
    ppermute x6, waiting for transfers between devices: 4.72 us -> 4.1 us  [exchange(): lax.ppermute(values[shift], axis, [(i, (i + shift) % count) for i in rang...]
    unnamed x24 -> x25, local copies, waits for them, and re-layouts: 0.06 us -> 0.66 us
    pallas_call x1, Pallas kernels: 6.62 us -> 7.19 us  [experts(): pl.pallas_call(functools.partial(experts_kernel, count, count // EXPERTS,...]
  transfers between devices with their start and end apart: 18 -> 18, of which waited for: 9 -> 11; matrix products, arithmetic and copies ran while one was open for 0% -> 1% of each run, Pallas kernels for 15% -> 14%
where the time goes in v4:
time: 54.8 us; the launch traced here: 54.6 us
  starting transfers between devices  24.1 us (44%)
  Pallas kernels  20.3 us (37%)
  waiting for transfers between devices  8.8 us (16%)
  between operations  0.82 us (1%)
  local copies, waits for them, and re-layouts  0.66 us (1%)
    ppermute x12, starting transfers between devices, gather(): lax.ppermute(value, axis, [(i, (i + shift) % count) for i in range(count)])  14.9 us
    ppermute x6, starting transfers between devices, exchange(): lax.ppermute(values[shift], axis, [(i, (i + shift) % count) for i in rang...  9.23 us
    pallas_call x1, Pallas kernels, experts(): pl.pallas_call(functools.partial(experts_kernel, count, count // EXPERTS,...  7.19 us
    pallas_call x2, Pallas kernels, load(): pl.pallas_call(functools.partial(load_kernel, [cut for _, cut, _ in items...  5.96 us
    ppermute x12, waiting for transfers between devices, gather(): lax.ppermute(value, axis, [(i, (i + shift) % count) for i in range(count)])  4.7 us
    ppermute x6, waiting for transfers between devices, exchange(): lax.ppermute(values[shift], axis, [(i, (i + shift) % count) for i in rang...  4.1 us
    pallas_call x1, Pallas kernels, attend(): pl.pallas_call(functools.partial(attend_kernel, count, own_rows, kv_heads...  3.59 us
    pallas_call x3, Pallas kernels, gate_product(): pl.pallas_call(gate_kernel, name='gate_product', out_shape=pltpu.VMEM((bl...  1.95 us
  transfers between devices with their start and end apart: 18, of which 11 were waited for; matrix products, arithmetic and copies ran while one was open for 1% of the time, Pallas kernels for 14%

profile of v4, /device:TPU:1, one launch (start us, length us, event | category | flops | bytes accessed | tf_op | source)
XLA Modules:
  0.0 54.6 jit_solution(5083314262162743445)
XLA Ops:
  0.6 2.2 %collective-permute-start = (bf16[4,1024]{1,0:T(4,128)(2,1)}, bf16[4,1024]{1,0:T(4,128)(2,1)S(1)}, u32[]{:S(2)}, u32[]{:S(2)}) collective-permute-start(bf16[4,1024]{1,0:T(4,128)(2,1)} %refs_0_.3), channel_id=1, source_target_pairs={{0,4},{4,8},{8,12},{12,0},{1,5},{5,9},{9,13},{13,1},{2,6},{6,10},{... | collective-permute-start | bytes 24584 | tf_op jit(solution)/shard_map/ppermute | solution.py:37
  2.8 2.1 %collective-permute-start.2 = (bf16[4,1024]{1,0:T(4,128)(2,1)}, bf16[4,1024]{1,0:T(4,128)(2,1)S(1)}, u32[]{:S(2)}, u32[]{:S(2)}) collective-permute-start(bf16[4,1024]{1,0:T(4,128)(2,1)} %refs_0_.3), channel_id=1, source_target_pairs={{0,12},{4,0},{8,4},{12,8},{1,13},{5,1},{9,5},{13,9},{2,14},{6,2},{... | collective-permute-start | bytes 24584 | tf_op jit(solution)/shard_map/ppermute | solution.py:37
  5.3 2.9 %load.2 = (bf16[4,1024]{1,0:T(4,128)(2,1)S(1)}, bf16[4,2,256]{2,1,0:T(2,128)(2,1)S(1)}, bf16[16,128,2,128]{3,2,1,0:T(2,128)(2,1)S(1)}, bf16[16,128,2,128]{3,2,1,0:T(2,128)(2,1)S(1)}, bf16[1024,2048]{1,0:T(8,128)(2,1)S(1)}) custom-call(bf16[4,1024]{1,0:T(4,128)(2,1)} %refs_0_.3, bf16[4,2,256]{2,1,0:T(2,128)(2,1)} %refs_1_.3, ...), custom_call_target="tpu_custom_call" | custom-call | flops 100000000 | bytes 1000 | tf_op jit(solution)/shard_map/load/pallas_call | solution.py:84
  8.5 3.6 %attend.1 = (bf16[144,128]{1,0:T(8,128)(2,1)S(1)}, bf16[1024,2048]{1,0:T(8,128)(2,1)S(1)}) custom-call(s32[16]{0:T(128)S(1)} %copy-done.2, s32[16]{0:T(128)S(1)} %copy-done.3, bf16[4,1024]{1,0:T(4,128)(2,1)S(1)} %get-tuple-element.23.refs_2_, bf16[4,1024]{1,0:T(4,128)(2,1)S(1)} %collective-permute-done.refs_3_, ...), custom_call_target="tpu_custom_call" | custom-call | flops 100000000 | bytes 1000 | tf_op jit(solution)/shard_map/attend/pallas_call | solution.py:222
  12.1 1.5 %collective-permute-start.5 = (bf16[144,128]{1,0:T(8,128)(2,1)S(1)}, bf16[144,128]{1,0:T(8,128)(2,1)S(1)}, u32[]{:S(2)}, u32[]{:S(2)}) collective-permute-start(bf16[144,128]{1,0:T(8,128)(2,1)S(1)} %get-tuple-element.27.refs_4_.refs_0_), channel_id=1, source_target_pairs={{0,12},{4,0},{8,4},{12,8},{1,13},{5,1},{9,5},{13,9},{2,14},{6,2},{... | collective-permute-start | bytes 110600 | tf_op jit(solution)/shard_map/ppermute | solution.py:37
  13.6 0.8 %collective-permute-start.4 = (bf16[144,128]{1,0:T(8,128)(2,1)S(1)}, bf16[144,128]{1,0:T(8,128)(2,1)S(1)}, u32[]{:S(2)}, u32[]{:S(2)}) collective-permute-start(bf16[144,128]{1,0:T(8,128)(2,1)S(1)} %get-tuple-element.27.refs_4_.refs_0_), channel_id=1, source_target_pairs={{0,8},{4,12},{8,0},{12,4},{1,9},{5,13},{9,1},{13,5},{2,10},{6,14},... | collective-permute-start | bytes 110600 | tf_op jit(solution)/shard_map/ppermute | solution.py:37
  14.4 1.0 %collective-permute-start.3 = (bf16[144,128]{1,0:T(8,128)(2,1)S(1)}, bf16[144,128]{1,0:T(8,128)(2,1)S(1)}, u32[]{:S(2)}, u32[]{:S(2)}) collective-permute-start(bf16[144,128]{1,0:T(8,128)(2,1)S(1)} %get-tuple-element.27.refs_4_.refs_0_), channel_id=1, source_target_pairs={{0,4},{4,8},{8,12},{12,0},{1,5},{5,9},{9,13},{13,1},{2,6},{6,10},{... | collective-permute-start | bytes 110600 | tf_op jit(solution)/shard_map/ppermute | solution.py:37
  15.4 3.0 %load.3 = (bf16[1024,1024]{1,0:T(8,128)(2,1)S(1)}, bf16[16,1024]{1,0:T(8,128)(2,1)S(1)}, bf16[1024]{0:T(1024)(128)(2,1)S(1)}, bf16[1024,2048]{1,0:T(8,128)(2,1)S(1)}) custom-call(bf16[1024,1024]{1,0:T(8,128)(2,1)} %refs_0_.5, bf16[16,1024]{1,0:T(8,128)(2,1)} %refs_1_.5, bf16[1024]{0:T(1024)(128)(2,1)} %refs_2_.3, bf16[4096,2048]{1,0:T(8,128)(2,1)} %bitcast.19, ...), custom_call_target="tpu_custom_call" | custom-call | flops 100000000 | bytes 1000 | tf_op jit(solution)/shard_map/load/pallas_call | solution.py:84
  19.0 0.8 %project.1.refs_0_ = bf16[16,1024]{1,0:T(8,128)(2,1)S(1)} custom-call(bf16[144,128]{1,0:T(8,128)(2,1)S(1)} %get-tuple-element.27.refs_4_.refs_0_, bf16[144,128]{1,0:T(8,128)(2,1)S(1)} %collective-permute-done.3.refs_1_, bf16[144,128]{1,0:T(8,128)(2,1)S(1)} %collective-permute-done.4.refs_2_, bf16[144,128]{1,0:T(8,128)(2,1)S(1)} %collective-permute-done.5.refs_3_, ...), custom_call_target="tpu_custom_call" | custom-call | flops 99999997952 | bytes 1000 | tf_op jit(solution)/shard_map/project/pallas_call | solution.py:283
  19.8 3.2 %collective-permute-start.8 = (bf16[16,1024]{1,0:T(8,128)(2,1)S(1)}, bf16[16,1024]{1,0:T(8,128)(2,1)S(1)}, u32[]{:S(2)}, u32[]{:S(2)}) collective-permute-start(bf16[16,1024]{1,0:T(8,128)(2,1)S(1)} %project.1.refs_0_), channel_id=1, source_target_pairs={{0,3},{1,0},{2,1},{3,2},{4,7},{5,4},{6,5},{7,6},{8,11},{9,8},{10,9... | collective-permute-start | bytes 98312 | tf_op jit(solution)/shard_map/ppermute | solution.py:37
  23.1 1.2 %collective-permute-start.7 = (bf16[16,1024]{1,0:T(8,128)(2,1)S(1)}, bf16[16,1024]{1,0:T(8,128)(2,1)S(1)}, u32[]{:S(2)}, u32[]{:S(2)}) collective-permute-start(bf16[16,1024]{1,0:T(8,128)(2,1)S(1)} %project.1.refs_0_), channel_id=1, source_target_pairs={{0,2},{1,3},{2,0},{3,1},{4,6},{5,7},{6,4},{7,5},{8,10},{9,11},{10,... | collective-permute-start | bytes 98312 | tf_op jit(solution)/shard_map/ppermute | solution.py:37
  24.7 1.3 %collective-permute-done.8.refs_3_ = bf16[16,1024]{1,0:T(8,128)(2,1)S(1)} collective-permute-done((bf16[16,1024]{1,0:T(8,128)(2,1)S(1)}, bf16[16,1024]{1,0:T(8,128)(2,1)S(1)}, u32[]{:S(2)}, u32[]{:S(2)}) %collective-permute-start.8) | collective-permute-done | bytes 32800 | tf_op jit(solution)/shard_map/ppermute | solution.py:37
  26.6 0.9 %collective-permute-start.11 = (bf16[16,1152]{1,0:T(8,128)(2,1)S(1)}, bf16[16,1152]{1,0:T(8,128)(2,1)S(1)}, u32[]{:S(2)}, u32[]{:S(2)}) collective-permute-start(bf16[16,1152]{1,0:T(8,128)(2,1)S(1)} %get-tuple-element.32.refs_0_), channel_id=1, source_target_pairs={{0,12},{4,0},{8,4},{12,8},{1,13},{5,1},{9,5},{13,9},{2,14},{6,2},{... | collective-permute-start | bytes 110600 | tf_op jit(solution)/shard_map/ppermute | solution.py:37
  29.4 0.7 %gate_product.4.refs_2_ = f32[16,2048]{1,0:T(8,128)S(1)} custom-call(bf16[16,1152]{1,0:T(8,128)(2,1)S(1)} %collective-permute-done.11.refs_0_.refs_3_, bf16[1024,2048]{1,0:T(8,128)(2,1)S(1)} %get-tuple-element.34.refs_1_, f32[16,2048]{1,0:T(8,128)S(1)} %gate_product.3.refs_2_), custom_call_target="tpu_custom_call" | custom-call | flops 100000000 | bytes 1000 | tf_op jit(solution)/shard_map/gate_product/pallas_call | solution.py:346
  30.1 1.8 %collective-permute-done.10.refs_0_.refs_2_ = bf16[16,1152]{1,0:T(8,128)(2,1)S(1)} collective-permute-done((bf16[16,1152]{1,0:T(8,128)(2,1)S(1)}, bf16[16,1152]{1,0:T(8,128)(2,1)S(1)}, u32[]{:S(2)}, u32[]{:S(2)}) %collective-permute-start.10) | collective-permute-done | bytes 36896 | tf_op jit(solution)/shard_map/ppermute | solution.py:37
  31.9 0.6 %gate_product.5.refs_9_ = f32[16,2048]{1,0:T(8,128)S(1)} custom-call(bf16[16,1152]{1,0:T(8,128)(2,1)S(1)} %collective-permute-done.10.refs_0_.refs_2_, bf16[1024,2048]{1,0:T(8,128)(2,1)S(1)} %get-tuple-element.33.refs_1_, f32[16,2048]{1,0:T(8,128)S(1)} %gate_product.4.refs_2_), custom_call_target="tpu_custom_call" | custom-call | flops 100000000 | bytes 1000 | tf_op jit(solution)/shard_map/gate_product/pallas_call | solution.py:346
  32.8 7.2 %experts.1 = (bf16[16,1024]{1,0:T(8,128)(2,1)S(1)}, bf16[16,1024]{1,0:T(8,128)(2,1)S(1)}, bf16[16,1024]{1,0:T(8,128)(2,1)S(1)}, bf16[16,1024]{1,0:T(8,128)(2,1)S(1)}) custom-call(bf16[16,1152]{1,0:T(8,128)(2,1)S(1)} %get-tuple-element.32.refs_0_, bf16[16,1152]{1,0:T(8,128)(2,1)S(1)} %collective-permute-done.9.refs_1_, ...), custom_call_target="tpu_custom_call" | custom-call | flops 100000000 | bytes 1000 | tf_op jit(solution)/shard_map/experts/pallas_call | solution.py:426
  40.1 1.2 %collective-permute-start.13 = (bf16[16,1024]{1,0:T(8,128)(2,1)S(1)}, bf16[16,1024]{1,0:T(8,128)(2,1)S(1)}, u32[]{:S(2)}, u32[]{:S(2)}) collective-permute-start(bf16[16,1024]{1,0:T(8,128)(2,1)S(1)} %get-tuple-element.38), channel_id=1, source_target_pairs={{0,8},{4,12},{8,0},{12,4},{1,9},{5,13},{9,1},{13,5},{2,10},{6,14},... | collective-permute-start | bytes 98312 | tf_op jit(solution)/shard_map/ppermute | solution.py:48
  41.3 2.0 %collective-permute-start.14 = (bf16[16,1024]{1,0:T(8,128)(2,1)S(1)}, bf16[16,1024]{1,0:T(8,128)(2,1)S(1)}, u32[]{:S(2)}, u32[]{:S(2)}) collective-permute-start(bf16[16,1024]{1,0:T(8,128)(2,1)S(1)} %get-tuple-element.39), channel_id=1, source_target_pairs={{0,12},{4,0},{8,4},{12,8},{1,13},{5,1},{9,5},{13,9},{2,14},{6,2},{... | collective-permute-start | bytes 98312 | tf_op jit(solution)/shard_map/ppermute | solution.py:48
  43.3 1.3 %collective-permute-done.12.refs_1_ = bf16[16,1024]{1,0:T(8,128)(2,1)S(1)} collective-permute-done((bf16[16,1024]{1,0:T(8,128)(2,1)S(1)}, bf16[16,1024]{1,0:T(8,128)(2,1)S(1)}, u32[]{:S(2)}, u32[]{:S(2)}) %collective-permute-start.12) | collective-permute-done | bytes 32800 | tf_op jit(solution)/shard_map/ppermute | solution.py:48
  45.0 5.1 %collective-permute-start.15 = (bf16[4,1024]{1,0:T(4,128)(2,1)S(1)}, bf16[4,1024]{1,0:T(4,128)(2,1)S(1)}, u32[]{:S(2)}, u32[]{:S(2)}) collective-permute-start(bf16[4,1024]{1,0:T(4,128)(2,1)S(1)} %get-tuple-element.41), channel_id=1, source_target_pairs={{0,1},{1,2},{2,3},{3,0},{4,5},{5,6},{6,7},{7,4},{8,9},{9,10},{10,1... | collective-permute-start | bytes 24584 | tf_op jit(solution)/shard_map/ppermute | solution.py:48
  50.1 0.9 %collective-permute-start.16 = (bf16[4,1024]{1,0:T(4,128)(2,1)S(1)}, bf16[4,1024]{1,0:T(4,128)(2,1)S(1)}, u32[]{:S(2)}, u32[]{:S(2)}) collective-permute-start(bf16[4,1024]{1,0:T(4,128)(2,1)S(1)} %get-tuple-element.42), channel_id=1, source_target_pairs={{0,2},{1,3},{2,0},{3,1},{4,6},{5,7},{6,4},{7,5},{8,10},{9,11},{10,... | collective-permute-start | bytes 24584 | tf_op jit(solution)/shard_map/ppermute | solution.py:48
  51.6 1.4 %collective-permute-done.16.refs_2_ = bf16[4,1024]{1,0:T(4,128)(2,1)S(1)} collective-permute-done((bf16[4,1024]{1,0:T(4,128)(2,1)S(1)}, bf16[4,1024]{1,0:T(4,128)(2,1)S(1)}, u32[]{:S(2)}, u32[]{:S(2)}) %collective-permute-start.16) | collective-permute-done | bytes 8224 | tf_op jit(solution)/shard_map/ppermute | solution.py:48
  52.9 1.1 %collective-permute-done.17.refs_3_ = bf16[4,1024]{1,0:T(4,128)(2,1)S(1)} collective-permute-done((bf16[4,1024]{1,0:T(4,128)(2,1)S(1)}, bf16[4,1024]{1,0:T(4,128)(2,1)S(1)}, u32[]{:S(2)}, u32[]{:S(2)}) %collective-permute-start.17) | collective-permute-done | bytes 8224 | tf_op jit(solution)/shard_map/ppermute | solution.py:48
  (50 shorter events, 6.1 us)
Async XLA Ops:
  0.6 7.6 %collective-permute-start = (bf16[4,1024]{1,0:T(4,128)(2,1)}, bf16[4,1024]{1,0:T(4,128)(2,1)S(1)}, u32[]{:S(2)}, u32[]{:S(2)}) collective-permute-start(bf16[4,1024]{1,0:T(4,128)(2,1)} %refs_0_.3), channel_id=1, source_target_pairs={{0,4},{4,8},{8,12},{12,0},{1,5},{5,9},{9,13},{13,1},{2,6},{6,10},{... | collective-permute-start | bytes 24584 | tf_op jit(solution)/shard_map/ppermute | solution.py:37
  2.8 5.4 %collective-permute-start.2 = (bf16[4,1024]{1,0:T(4,128)(2,1)}, bf16[4,1024]{1,0:T(4,128)(2,1)S(1)}, u32[]{:S(2)}, u32[]{:S(2)}) collective-permute-start(bf16[4,1024]{1,0:T(4,128)(2,1)} %refs_0_.3), channel_id=1, source_target_pairs={{0,12},{4,0},{8,4},{12,8},{1,13},{5,1},{9,5},{13,9},{2,14},{6,2},{... | collective-permute-start | bytes 24584 | tf_op jit(solution)/shard_map/ppermute | solution.py:37
  4.9 3.6 %collective-permute-start.1 = (bf16[4,1024]{1,0:T(4,128)(2,1)}, bf16[4,1024]{1,0:T(4,128)(2,1)S(1)}, u32[]{:S(2)}, u32[]{:S(2)}) collective-permute-start(bf16[4,1024]{1,0:T(4,128)(2,1)} %refs_0_.3), channel_id=1, source_target_pairs={{0,8},{4,12},{8,0},{12,4},{1,9},{5,13},{9,1},{13,5},{2,10},{6,14},... | collective-permute-start | bytes 24584 | tf_op jit(solution)/shard_map/ppermute | solution.py:37
  12.1 6.3 %collective-permute-start.5 = (bf16[144,128]{1,0:T(8,128)(2,1)S(1)}, bf16[144,128]{1,0:T(8,128)(2,1)S(1)}, u32[]{:S(2)}, u32[]{:S(2)}) collective-permute-start(bf16[144,128]{1,0:T(8,128)(2,1)S(1)} %get-tuple-element.27.refs_4_.refs_0_), channel_id=1, source_target_pairs={{0,12},{4,0},{8,4},{12,8},{1,13},{5,1},{9,5},{13,9},{2,14},{6,2},{... | collective-permute-start | bytes 110600 | tf_op jit(solution)/shard_map/ppermute | solution.py:37
  13.6 4.9 %collective-permute-start.4 = (bf16[144,128]{1,0:T(8,128)(2,1)S(1)}, bf16[144,128]{1,0:T(8,128)(2,1)S(1)}, u32[]{:S(2)}, u32[]{:S(2)}) collective-permute-start(bf16[144,128]{1,0:T(8,128)(2,1)S(1)} %get-tuple-element.27.refs_4_.refs_0_), channel_id=1, source_target_pairs={{0,8},{4,12},{8,0},{12,4},{1,9},{5,13},{9,1},{13,5},{2,10},{6,14},... | collective-permute-start | bytes 110600 | tf_op jit(solution)/shard_map/ppermute | solution.py:37
  14.4 4.6 %collective-permute-start.3 = (bf16[144,128]{1,0:T(8,128)(2,1)S(1)}, bf16[144,128]{1,0:T(8,128)(2,1)S(1)}, u32[]{:S(2)}, u32[]{:S(2)}) collective-permute-start(bf16[144,128]{1,0:T(8,128)(2,1)S(1)} %get-tuple-element.27.refs_4_.refs_0_), channel_id=1, source_target_pairs={{0,4},{4,8},{8,12},{12,0},{1,5},{5,9},{9,13},{13,1},{2,6},{6,10},{... | collective-permute-start | bytes 110600 | tf_op jit(solution)/shard_map/ppermute | solution.py:37
  15.4 17.4 %slice-start = ((s8[16777216]{0:T(1024)(128)(4,1)}), s8[4194304]{0:T(1024)(128)(4,1)S(1)}, s32[]{:S(2)}) async-start(s8[16777216]{0:T(1024)(128)(4,1)} %bitcast.7), calls=%async_computation | async-start | bytes 8388608
  15.4 17.4 %slice-start.4 = ((s8[16777216]{0:T(1024)(128)(4,1)}), s8[4194304]{0:T(1024)(128)(4,1)S(1)}, s32[]{:S(2)}) async-start(s8[16777216]{0:T(1024)(128)(4,1)} %bitcast.10), calls=%async_computation.4 | async-start | bytes 8388608
  19.0 13.7 %slice-start.3 = ((s8[16777216]{0:T(1024)(128)(4,1)}), s8[4194304]{0:T(1024)(128)(4,1)S(1)}, s32[]{:S(2)}) async-start(s8[16777216]{0:T(1024)(128)(4,1)} %bitcast.7), calls=%async_computation.3 | async-start | bytes 8388608
  19.0 13.7 %slice-start.5 = ((s8[16777216]{0:T(1024)(128)(4,1)}), s8[4194304]{0:T(1024)(128)(4,1)S(1)}, s32[]{:S(2)}) async-start(s8[16777216]{0:T(1024)(128)(4,1)} %bitcast.10), calls=%async_computation.5 | async-start | bytes 8388608
  19.0 13.7 %slice-start.6 = ((s8[16777216]{0:T(1024)(128)(4,1)}), s8[4194304]{0:T(1024)(128)(4,1)S(1)}, s32[]{:S(2)}) async-start(s8[16777216]{0:T(1024)(128)(4,1)} %bitcast.10), calls=%async_computation.6 | async-start | bytes 8388608
  19.0 13.7 %slice-start.7 = ((s8[16777216]{0:T(1024)(128)(4,1)}), s8[4194304]{0:T(1024)(128)(4,1)S(1)}, s32[]{:S(2)}) async-start(s8[16777216]{0:T(1024)(128)(4,1)} %bitcast.10), calls=%async_computation.7 | async-start | bytes 8388608
  19.8 6.2 %collective-permute-start.8 = (bf16[16,1024]{1,0:T(8,128)(2,1)S(1)}, bf16[16,1024]{1,0:T(8,128)(2,1)S(1)}, u32[]{:S(2)}, u32[]{:S(2)}) collective-permute-start(bf16[16,1024]{1,0:T(8,128)(2,1)S(1)} %project.1.refs_0_), channel_id=1, source_target_pairs={{0,3},{1,0},{2,1},{3,2},{4,7},{5,4},{6,5},{7,6},{8,11},{9,8},{10,9... | collective-permute-start | bytes 98312 | tf_op jit(solution)/shard_map/ppermute | solution.py:37
  23.1 3.4 %collective-permute-start.7 = (bf16[16,1024]{1,0:T(8,128)(2,1)S(1)}, bf16[16,1024]{1,0:T(8,128)(2,1)S(1)}, u32[]{:S(2)}, u32[]{:S(2)}) collective-permute-start(bf16[16,1024]{1,0:T(8,128)(2,1)S(1)} %project.1.refs_0_), channel_id=1, source_target_pairs={{0,2},{1,3},{2,0},{3,1},{4,6},{5,7},{6,4},{7,5},{8,10},{9,11},{10,... | collective-permute-start | bytes 98312 | tf_op jit(solution)/shard_map/ppermute | solution.py:37
  24.3 2.2 %collective-permute-start.6 = (bf16[16,1024]{1,0:T(8,128)(2,1)S(1)}, bf16[16,1024]{1,0:T(8,128)(2,1)S(1)}, u32[]{:S(2)}, u32[]{:S(2)}) collective-permute-start(bf16[16,1024]{1,0:T(8,128)(2,1)S(1)} %project.1.refs_0_), channel_id=1, source_target_pairs={{0,1},{1,2},{2,3},{3,0},{4,5},{5,6},{6,7},{7,4},{8,9},{9,10},{10,1... | collective-permute-start | bytes 98312 | tf_op jit(solution)/shard_map/ppermute | solution.py:37
  26.6 2.8 %collective-permute-start.11 = (bf16[16,1152]{1,0:T(8,128)(2,1)S(1)}, bf16[16,1152]{1,0:T(8,128)(2,1)S(1)}, u32[]{:S(2)}, u32[]{:S(2)}) collective-permute-start(bf16[16,1152]{1,0:T(8,128)(2,1)S(1)} %get-tuple-element.32.refs_0_), channel_id=1, source_target_pairs={{0,12},{4,0},{8,4},{12,8},{1,13},{5,1},{9,5},{13,9},{2,14},{6,2},{... | collective-permute-start | bytes 110600 | tf_op jit(solution)/shard_map/ppermute | solution.py:37
  27.5 4.4 %collective-permute-start.10 = (bf16[16,1152]{1,0:T(8,128)(2,1)S(1)}, bf16[16,1152]{1,0:T(8,128)(2,1)S(1)}, u32[]{:S(2)}, u32[]{:S(2)}) collective-permute-start(bf16[16,1152]{1,0:T(8,128)(2,1)S(1)} %get-tuple-element.32.refs_0_), channel_id=1, source_target_pairs={{0,8},{4,12},{8,0},{12,4},{1,9},{5,13},{9,1},{13,5},{2,10},{6,14},... | collective-permute-start | bytes 110600 | tf_op jit(solution)/shard_map/ppermute | solution.py:37
  28.1 4.6 %collective-permute-start.9 = (bf16[16,1152]{1,0:T(8,128)(2,1)S(1)}, bf16[16,1152]{1,0:T(8,128)(2,1)S(1)}, u32[]{:S(2)}, u32[]{:S(2)}) collective-permute-start(bf16[16,1152]{1,0:T(8,128)(2,1)S(1)} %get-tuple-element.32.refs_0_), channel_id=1, source_target_pairs={{0,4},{4,8},{8,12},{12,0},{1,5},{5,9},{9,13},{13,1},{2,6},{6,10},{... | collective-permute-start | bytes 110600 | tf_op jit(solution)/shard_map/ppermute | solution.py:37
  40.0 4.6 %collective-permute-start.12 = (bf16[16,1024]{1,0:T(8,128)(2,1)S(1)}, bf16[16,1024]{1,0:T(8,128)(2,1)S(1)}, u32[]{:S(2)}, u32[]{:S(2)}) collective-permute-start(bf16[16,1024]{1,0:T(8,128)(2,1)S(1)} %get-tuple-element.37), channel_id=1, source_target_pairs={{0,4},{4,8},{8,12},{12,0},{1,5},{5,9},{9,13},{13,1},{2,6},{6,10},{... | collective-permute-start | bytes 98312 | tf_op jit(solution)/shard_map/ppermute | solution.py:48
  40.1 4.6 %collective-permute-start.13 = (bf16[16,1024]{1,0:T(8,128)(2,1)S(1)}, bf16[16,1024]{1,0:T(8,128)(2,1)S(1)}, u32[]{:S(2)}, u32[]{:S(2)}) collective-permute-start(bf16[16,1024]{1,0:T(8,128)(2,1)S(1)} %get-tuple-element.38), channel_id=1, source_target_pairs={{0,8},{4,12},{8,0},{12,4},{1,9},{5,13},{9,1},{13,5},{2,10},{6,14},... | collective-permute-start | bytes 98312 | tf_op jit(solution)/shard_map/ppermute | solution.py:48
  41.3 3.7 %collective-permute-start.14 = (bf16[16,1024]{1,0:T(8,128)(2,1)S(1)}, bf16[16,1024]{1,0:T(8,128)(2,1)S(1)}, u32[]{:S(2)}, u32[]{:S(2)}) collective-permute-start(bf16[16,1024]{1,0:T(8,128)(2,1)S(1)} %get-tuple-element.39), channel_id=1, source_target_pairs={{0,12},{4,0},{8,4},{12,8},{1,13},{5,1},{9,5},{13,9},{2,14},{6,2},{... | collective-permute-start | bytes 98312 | tf_op jit(solution)/shard_map/ppermute | solution.py:48
  45.0 6.5 %collective-permute-start.15 = (bf16[4,1024]{1,0:T(4,128)(2,1)S(1)}, bf16[4,1024]{1,0:T(4,128)(2,1)S(1)}, u32[]{:S(2)}, u32[]{:S(2)}) collective-permute-start(bf16[4,1024]{1,0:T(4,128)(2,1)S(1)} %get-tuple-element.41), channel_id=1, source_target_pairs={{0,1},{1,2},{2,3},{3,0},{4,5},{5,6},{6,7},{7,4},{8,9},{9,10},{10,1... | collective-permute-start | bytes 24584 | tf_op jit(solution)/shard_map/ppermute | solution.py:48
  50.1 2.8 %collective-permute-start.16 = (bf16[4,1024]{1,0:T(4,128)(2,1)S(1)}, bf16[4,1024]{1,0:T(4,128)(2,1)S(1)}, u32[]{:S(2)}, u32[]{:S(2)}) collective-permute-start(bf16[4,1024]{1,0:T(4,128)(2,1)S(1)} %get-tuple-element.42), channel_id=1, source_target_pairs={{0,2},{1,3},{2,0},{3,1},{4,6},{5,7},{6,4},{7,5},{8,10},{9,11},{10,... | collective-permute-start | bytes 24584 | tf_op jit(solution)/shard_map/ppermute | solution.py:48
  51.0 3.1 %collective-permute-start.17 = (bf16[4,1024]{1,0:T(4,128)(2,1)S(1)}, bf16[4,1024]{1,0:T(4,128)(2,1)S(1)}, u32[]{:S(2)}, u32[]{:S(2)}) collective-permute-start(bf16[4,1024]{1,0:T(4,128)(2,1)S(1)} %get-tuple-element.43), channel_id=1, source_target_pairs={{0,3},{1,0},{2,1},{3,2},{4,7},{5,4},{6,5},{7,6},{8,11},{9,8},{10,9... | collective-permute-start | bytes 24584 | tf_op jit(solution)/shard_map/ppermute | solution.py:48
  (6 other events, 40.6 us)

commit v5 on v3

--- a/solution.py
+++ b/solution.py
@@ -18,7 +18,8 @@
 LANES = 128
 STATS = 16
 MOST_PERMUTES = 4
-GATE_PARTS = 4
+CHUNKS = 4
+TILE = 512
 
 BF = jnp.bfloat16
 F32 = jnp.float32
@@ -70,7 +71,7 @@
     sources, outs, sems = refs[:count], refs[count + waits : -1], refs[-1]
     copies = []
     for i, cut in enumerate(cuts):
-        view = sources[i] if cut is None else sources[i].at[cut]
+        view = sources[i] if cut is None else sources[i].at[cut() if callable(cut) else cut]
         copies.append(pltpu.make_async_copy(view, outs[i], sems.at[i]))
     for copy in copies:
         copy.start()
@@ -96,18 +97,52 @@
     return (array, None, array.shape)
 
 
-def rows_of(array, part, parts):
-    step = array.shape[0] // parts
-    return (array, (pl.ds(part * step, step), slice(None)), (step, array.shape[1]))
-
-
-def attend_kernel(count, own_rows, kv_heads, group, positions, *refs):
+def rows_at(part, count, step, relative):
+    if relative:
+        part = lax.rem(lax.axis_index("expert") - part + count, count)
+        return (pl.ds(pl.multiple_of(part * step, step), step), slice(None))
+    return (pl.ds(part * step, step), slice(None))
+
+
+def rows_of(array, part, count, relative):
+    step = array.shape[0] // count
+    cut = functools.partial(rows_at, part, count, step, relative)
+    return (array, cut, (step, array.shape[1]))
+
+
+def with_copy(copies, work):
+    for copy in copies:
+        copy.start()
+    pl.when(lax.axis_index("expert") >= 0)(work)
+    for copy in copies:
+        copy.wait()
+
+
+def attend_kernel(count, own_rows, kv_heads, group, positions, cut, *refs):
     taken = grouped(count)
     slot_ref, length_ref = refs[0], refs[1]
     query_refs = refs[2 : 2 + taken]
     new_ref = refs[2 + taken]
     cache_refs = refs[3 + taken : 3 + taken + kv_heads]
-    out_ref, q_rows, score, acc, fresh = refs[3 + taken + kv_heads :]
+    refs = refs[3 + taken + kv_heads :]
+    attend_body = functools.partial(
+        attend_block,
+        (count, own_rows, kv_heads, group, positions),
+        (slot_ref, length_ref, query_refs, new_ref, cache_refs),
+    )
+    if cut is None:
+        attend_body(*refs)
+        return
+    chunk_hbm, out_ref, chunk_ref, *scratch, chunk_sem = refs
+    with_copy(
+        [pltpu.make_async_copy(chunk_hbm.at[cut()], chunk_ref, chunk_sem)],
+        lambda: attend_body(out_ref, *scratch),
+    )
+
+
+def attend_block(sizes, inputs, out_ref, q_rows, score, acc, fresh):
+    count, own_rows, kv_heads, group, positions = sizes
+    slot_ref, length_ref, query_refs, new_ref, cache_refs = inputs
     me = lax.axis_index("expert")
     heads = kv_heads * group
     total = count * own_rows
@@ -197,28 +232,36 @@
         out_ref[rows + part * STATS : rows + (part + 1) * STATS, :] = turned[0:STATS, :].astype(BF)
 
 
-def attend(slot_of, lengths, queries, new_kv, caches, count):
+def attend(slot_of, lengths, queries, new_kv, caches, chunk, count):
     own_rows, _, kv_width = new_kv.shape
     kv_heads = kv_width // HD
     group = HEADS // KVH
     heads = kv_heads * group
     positions = caches[0].shape[1] // 2
     rows = count * own_rows * heads
-    return pl.pallas_call(
-        functools.partial(attend_kernel, count, own_rows, kv_heads, group, positions),
+    out_shape = [pltpu.VMEM((rows + STATS * (rows // LANES), LANES), BF)]
+    scratch_shapes = [
+        pltpu.VMEM((count, own_rows * heads, HD), F32),
+        pltpu.VMEM((rows, 2 * positions), F32),
+        pltpu.VMEM((rows, HD), F32),
+        pltpu.VMEM((2, own_rows * heads, HD), F32),
+    ]
+    cut, more = None, []
+    if chunk is not None:
+        array, cut, shape = chunk
+        more = [pltpu.with_memory_space_constraint(array, pltpu.HBM)]
+        out_shape.append(pltpu.VMEM(shape, BF))
+        scratch_shapes.append(pltpu.SemaphoreType.DMA)
+    return pl.pallas_call(
+        functools.partial(attend_kernel, count, own_rows, kv_heads, group, positions, cut),
         name="attend",
-        out_shape=jax.ShapeDtypeStruct((rows + STATS * (rows // LANES), LANES), BF),
-        in_specs=[SMEM, SMEM] + [VMEM] * (len(queries) + 1 + kv_heads),
-        out_specs=VMEM,
-        scratch_shapes=[
-            pltpu.VMEM((count, own_rows * heads, HD), F32),
-            pltpu.VMEM((rows, 2 * positions), F32),
-            pltpu.VMEM((rows, HD), F32),
-            pltpu.VMEM((2, own_rows * heads, HD), F32),
-        ],
+        out_shape=tuple(out_shape),
+        in_specs=[SMEM, SMEM] + [VMEM] * (len(queries) + 1 + kv_heads) + [HBM] * len(more),
+        out_specs=tuple([VMEM] * len(out_shape)),
+        scratch_shapes=scratch_shapes,
         compiler_params=pltpu.CompilerParams(vmem_limit_bytes=6 << 20),
         cost_estimate=pl.CostEstimate(flops=10**8, bytes_accessed=1000, transcendentals=0),
-    )(slot_of, lengths, *queries, new_kv, *caches)
+    )(slot_of, lengths, *queries, new_kv, *caches, *more)
 
 
 def project_kernel(count, rows, heads, *refs):
@@ -298,8 +341,8 @@
         functools.partial(residual_kernel, count),
         name="residual",
         out_shape=(
-            jax.ShapeDtypeStruct((rows, width), BF),
-            jax.ShapeDtypeStruct((rows, width + LANES), BF),
+            pltpu.VMEM((rows, width), BF),
+            pltpu.VMEM((rows, width + LANES), BF),
         ),
         in_specs=[VMEM] * (len(parts) + 2),
         out_specs=(VMEM, VMEM),
@@ -309,27 +352,56 @@
     )(*parts, resid, gain)
 
 
-def experts_kernel(count, sharing, gates, *refs):
-    taken = grouped(count)
-    part_refs, refs = refs[:taken], refs[taken:]
-    ids_ref, logits_ref, refs = refs[0], refs[1], refs[2:]
-    up_ref, down_ref, refs = *refs[:2], refs[2:]
-    gate_refs, refs = refs[:gates], refs[gates:]
-    out_refs, refs = refs[:taken], refs[taken:]
-    spread, act = refs
-    me = lax.axis_index("expert")
-    depth = up_ref.shape[0]
-    rows = spread.shape[0]
-    width = depth // count
-    squares = jnp.zeros((rows, 1), F32)
-    for shift in range(count):
-        block = piece(part_refs, count, shift)
-        at = source(part_refs, count, me, shift)
-        spread[:, pl.ds(pl.multiple_of(at * width, width), width)] = block[:, 0:width]
-        tail = block[:, width:].astype(F32)
-        squares = squares + (tail[:, 0:1] + tail[:, 1:2] + tail[:, 2:3])
-    inverse = lax.rsqrt(squares / depth + EPSILON)
-    mine = me // sharing
+def tiles(width):
+    step = math.gcd(width, TILE)
+    return [slice(i, i + step) for i in range(0, width, step)]
+
+
+def product_kernel(shift, count, cut, *refs):
+    block_ref, gate_ref, up_ref, refs = *refs[:3], refs[3:]
+    sums, refs = (refs[:2], refs[2:]) if shift else ((), refs)
+    step = gate_ref.shape[0]
+    at, _ = rows_at(shift, count, step, True)
+
+    def work(gate_out, up_out):
+        block = block_ref[:, 0:step]
+        for columns in tiles(gate_ref.shape[1]):
+            gate_made = jnp.dot(block, gate_ref[:, columns], preferred_element_type=F32)
+            up_made = jnp.dot(block, up_ref[at, columns], preferred_element_type=F32)
+            gate_out[:, columns] = gate_made + sums[0][:, columns] if sums else gate_made
+            up_out[:, columns] = up_made + sums[1][:, columns] if sums else up_made
+
+    if cut is None:
+        work(*refs)
+        return
+    chunk_hbm, gate_out, up_out, chunk_ref, sem = refs
+    with_copy(
+        [pltpu.make_async_copy(chunk_hbm.at[cut()], chunk_ref, sem)],
+        lambda: work(gate_out, up_out),
+    )
+
+
+def product(shift, count, block, gate, up, sums, chunk=None):
+    one = pltpu.VMEM((block.shape[0], gate.shape[1]), F32)
+    out_shape, scratch_shapes, cut, more = [one, one], [], None, []
+    if chunk is not None:
+        array, cut, shape = chunk
+        more = [pltpu.with_memory_space_constraint(array, pltpu.HBM)]
+        out_shape.append(pltpu.VMEM(shape, BF))
+        scratch_shapes.append(pltpu.SemaphoreType.DMA)
+    return pl.pallas_call(
+        functools.partial(product_kernel, shift, count, cut),
+        name="product",
+        out_shape=tuple(out_shape),
+        in_specs=[VMEM] * (3 + len(sums)) + [HBM] * len(more),
+        out_specs=tuple([VMEM] * len(out_shape)),
+        scratch_shapes=scratch_shapes,
+        compiler_params=pltpu.CompilerParams(vmem_limit_bytes=6 << 20),
+        cost_estimate=pl.CostEstimate(flops=10**8, bytes_accessed=1000, transcendentals=0),
+    )(block, gate, up, *sums, *more)
+
+
+def routing(ids_ref, logits_ref, mine, rows):
     logits = logits_ref[...]
     first = 1.0 / (1.0 + jnp.exp(logits[1:2, :] - logits[0:1, :]))
     ids = ids_ref[...]
@@ -339,47 +411,128 @@
     eye = lax.broadcasted_iota(jnp.int32, (rows, rows), 0) == lax.broadcasted_iota(
         jnp.int32, (rows, rows), 1
     )
-    mix = jnp.sum(jnp.where(eye, mix_row, 0.0), axis=1, keepdims=True)
-    step = depth // gates
-    gate_sum = sum(
-        jnp.dot(spread[:, i * step : (i + 1) * step], ref[...], preferred_element_type=F32)
-        for i, ref in enumerate(gate_refs)
-    )
+    return jnp.sum(jnp.where(eye, mix_row, 0.0), axis=1, keepdims=True)
+
+
+def inverse_rms(blocks, width, depth):
+    squares = 0.0
+    for block in blocks:
+        tail = block[:, width:].astype(F32)
+        squares = squares + (tail[:, 0:1] + tail[:, 1:2] + tail[:, 2:3])
+    return lax.rsqrt(squares / depth + EPSILON)
+
+
+def activate(gate_sum, up_sum, inverse):
+    gate_sum = gate_sum * inverse
+    return (gate_sum / (1.0 + jnp.exp(-gate_sum)) * (up_sum * inverse)).astype(BF)
+
+
+def experts_kernel(count, sharing, last, cut, *refs):
+    part_refs, refs = refs[:count], refs[count:]
+    ids_ref, logits_ref, gate_ref, up_ref, gate_sum_ref, up_sum_ref, refs = *refs[:6], refs[6:]
+    down_refs, down_hbm, refs = refs[: count - 1], refs[count - 1], refs[count:]
+    out_refs, refs = refs[:count], refs[count:]
+    act, made, mix_ref, last_down, sem = refs
+    me = lax.axis_index("expert")
+    rows, hidden_units = act.shape
+    width = gate_ref.shape[0]
+    step = last_down.shape[0]
+
+    def work():
+        mix_ref[...] = jnp.broadcast_to(
+            routing(ids_ref, logits_ref, me // sharing, rows), mix_ref.shape
+        )
+        inverse = inverse_rms([ref[...] for ref in part_refs], width, count * width)
+        block = part_refs[last][:, 0:width]
+        at, _ = rows_at(last, count, width, True)
+        for columns in tiles(hidden_units):
+            gate_sum = gate_sum_ref[:, columns] + jnp.dot(
+                block, gate_ref[:, columns], preferred_element_type=F32
+            )
+            up_sum = up_sum_ref[:, columns] + jnp.dot(
+                block, up_ref[at, columns], preferred_element_type=F32
+            )
+            act[:, columns] = activate(gate_sum, up_sum, inverse)
+        for columns in tiles(count * width):
+            made[:, columns] = sum(
+                jnp.dot(
+                    act[:, c * step : (c + 1) * step], ref[:, columns], preferred_element_type=F32
+                )
+                for c, ref in enumerate(down_refs)
+            )
+
+    with_copy([pltpu.make_async_copy(down_hbm.at[cut()], last_down, sem)], work)
+    mix = mix_ref[:, 0:1]
+    for shift in range(count):
+        at = target(False, count, me, shift)
+        columns = pl.ds(pl.multiple_of(at * width, width), width)
+        total = made[:, columns] + jnp.dot(
+            act[:, hidden_units - step :], last_down[:, columns], preferred_element_type=F32
+        )
+        out_refs[shift][...] = (total * mix).astype(BF)
+
+
+def experts(last, parts, ids, logits, gate, up, sums, downs, down_last, count):
+    rows, hidden_units = sums[0].shape
+    width = gate.shape[0]
+    array, cut, shape = down_last
+    return pl.pallas_call(
+        functools.partial(experts_kernel, count, count // EXPERTS, last, cut),
+        name="experts",
+        out_shape=tuple([pltpu.VMEM((rows, width), BF)] * count),
+        in_specs=[VMEM] * (len(parts) + 6 + len(downs)) + [HBM],
+        out_specs=tuple([VMEM] * count),
+        scratch_shapes=[
+            pltpu.VMEM((rows, hidden_units), BF),
+            pltpu.VMEM((rows, count * width), F32),
+            pltpu.VMEM((rows, LANES), F32),
+            pltpu.VMEM(shape, BF),
+            pltpu.SemaphoreType.DMA,
+        ],
+        compiler_params=pltpu.CompilerParams(vmem_limit_bytes=7 << 20),
+        cost_estimate=pl.CostEstimate(flops=10**8, bytes_accessed=1000, transcendentals=0),
+    )(
+        *parts,
+        ids,
+        logits,
+        gate,
+        up,
+        *sums,
+        *downs,
+        pltpu.with_memory_space_constraint(array, pltpu.HBM),
+    )
+
+
+def all_experts_kernel(count, sharing, *refs):
+    parts_ref, ids_ref, logits_ref, gate_ref, up_ref, down_ref, out_ref, spread = refs
+    depth = gate_ref.shape[0]
+    rows = spread.shape[0]
+    width = depth // count
+    for i in range(count):
+        spread[:, i * width : (i + 1) * width] = parts_ref[i, :, 0:width]
+    inverse = inverse_rms([parts_ref[i] for i in range(count)], width, depth)
+    mix = routing(ids_ref, logits_ref, lax.axis_index("expert") // sharing, rows)
+    gate_sum = jnp.dot(spread[...], gate_ref[...], preferred_element_type=F32)
     up_sum = jnp.dot(spread[...], up_ref[...], preferred_element_type=F32)
-    gate_sum = gate_sum * inverse
-    act[...] = (gate_sum / (1.0 + jnp.exp(-gate_sum)) * (up_sum * inverse)).astype(BF)
-    stacked = taken == 1
-    for shift in range(count):
-        at = target(stacked, count, me, shift)
-        columns = pl.ds(pl.multiple_of(at * width, width), width)
-        made = jnp.dot(act[...], down_ref[:, columns], preferred_element_type=F32)
-        made = (made * mix).astype(BF)
-        if stacked:
-            out_refs[0][shift] = made
-        else:
-            out_refs[shift][...] = made
-
-
-def experts(parts, ids, logits, gates, up, down, count):
-    hidden_units, depth = down.shape
-    rows = ids.shape[1]
-    width = depth // count
-    stacked = len(parts) != count
-    one = pltpu.VMEM((rows, width), BF)
-    out_shape = (pltpu.VMEM((count, rows, width), BF),) if stacked else tuple([one] * count)
-    return pl.pallas_call(
-        functools.partial(experts_kernel, count, count // EXPERTS, len(gates)),
+    act = activate(gate_sum, up_sum, inverse)
+    for i in range(count):
+        made = jnp.dot(
+            act, down_ref[:, i * width : (i + 1) * width], preferred_element_type=F32
+        )
+        out_ref[i] = (made * mix).astype(BF)
+
+
+def all_experts(parts, ids, logits, gate, up, down, count):
+    rows, depth = ids.shape[1], gate.shape[0]
+    return pl.pallas_call(
+        functools.partial(all_experts_kernel, count, count // EXPERTS),
         name="experts",
-        out_shape=out_shape,
-        in_specs=[VMEM] * (len(parts) + 4 + len(gates)),
-        out_specs=tuple([VMEM] * len(out_shape)),
-        scratch_shapes=[
-            pltpu.VMEM((rows, depth), BF),
-            pltpu.VMEM((rows, hidden_units), BF),
-        ],
-        compiler_params=pltpu.CompilerParams(vmem_limit_bytes=(16 if stacked else 4) << 20),
-        cost_estimate=pl.CostEstimate(flops=10**8, bytes_accessed=1000, transcendentals=0),
-    )(*parts, ids, logits, up, down, *gates)
+        out_shape=(jax.ShapeDtypeStruct((count, rows, depth // count), BF),),
+        in_specs=[VMEM] * 6,
+        out_specs=(VMEM,),
+        scratch_shapes=[pltpu.VMEM((rows, depth), BF)],
+        compiler_params=pltpu.CompilerParams(vmem_limit_bytes=24 << 20),
+    )(parts[0], ids, logits, gate, up, down)
 
 
 def first_sum_kernel(count, other, *refs):
@@ -452,35 +605,60 @@
     slots, positions, _, kv_width = kv_prefill.shape
     kv_heads = kv_width // HD
     queries = gather(query, "expert")
+    split = len(queries) == expert_count == CHUNKS
+    gate, up, down = gate_weight_slabs[0], w_up[0], w_down[0]
+    gate_rows = [[rows_of(gate, i, CHUNKS, True)] if split else [] for i in range(CHUNKS)]
+    down_rows = [[rows_of(down, i, CHUNKS, False)] if split else [] for i in range(CHUNKS)]
     head_shape = (slots, positions, 2, HD)
     heads = [
         (kv_prefill, (slice(None), slice(None), slice(None), pl.ds(g * HD, HD)), head_shape)
         for g in range(kv_heads)
     ]
-    gate = gate_weight_slabs[0]
-    loaded = load([whole(query), whole(new_kv), *heads, rows_of(gate, 0, GATE_PARTS), rows_of(gate, 1, GATE_PARTS)])
-    if len(queries) == expert_count:
-        queries[0] = loaded[0]
-    fresh, caches = loaded[1], loaded[2 : 2 + kv_heads]
-    gate_0 = loaded[2 + kv_heads]
-    gate_1 = loaded[3 + kv_heads]
+    own, fresh, *loaded = load(
+        [whole(query), whole(new_kv), *heads, *gate_rows[0], *gate_rows[3]]
+    )
+    caches, first_gates = loaded[:kv_heads], loaded[kv_heads:]
+    if split:
+        queries[0] = own
     caches = [cache.reshape(slots, 2 * positions, HD) for cache in caches]
-    part = attend(slot_of, lengths, queries, fresh, caches, expert_count)
+    part, *second_gates = attend(
+        slot_of,
+        lengths,
+        queries,
+        fresh,
+        caches,
+        gate_rows[2][0] if split else None,
+        expert_count,
+    )
     parts = gather(part, "expert")
-    wo_here, resid_here, gain_here, gate_2, gate_3 = load([whole(wo), whole(resid), whole(norm_gain), rows_of(gate, 2, GATE_PARTS), rows_of(gate, 3, GATE_PARTS)], [part])
+    wo_here, resid_here, gain_here, *third = load(
+        [whole(wo), whole(resid), whole(norm_gain), *gate_rows[1], *down_rows[0]], [part]
+    )
     projected = project(parts, wo_here, expert_count, total)
     partials = gather(projected, "tensor")
     attention, scaled = residual(partials, resid_here, gain_here, tensor_count)
     blocks = gather(scaled, "expert")
-    outgoing = experts(
-        blocks,
-        expert_ids.T,
-        gate_logits.T,
-        (gate_0, gate_1, gate_2, gate_3),
-        w_up[0],
-        w_down[0],
-        expert_count,
-    )
+    if split:
+        g_0, g_3, g_2, g_1, d_0 = *first_gates, *second_gates, *third
+        *sums, d_1 = product(0, CHUNKS, blocks[0], g_0, up, (), down_rows[1][0])
+        *sums, d_2 = product(3, CHUNKS, blocks[3], g_3, up, sums, down_rows[2][0])
+        sums = product(2, CHUNKS, blocks[2], g_2, up, sums)
+        outgoing = experts(
+            1,
+            blocks,
+            expert_ids.T,
+            gate_logits.T,
+            g_1,
+            up,
+            sums,
+            (d_0, d_1, d_2),
+            down_rows[3][0],
+            CHUNKS,
+        )
+    else:
+        outgoing = all_experts(
+            blocks, expert_ids.T, gate_logits.T, gate, up, down, expert_count
+        )
     column_parts = first_sum(
         exchange(outgoing, "expert"), expert_count, tensor_count, total, width
     )

time: 54.3 us -> 53.7 us (0.989)
  waiting for transfers between devices: 10.8 us -> 7.49 us
  Pallas kernels: 18.7 us -> 21.8 us
  starting transfers between devices: 23.6 us -> 22.7 us
  local copies, waits for them, and re-layouts: 0.06 us -> 0.66 us
    pallas_call x0 -> x3, Pallas kernels: none -> 5.61 us  [product(): pl.pallas_call(functools.partial(product_kernel, shift, count, cut), name...]
    pallas_call x1, Pallas kernels: 6.62 us -> 3.55 us  [experts(): pl.pallas_call(functools.partial(experts_kernel, count, count // EXPERTS,...]
    ppermute x12, waiting for transfers between devices: 6.1 us -> 3.2 us  [gather(): lax.ppermute(value, axis, [(i, (i + shift) % count) for i in range(count)])]
    ppermute x6, starting transfers between devices: 8.91 us -> 7.06 us  [exchange(): lax.ppermute(values[shift], axis, [(i, (i + shift) % count) for i in rang...]
    pallas_call x1, Pallas kernels: 1.71 us -> 2.76 us  [attend(): pl.pallas_call(functools.partial(attend_kernel, count, own_rows, kv_heads...]
    ppermute x12, starting transfers between devices: 14.7 us -> 15.7 us  [gather(): lax.ppermute(value, axis, [(i, (i + shift) % count) for i in range(count)])]
    unnamed x24 -> x17, local copies, waits for them, and re-layouts: 0.06 us -> 0.66 us
  transfers between devices with their start and end apart: 18 -> 18, of which waited for: 9 -> 7; matrix products, arithmetic and copies ran while one was open for 0% -> 1% of each run, Pallas kernels for 15% -> 26%
where the time goes in v5:
time: 53.7 us; the launch traced here: 53.5 us
  starting transfers between devices  22.7 us (42%)
  Pallas kernels  21.8 us (41%)
  waiting for transfers between devices  7.49 us (14%)
  between operations  0.86 us (2%)
  local copies, waits for them, and re-layouts  0.66 us (1%)
    ppermute x12, starting transfers between devices, gather(): lax.ppermute(value, axis, [(i, (i + shift) % count) for i in range(count)])  15.7 us
    pallas_call x2, Pallas kernels, load(): pl.pallas_call(functools.partial(load_kernel, [cut for _, cut, _ in items...  8.26 us
    ppermute x6, starting transfers between devices, exchange(): lax.ppermute(values[shift], axis, [(i, (i + shift) % count) for i in rang...  7.06 us
    pallas_call x3, Pallas kernels, product(): pl.pallas_call(functools.partial(product_kernel, shift, count, cut), name...  5.61 us
    ppermute x6, waiting for transfers between devices, exchange(): lax.ppermute(values[shift], axis, [(i, (i + shift) % count) for i in rang...  4.29 us
    pallas_call x1, Pallas kernels, experts(): pl.pallas_call(functools.partial(experts_kernel, count, count // EXPERTS,...  3.55 us
    ppermute x12, waiting for transfers between devices, gather(): lax.ppermute(value, axis, [(i, (i + shift) % count) for i in range(count)])  3.2 us
    pallas_call x1, Pallas kernels, attend(): pl.pallas_call(functools.partial(attend_kernel, count, own_rows, kv_heads...  2.76 us
  transfers between devices with their start and end apart: 18, of which 7 were waited for; matrix products, arithmetic and copies ran while one was open for 1% of the time, Pallas kernels for 26%

profile of v5, /device:TPU:1, one launch (start us, length us, event | category | flops | bytes accessed | tf_op | source)
XLA Modules:
  0.0 53.5 jit_solution(5149040430699275917)
XLA Ops:
  0.6 2.2 %collective-permute-start = (bf16[4,1024]{1,0:T(4,128)(2,1)}, bf16[4,1024]{1,0:T(4,128)(2,1)S(1)}, u32[]{:S(2)}, u32[]{:S(2)}) collective-permute-start(bf16[4,1024]{1,0:T(4,128)(2,1)} %refs_0_.3), channel_id=1, source_target_pairs={{0,4},{4,8},{8,12},{12,0},{1,5},{5,9},{9,13},{13,1},{2,6},{6,10},{... | collective-permute-start | bytes 24584 | tf_op jit(solution)/shard_map/ppermute | solution.py:37
  2.8 2.3 %collective-permute-start.1 = (bf16[4,1024]{1,0:T(4,128)(2,1)}, bf16[4,1024]{1,0:T(4,128)(2,1)S(1)}, u32[]{:S(2)}, u32[]{:S(2)}) collective-permute-start(bf16[4,1024]{1,0:T(4,128)(2,1)} %refs_0_.3), channel_id=1, source_target_pairs={{0,8},{4,12},{8,0},{12,4},{1,9},{5,13},{9,1},{13,5},{2,10},{6,14},... | collective-permute-start | bytes 24584 | tf_op jit(solution)/shard_map/ppermute | solution.py:37
  5.1 1.1 %collective-permute-start.2 = (bf16[4,1024]{1,0:T(4,128)(2,1)}, bf16[4,1024]{1,0:T(4,128)(2,1)S(1)}, u32[]{:S(2)}, u32[]{:S(2)}) collective-permute-start(bf16[4,1024]{1,0:T(4,128)(2,1)} %refs_0_.3), channel_id=1, source_target_pairs={{0,12},{4,0},{8,4},{12,8},{1,13},{5,1},{9,5},{13,9},{2,14},{6,2},{... | collective-permute-start | bytes 24584 | tf_op jit(solution)/shard_map/ppermute | solution.py:37
  6.2 4.1 %load.2 = (bf16[4,1024]{1,0:T(4,128)(2,1)S(1)}, bf16[4,2,256]{2,1,0:T(2,128)(2,1)S(1)}, bf16[16,128,2,128]{3,2,1,0:T(2,128)(2,1)S(1)}, bf16[16,128,2,128]{3,2,1,...) custom-call(bf16[4,1024]{1,0:T(4,128)(2,1)} %refs_0_.3, bf16[4,2,256]{2,1,0:T(2,128)(2,1)} %refs_1_.3, ...), custom_call_target="tpu_custom_call" | custom-call | flops 100000000 | bytes 1000 | tf_op jit(solution)/shard_map/load/pallas_call | solution.py:84
  10.4 2.8 %attend.1 = (bf16[144,128]{1,0:T(8,128)(2,1)S(1)}, bf16[1024,2048]{1,0:T(8,128)(2,1)S(1)}) custom-call(s32[16]{0:T(128)S(1)} %copy-done.2, s32[16]{0:T(128)S(1)} %copy-done.3, bf16[4,1024]{1,0:T(4,128)(2,1)S(1)} %get-tuple-element.33.refs_2_, bf16[4,1024]{1,0:T(4,128)(2,1)S(1)} %collective-permute-done.refs_3_, ...), custom_call_target="tpu_custom_call" | custom-call | flops 100000000 | bytes 1000 | tf_op jit(solution)/shard_map/attend/pallas_call | solution.py:255
  13.8 2.7 %collective-permute-start.5 = (bf16[144,128]{1,0:T(8,128)(2,1)S(1)}, bf16[144,128]{1,0:T(8,128)(2,1)S(1)}, u32[]{:S(2)}, u32[]{:S(2)}) collective-permute-start(bf16[144,128]{1,0:T(8,128)(2,1)S(1)} %get-tuple-element.37.refs_5_.refs_0_), channel_id=1, source_target_pairs={{0,12},{4,0},{8,4},{12,8},{1,13},{5,1},{9,5},{13,9},{2,14},{6,2},{... | collective-permute-start | bytes 110600 | tf_op jit(solution)/shard_map/ppermute | solution.py:37
  16.5 4.1 %load.3 = (bf16[1024,1024]{1,0:T(8,128)(2,1)S(1)}, bf16[16,1024]{1,0:T(8,128)(2,1)S(1)}, bf16[1024]{0:T(1024)(128)(2,1)S(1)}, bf16[1024,2048]{1,0:T(8,128)(2,1)S(1)}, bf16[512,4096]{1,0:T(8,128)(2,1)S(1)}) custom-call(bf16[1024,1024]{1,0:T(8,128)(2,1)} %refs_0_.5, bf16[16,1024]{1,0:T(8,128)(2,1)} %refs_1_.5, bf16[1024]{0:T(1024)(128)(2,1)} %refs_2_.3, ...), custom_call_target="tpu_custom_call" | custom-call | flops 100000000 | bytes 1000 | tf_op jit(solution)/shard_map/load/pallas_call | solution.py:84
  20.7 0.8 %project.1.refs_0_ = bf16[16,1024]{1,0:T(8,128)(2,1)S(1)} custom-call(bf16[144,128]{1,0:T(8,128)(2,1)S(1)} %get-tuple-element.37.refs_5_.refs_0_, bf16[144,128]{1,0:T(8,128)(2,1)S(1)} %collective-permute-done.3.refs_1_, bf16[144,128]{1,0:T(8,128)(2,1)S(1)} %collective-permute-done.4.refs_2_, bf16[144,128]{1,0:T(8,128)(2,1)S(1)} %collective-permute-done.5.refs_3_, ...), custom_call_target="tpu_custom_call" | custom-call | flops 99999997952 | bytes 1000 | tf_op jit(solution)/shard_map/project/pallas_call | solution.py:300
  21.4 3.2 %collective-permute-start.6 = (bf16[16,1024]{1,0:T(8,128)(2,1)S(1)}, bf16[16,1024]{1,0:T(8,128)(2,1)S(1)}, u32[]{:S(2)}, u32[]{:S(2)}) collective-permute-start(bf16[16,1024]{1,0:T(8,128)(2,1)S(1)} %project.1.refs_0_), channel_id=1, source_target_pairs={{0,1},{1,2},{2,3},{3,0},{4,5},{5,6},{6,7},{7,4},{8,9},{9,10},{10,1... | collective-permute-start | bytes 98312 | tf_op jit(solution)/shard_map/ppermute | solution.py:37
  25.7 1.7 %collective-permute-done.7.refs_2_ = bf16[16,1024]{1,0:T(8,128)(2,1)S(1)} collective-permute-done((bf16[16,1024]{1,0:T(8,128)(2,1)S(1)}, bf16[16,1024]{1,0:T(8,128)(2,1)S(1)}, u32[]{:S(2)}, u32[]{:S(2)}) %collective-permute-start.7) | collective-permute-done | bytes 32800 | tf_op jit(solution)/shard_map/ppermute | solution.py:37
  27.4 0.8 %collective-permute-done.8.refs_3_ = bf16[16,1024]{1,0:T(8,128)(2,1)S(1)} collective-permute-done((bf16[16,1024]{1,0:T(8,128)(2,1)S(1)}, bf16[16,1024]{1,0:T(8,128)(2,1)S(1)}, u32[]{:S(2)}, u32[]{:S(2)}) %collective-permute-start.8) | collective-permute-done | bytes 32800 | tf_op jit(solution)/shard_map/ppermute | solution.py:37
  28.4 1.3 %collective-permute-start.11 = (bf16[16,1152]{1,0:T(8,128)(2,1)S(1)}, bf16[16,1152]{1,0:T(8,128)(2,1)S(1)}, u32[]{:S(2)}, u32[]{:S(2)}) collective-permute-start(bf16[16,1152]{1,0:T(8,128)(2,1)S(1)} %get-tuple-element.42.refs_0_), channel_id=1, source_target_pairs={{0,12},{4,0},{8,4},{12,8},{1,13},{5,1},{9,5},{13,9},{2,14},{6,2},{... | collective-permute-start | bytes 110600 | tf_op jit(solution)/shard_map/ppermute | solution.py:37
  30.2 1.4 %collective-permute-start.9 = (bf16[16,1152]{1,0:T(8,128)(2,1)S(1)}, bf16[16,1152]{1,0:T(8,128)(2,1)S(1)}, u32[]{:S(2)}, u32[]{:S(2)}) collective-permute-start(bf16[16,1152]{1,0:T(8,128)(2,1)S(1)} %get-tuple-element.42.refs_0_), channel_id=1, source_target_pairs={{0,4},{4,8},{8,12},{12,0},{1,5},{5,9},{9,13},{13,1},{2,6},{6,10},{... | collective-permute-start | bytes 110600 | tf_op jit(solution)/shard_map/ppermute | solution.py:37
  31.6 2.2 %product.3 = (f32[16,2048]{1,0:T(8,128)S(1)}, f32[16,2048]{1,0:T(8,128)S(1)}, bf16[512,4096]{1,0:T(8,128)(2,1)S(1)}) custom-call(bf16[16,1152]{1,0:T(8,128)(2,1)S(1)} %get-tuple-element.42.refs_0_, bf16[1024,2048]{1,0:T(8,128)(2,1)S(1)} %get-tuple-element.46.refs_1_, bf16[4096,2048]{1,0:T(8,128)(2,1)S(1)} %bitcast.9, bf16[2048,4096]{1,0:T(8,128)(2,1)} %bitcast.18), custom_call_target="tpu_custom_call" | custom-call | flops 100000000 | bytes 1000 | tf_op jit(solution)/shard_map/product/pallas_call | solution.py:392
  33.8 2.2 %product.4 = (f32[16,2048]{1,0:T(8,128)S(1)}, f32[16,2048]{1,0:T(8,128)S(1)}, bf16[512,4096]{1,0:T(8,128)(2,1)S(1)}) custom-call(bf16[16,1152]{1,0:T(8,128)(2,1)S(1)} %collective-permute-done.11.refs_0_.refs_3_, bf16[1024,2048]{1,0:T(8,128)(2,1)S(1)} %get-tuple-element.45.refs_1_, bf16[4096,2048]{1,0:T(8,128)(2,1)S(1)} %bitcast.10, ...), custom_call_target="tpu_custom_call" | custom-call | flops 100000000 | bytes 1000 | tf_op jit(solution)/shard_map/product/pallas_call | solution.py:392
  36.1 1.2 %product.5 = (f32[16,2048]{1,0:T(8,128)S(1)}, f32[16,2048]{1,0:T(8,128)S(1)}) custom-call(bf16[16,1152]{1,0:T(8,128)(2,1)S(1)} %collective-permute-done.10.refs_0_.refs_2_, bf16[1024,2048]{1,0:T(8,128)(2,1)S(1)} %get-tuple-element.44.refs_1_, bf16[4096,2048]{1,0:T(8,128)(2,1)S(1)} %bitcast.11, f32[16,2048]{1,0:T(8,128)S(1)} %get-tuple-element.49.refs_3_, ...), custom_call_target="tpu_custom_call" | custom-call | flops 100000000 | bytes 1000 | tf_op jit(solution)/shard_map/product/pallas_call | solution.py:392
  37.3 3.5 %experts.1 = (bf16[16,1024]{1,0:T(8,128)(2,1)S(1)}, bf16[16,1024]{1,0:T(8,128)(2,1)S(1)}, bf16[16,1024]{1,0:T(8,128)(2,1)S(1)}, bf16[16,1024]{1,0:T(8,128)(2,1)S(1)}) custom-call(bf16[16,1152]{1,0:T(8,128)(2,1)S(1)} %get-tuple-element.42.refs_0_, bf16[16,1152]{1,0:T(8,128)(2,1)S(1)} %collective-permute-done.9.refs_1_, ...), custom_call_target="tpu_custom_call" | custom-call | flops 100000000 | bytes 1000 | tf_op jit(solution)/shard_map/experts/pallas_call | solution.py:479
  40.8 0.8 %collective-permute-start.12 = (bf16[16,1024]{1,0:T(8,128)(2,1)S(1)}, bf16[16,1024]{1,0:T(8,128)(2,1)S(1)}, u32[]{:S(2)}, u32[]{:S(2)}) collective-permute-start(bf16[16,1024]{1,0:T(8,128)(2,1)S(1)} %get-tuple-element.57), channel_id=1, source_target_pairs={{0,4},{4,8},{8,12},{12,0},{1,5},{5,9},{9,13},{13,1},{2,6},{6,10},{... | collective-permute-start | bytes 98312 | tf_op jit(solution)/shard_map/ppermute | solution.py:48
  41.6 1.4 %collective-permute-start.13 = (bf16[16,1024]{1,0:T(8,128)(2,1)S(1)}, bf16[16,1024]{1,0:T(8,128)(2,1)S(1)}, u32[]{:S(2)}, u32[]{:S(2)}) collective-permute-start(bf16[16,1024]{1,0:T(8,128)(2,1)S(1)} %get-tuple-element.58), channel_id=1, source_target_pairs={{0,8},{4,12},{8,0},{12,4},{1,9},{5,13},{9,1},{13,5},{2,10},{6,14},... | collective-permute-start | bytes 98312 | tf_op jit(solution)/shard_map/ppermute | solution.py:48
  43.0 1.1 %collective-permute-start.14 = (bf16[16,1024]{1,0:T(8,128)(2,1)S(1)}, bf16[16,1024]{1,0:T(8,128)(2,1)S(1)}, u32[]{:S(2)}, u32[]{:S(2)}) collective-permute-start(bf16[16,1024]{1,0:T(8,128)(2,1)S(1)} %get-tuple-element.59), channel_id=1, source_target_pairs={{0,12},{4,0},{8,4},{12,8},{1,13},{5,1},{9,5},{13,9},{2,14},{6,2},{... | collective-permute-start | bytes 98312 | tf_op jit(solution)/shard_map/ppermute | solution.py:48
  44.2 1.4 %collective-permute-done.12.refs_1_ = bf16[16,1024]{1,0:T(8,128)(2,1)S(1)} collective-permute-done((bf16[16,1024]{1,0:T(8,128)(2,1)S(1)}, bf16[16,1024]{1,0:T(8,128)(2,1)S(1)}, u32[]{:S(2)}, u32[]{:S(2)}) %collective-permute-start.12) | collective-permute-done | bytes 32800 | tf_op jit(solution)/shard_map/ppermute | solution.py:48
  46.1 3.2 %collective-permute-start.15 = (bf16[4,1024]{1,0:T(4,128)(2,1)S(1)}, bf16[4,1024]{1,0:T(4,128)(2,1)S(1)}, u32[]{:S(2)}, u32[]{:S(2)}) collective-permute-start(bf16[4,1024]{1,0:T(4,128)(2,1)S(1)} %get-tuple-element.61), channel_id=1, source_target_pairs={{0,1},{1,2},{2,3},{3,0},{4,5},{5,6},{6,7},{7,4},{8,9},{9,10},{10,1... | collective-permute-start | bytes 24584 | tf_op jit(solution)/shard_map/ppermute | solution.py:48
  50.4 1.4 %collective-permute-done.16.refs_2_ = bf16[4,1024]{1,0:T(4,128)(2,1)S(1)} collective-permute-done((bf16[4,1024]{1,0:T(4,128)(2,1)S(1)}, bf16[4,1024]{1,0:T(4,128)(2,1)S(1)}, u32[]{:S(2)}, u32[]{:S(2)}) %collective-permute-start.16) | collective-permute-done | bytes 8224 | tf_op jit(solution)/shard_map/ppermute | solution.py:48
  51.8 1.1 %collective-permute-done.17.refs_3_ = bf16[4,1024]{1,0:T(4,128)(2,1)S(1)} collective-permute-done((bf16[4,1024]{1,0:T(4,128)(2,1)S(1)}, bf16[4,1024]{1,0:T(4,128)(2,1)S(1)}, u32[]{:S(2)}, u32[]{:S(2)}) %collective-permute-start.17) | collective-permute-done | bytes 8224 | tf_op jit(solution)/shard_map/ppermute | solution.py:48
  (41 shorter events, 4.7 us)
Async XLA Ops:
  0.6 9.7 %collective-permute-start = (bf16[4,1024]{1,0:T(4,128)(2,1)}, bf16[4,1024]{1,0:T(4,128)(2,1)S(1)}, u32[]{:S(2)}, u32[]{:S(2)}) collective-permute-start(bf16[4,1024]{1,0:T(4,128)(2,1)} %refs_0_.3), channel_id=1, source_target_pairs={{0,4},{4,8},{8,12},{12,0},{1,5},{5,9},{9,13},{13,1},{2,6},{6,10},{... | collective-permute-start | bytes 24584 | tf_op jit(solution)/shard_map/ppermute | solution.py:37
  2.8 7.6 %collective-permute-start.1 = (bf16[4,1024]{1,0:T(4,128)(2,1)}, bf16[4,1024]{1,0:T(4,128)(2,1)S(1)}, u32[]{:S(2)}, u32[]{:S(2)}) collective-permute-start(bf16[4,1024]{1,0:T(4,128)(2,1)} %refs_0_.3), channel_id=1, source_target_pairs={{0,8},{4,12},{8,0},{12,4},{1,9},{5,13},{9,1},{13,5},{2,10},{6,14},... | collective-permute-start | bytes 24584 | tf_op jit(solution)/shard_map/ppermute | solution.py:37
  5.1 5.3 %collective-permute-start.2 = (bf16[4,1024]{1,0:T(4,128)(2,1)}, bf16[4,1024]{1,0:T(4,128)(2,1)S(1)}, u32[]{:S(2)}, u32[]{:S(2)}) collective-permute-start(bf16[4,1024]{1,0:T(4,128)(2,1)} %refs_0_.3), channel_id=1, source_target_pairs={{0,12},{4,0},{8,4},{12,8},{1,13},{5,1},{9,5},{13,9},{2,14},{6,2},{... | collective-permute-start | bytes 24584 | tf_op jit(solution)/shard_map/ppermute | solution.py:37
  6.2 4.2 %copy-start.2 = (s32[16]{0:T(128)S(1)}, s32[16]{0:T(128)}, u32[]{:S(2)}) copy-start(s32[16]{0:T(128)} %refs_0_.4) | copy-start | bytes 196
  6.2 4.2 %copy-start.3 = (s32[16]{0:T(128)S(1)}, s32[16]{0:T(128)}, u32[]{:S(2)}) copy-start(s32[16]{0:T(128)} %refs_1_.4) | copy-start | bytes 196
  13.2 7.4 %collective-permute-start.3 = (bf16[144,128]{1,0:T(8,128)(2,1)S(1)}, bf16[144,128]{1,0:T(8,128)(2,1)S(1)}, u32[]{:S(2)}, u32[]{:S(2)}) collective-permute-start(bf16[144,128]{1,0:T(8,128)(2,1)S(1)} %get-tuple-element.37.refs_5_.refs_0_), channel_id=1, source_target_pairs={{0,4},{4,8},{8,12},{12,0},{1,5},{5,9},{9,13},{13,1},{2,6},{6,10},{... | collective-permute-start | bytes 110600 | tf_op jit(solution)/shard_map/ppermute | solution.py:37
  13.6 7.0 %collective-permute-start.4 = (bf16[144,128]{1,0:T(8,128)(2,1)S(1)}, bf16[144,128]{1,0:T(8,128)(2,1)S(1)}, u32[]{:S(2)}, u32[]{:S(2)}) collective-permute-start(bf16[144,128]{1,0:T(8,128)(2,1)S(1)} %get-tuple-element.37.refs_5_.refs_0_), channel_id=1, source_target_pairs={{0,8},{4,12},{8,0},{12,4},{1,9},{5,13},{9,1},{13,5},{2,10},{6,14},... | collective-permute-start | bytes 110600 | tf_op jit(solution)/shard_map/ppermute | solution.py:37
  13.8 6.8 %collective-permute-start.5 = (bf16[144,128]{1,0:T(8,128)(2,1)S(1)}, bf16[144,128]{1,0:T(8,128)(2,1)S(1)}, u32[]{:S(2)}, u32[]{:S(2)}) collective-permute-start(bf16[144,128]{1,0:T(8,128)(2,1)S(1)} %get-tuple-element.37.refs_5_.refs_0_), channel_id=1, source_target_pairs={{0,12},{4,0},{8,4},{12,8},{1,13},{5,1},{9,5},{13,9},{2,14},{6,2},{... | collective-permute-start | bytes 110600 | tf_op jit(solution)/shard_map/ppermute | solution.py:37
  20.6 11.0 %slice-start = ((s8[16777216]{0:T(1024)(128)(4,1)}), s8[4194304]{0:T(1024)(128)(4,1)S(1)}, s32[]{:S(2)}) async-start(s8[16777216]{0:T(1024)(128)(4,1)} %bitcast.7), calls=%async_computation | async-start | bytes 8388608
  20.6 10.9 %slice-start.1 = ((s8[16777216]{0:T(1024)(128)(4,1)}), s8[4194304]{0:T(1024)(128)(4,1)S(1)}, s32[]{:S(2)}) async-start(s8[16777216]{0:T(1024)(128)(4,1)} %bitcast.7), calls=%async_computation.1 | async-start | bytes 8388608
  20.6 10.9 %slice-start.2 = ((s8[16777216]{0:T(1024)(128)(4,1)}), s8[4194304]{0:T(1024)(128)(4,1)S(1)}, s32[]{:S(2)}) async-start(s8[16777216]{0:T(1024)(128)(4,1)} %bitcast.7), calls=%async_computation.2 | async-start | bytes 8388608
  20.7 10.9 %slice-start.3 = ((s8[16777216]{0:T(1024)(128)(4,1)}), s8[4194304]{0:T(1024)(128)(4,1)S(1)}, s32[]{:S(2)}) async-start(s8[16777216]{0:T(1024)(128)(4,1)} %bitcast.7), calls=%async_computation.3 | async-start | bytes 8388608
  21.4 4.2 %collective-permute-start.6 = (bf16[16,1024]{1,0:T(8,128)(2,1)S(1)}, bf16[16,1024]{1,0:T(8,128)(2,1)S(1)}, u32[]{:S(2)}, u32[]{:S(2)}) collective-permute-start(bf16[16,1024]{1,0:T(8,128)(2,1)S(1)} %project.1.refs_0_), channel_id=1, source_target_pairs={{0,1},{1,2},{2,3},{3,0},{4,5},{5,6},{6,7},{7,4},{8,9},{9,10},{10,1... | collective-permute-start | bytes 98312 | tf_op jit(solution)/shard_map/ppermute | solution.py:37
  24.6 2.8 %collective-permute-start.7 = (bf16[16,1024]{1,0:T(8,128)(2,1)S(1)}, bf16[16,1024]{1,0:T(8,128)(2,1)S(1)}, u32[]{:S(2)}, u32[]{:S(2)}) collective-permute-start(bf16[16,1024]{1,0:T(8,128)(2,1)S(1)} %project.1.refs_0_), channel_id=1, source_target_pairs={{0,2},{1,3},{2,0},{3,1},{4,6},{5,7},{6,4},{7,5},{8,10},{9,11},{10,... | collective-permute-start | bytes 98312 | tf_op jit(solution)/shard_map/ppermute | solution.py:37
  24.9 3.3 %collective-permute-start.8 = (bf16[16,1024]{1,0:T(8,128)(2,1)S(1)}, bf16[16,1024]{1,0:T(8,128)(2,1)S(1)}, u32[]{:S(2)}, u32[]{:S(2)}) collective-permute-start(bf16[16,1024]{1,0:T(8,128)(2,1)S(1)} %project.1.refs_0_), channel_id=1, source_target_pairs={{0,3},{1,0},{2,1},{3,2},{4,7},{5,4},{6,5},{7,6},{8,11},{9,8},{10,9... | collective-permute-start | bytes 98312 | tf_op jit(solution)/shard_map/ppermute | solution.py:37
  28.4 5.4 %collective-permute-start.11 = (bf16[16,1152]{1,0:T(8,128)(2,1)S(1)}, bf16[16,1152]{1,0:T(8,128)(2,1)S(1)}, u32[]{:S(2)}, u32[]{:S(2)}) collective-permute-start(bf16[16,1152]{1,0:T(8,128)(2,1)S(1)} %get-tuple-element.42.refs_0_), channel_id=1, source_target_pairs={{0,12},{4,0},{8,4},{12,8},{1,13},{5,1},{9,5},{13,9},{2,14},{6,2},{... | collective-permute-start | bytes 110600 | tf_op jit(solution)/shard_map/ppermute | solution.py:37
  29.7 6.4 %collective-permute-start.10 = (bf16[16,1152]{1,0:T(8,128)(2,1)S(1)}, bf16[16,1152]{1,0:T(8,128)(2,1)S(1)}, u32[]{:S(2)}, u32[]{:S(2)}) collective-permute-start(bf16[16,1152]{1,0:T(8,128)(2,1)S(1)} %get-tuple-element.42.refs_0_), channel_id=1, source_target_pairs={{0,8},{4,12},{8,0},{12,4},{1,9},{5,13},{9,1},{13,5},{2,10},{6,14},... | collective-permute-start | bytes 110600 | tf_op jit(solution)/shard_map/ppermute | solution.py:37
  30.2 7.1 %collective-permute-start.9 = (bf16[16,1152]{1,0:T(8,128)(2,1)S(1)}, bf16[16,1152]{1,0:T(8,128)(2,1)S(1)}, u32[]{:S(2)}, u32[]{:S(2)}) collective-permute-start(bf16[16,1152]{1,0:T(8,128)(2,1)S(1)} %get-tuple-element.42.refs_0_), channel_id=1, source_target_pairs={{0,4},{4,8},{8,12},{12,0},{1,5},{5,9},{9,13},{13,1},{2,6},{6,10},{... | collective-permute-start | bytes 110600 | tf_op jit(solution)/shard_map/ppermute | solution.py:37
  40.8 4.7 %collective-permute-start.12 = (bf16[16,1024]{1,0:T(8,128)(2,1)S(1)}, bf16[16,1024]{1,0:T(8,128)(2,1)S(1)}, u32[]{:S(2)}, u32[]{:S(2)}) collective-permute-start(bf16[16,1024]{1,0:T(8,128)(2,1)S(1)} %get-tuple-element.57), channel_id=1, source_target_pairs={{0,4},{4,8},{8,12},{12,0},{1,5},{5,9},{9,13},{13,1},{2,6},{6,10},{... | collective-permute-start | bytes 98312 | tf_op jit(solution)/shard_map/ppermute | solution.py:48
  41.6 4.4 %collective-permute-start.13 = (bf16[16,1024]{1,0:T(8,128)(2,1)S(1)}, bf16[16,1024]{1,0:T(8,128)(2,1)S(1)}, u32[]{:S(2)}, u32[]{:S(2)}) collective-permute-start(bf16[16,1024]{1,0:T(8,128)(2,1)S(1)} %get-tuple-element.58), channel_id=1, source_target_pairs={{0,8},{4,12},{8,0},{12,4},{1,9},{5,13},{9,1},{13,5},{2,10},{6,14},... | collective-permute-start | bytes 98312 | tf_op jit(solution)/shard_map/ppermute | solution.py:48
  43.0 3.0 %collective-permute-start.14 = (bf16[16,1024]{1,0:T(8,128)(2,1)S(1)}, bf16[16,1024]{1,0:T(8,128)(2,1)S(1)}, u32[]{:S(2)}, u32[]{:S(2)}) collective-permute-start(bf16[16,1024]{1,0:T(8,128)(2,1)S(1)} %get-tuple-element.59), channel_id=1, source_target_pairs={{0,12},{4,0},{8,4},{12,8},{1,13},{5,1},{9,5},{13,9},{2,14},{6,2},{... | collective-permute-start | bytes 98312 | tf_op jit(solution)/shard_map/ppermute | solution.py:48
  46.1 4.4 %collective-permute-start.15 = (bf16[4,1024]{1,0:T(4,128)(2,1)S(1)}, bf16[4,1024]{1,0:T(4,128)(2,1)S(1)}, u32[]{:S(2)}, u32[]{:S(2)}) collective-permute-start(bf16[4,1024]{1,0:T(4,128)(2,1)S(1)} %get-tuple-element.61), channel_id=1, source_target_pairs={{0,1},{1,2},{2,3},{3,0},{4,5},{5,6},{6,7},{7,4},{8,9},{9,10},{10,1... | collective-permute-start | bytes 24584 | tf_op jit(solution)/shard_map/ppermute | solution.py:48
  49.2 2.6 %collective-permute-start.16 = (bf16[4,1024]{1,0:T(4,128)(2,1)S(1)}, bf16[4,1024]{1,0:T(4,128)(2,1)S(1)}, u32[]{:S(2)}, u32[]{:S(2)}) collective-permute-start(bf16[4,1024]{1,0:T(4,128)(2,1)S(1)} %get-tuple-element.62), channel_id=1, source_target_pairs={{0,2},{1,3},{2,0},{3,1},{4,6},{5,7},{6,4},{7,5},{8,10},{9,11},{10,... | collective-permute-start | bytes 24584 | tf_op jit(solution)/shard_map/ppermute | solution.py:48
  49.8 3.1 %collective-permute-start.17 = (bf16[4,1024]{1,0:T(4,128)(2,1)S(1)}, bf16[4,1024]{1,0:T(4,128)(2,1)S(1)}, u32[]{:S(2)}, u32[]{:S(2)}) collective-permute-start(bf16[4,1024]{1,0:T(4,128)(2,1)S(1)} %get-tuple-element.63), channel_id=1, source_target_pairs={{0,3},{1,0},{2,1},{3,2},{4,7},{5,4},{6,5},{7,6},{8,11},{9,8},{10,9... | collective-permute-start | bytes 24584 | tf_op jit(solution)/shard_map/ppermute | solution.py:48
  (2 other events, 2.5 us)

commit v6 on v5

--- a/solution.py
+++ b/solution.py
@@ -20,6 +20,7 @@
 MOST_PERMUTES = 4
 CHUNKS = 4
 TILE = 512
+EXPERTS_MIB = 4
 
 BF = jnp.bfloat16
 F32 = jnp.float32
@@ -110,39 +111,13 @@
     return (array, cut, (step, array.shape[1]))
 
 
-def with_copy(copies, work):
-    for copy in copies:
-        copy.start()
-    pl.when(lax.axis_index("expert") >= 0)(work)
-    for copy in copies:
-        copy.wait()
-
-
-def attend_kernel(count, own_rows, kv_heads, group, positions, cut, *refs):
+def attend_kernel(count, own_rows, kv_heads, group, positions, *refs):
     taken = grouped(count)
     slot_ref, length_ref = refs[0], refs[1]
     query_refs = refs[2 : 2 + taken]
     new_ref = refs[2 + taken]
     cache_refs = refs[3 + taken : 3 + taken + kv_heads]
-    refs = refs[3 + taken + kv_heads :]
-    attend_body = functools.partial(
-        attend_block,
-        (count, own_rows, kv_heads, group, positions),
-        (slot_ref, length_ref, query_refs, new_ref, cache_refs),
-    )
-    if cut is None:
-        attend_body(*refs)
-        return
-    chunk_hbm, out_ref, chunk_ref, *scratch, chunk_sem = refs
-    with_copy(
-        [pltpu.make_async_copy(chunk_hbm.at[cut()], chunk_ref, chunk_sem)],
-        lambda: attend_body(out_ref, *scratch),
-    )
-
-
-def attend_block(sizes, inputs, out_ref, q_rows, score, acc, fresh):
-    count, own_rows, kv_heads, group, positions = sizes
-    slot_ref, length_ref, query_refs, new_ref, cache_refs = inputs
+    out_ref, q_rows, score, acc, fresh = refs[3 + taken + kv_heads :]
     me = lax.axis_index("expert")
     heads = kv_heads * group
     total = count * own_rows
@@ -232,36 +207,28 @@
         out_ref[rows + part * STATS : rows + (part + 1) * STATS, :] = turned[0:STATS, :].astype(BF)
 
 
-def attend(slot_of, lengths, queries, new_kv, caches, chunk, count):
+def attend(slot_of, lengths, queries, new_kv, caches, count):
     own_rows, _, kv_width = new_kv.shape
     kv_heads = kv_width // HD
     group = HEADS // KVH
     heads = kv_heads * group
     positions = caches[0].shape[1] // 2
     rows = count * own_rows * heads
-    out_shape = [pltpu.VMEM((rows + STATS * (rows // LANES), LANES), BF)]
-    scratch_shapes = [
-        pltpu.VMEM((count, own_rows * heads, HD), F32),
-        pltpu.VMEM((rows, 2 * positions), F32),
-        pltpu.VMEM((rows, HD), F32),
-        pltpu.VMEM((2, own_rows * heads, HD), F32),
-    ]
-    cut, more = None, []
-    if chunk is not None:
-        array, cut, shape = chunk
-        more = [pltpu.with_memory_space_constraint(array, pltpu.HBM)]
-        out_shape.append(pltpu.VMEM(shape, BF))
-        scratch_shapes.append(pltpu.SemaphoreType.DMA)
-    return pl.pallas_call(
-        functools.partial(attend_kernel, count, own_rows, kv_heads, group, positions, cut),
+    return pl.pallas_call(
+        functools.partial(attend_kernel, count, own_rows, kv_heads, group, positions),
         name="attend",
-        out_shape=tuple(out_shape),
-        in_specs=[SMEM, SMEM] + [VMEM] * (len(queries) + 1 + kv_heads) + [HBM] * len(more),
-        out_specs=tuple([VMEM] * len(out_shape)),
-        scratch_shapes=scratch_shapes,
+        out_shape=pltpu.VMEM((rows + STATS * (rows // LANES), LANES), BF),
+        in_specs=[SMEM, SMEM] + [VMEM] * (len(queries) + 1 + kv_heads),
+        out_specs=VMEM,
+        scratch_shapes=[
+            pltpu.VMEM((count, own_rows * heads, HD), F32),
+            pltpu.VMEM((rows, 2 * positions), F32),
+            pltpu.VMEM((rows, HD), F32),
+            pltpu.VMEM((2, own_rows * heads, HD), F32),
+        ],
         compiler_params=pltpu.CompilerParams(vmem_limit_bytes=6 << 20),
         cost_estimate=pl.CostEstimate(flops=10**8, bytes_accessed=1000, transcendentals=0),
-    )(slot_of, lengths, *queries, new_kv, *caches, *more)
+    )(slot_of, lengths, *queries, new_kv, *caches)
 
 
 def project_kernel(count, rows, heads, *refs):
@@ -357,48 +324,24 @@
     return [slice(i, i + step) for i in range(0, width, step)]
 
 
-def product_kernel(shift, count, cut, *refs):
-    block_ref, gate_ref, up_ref, refs = *refs[:3], refs[3:]
-    sums, refs = (refs[:2], refs[2:]) if shift else ((), refs)
-    step = gate_ref.shape[0]
-    at, _ = rows_at(shift, count, step, True)
-
-    def work(gate_out, up_out):
-        block = block_ref[:, 0:step]
-        for columns in tiles(gate_ref.shape[1]):
-            gate_made = jnp.dot(block, gate_ref[:, columns], preferred_element_type=F32)
-            up_made = jnp.dot(block, up_ref[at, columns], preferred_element_type=F32)
-            gate_out[:, columns] = gate_made + sums[0][:, columns] if sums else gate_made
-            up_out[:, columns] = up_made + sums[1][:, columns] if sums else up_made
-
-    if cut is None:
-        work(*refs)
-        return
-    chunk_hbm, gate_out, up_out, chunk_ref, sem = refs
-    with_copy(
-        [pltpu.make_async_copy(chunk_hbm.at[cut()], chunk_ref, sem)],
-        lambda: work(gate_out, up_out),
-    )
-
-
-def product(shift, count, block, gate, up, sums, chunk=None):
-    one = pltpu.VMEM((block.shape[0], gate.shape[1]), F32)
-    out_shape, scratch_shapes, cut, more = [one, one], [], None, []
-    if chunk is not None:
-        array, cut, shape = chunk
-        more = [pltpu.with_memory_space_constraint(array, pltpu.HBM)]
-        out_shape.append(pltpu.VMEM(shape, BF))
-        scratch_shapes.append(pltpu.SemaphoreType.DMA)
-    return pl.pallas_call(
-        functools.partial(product_kernel, shift, count, cut),
+def product_kernel(block_ref, gate_ref, *refs):
+    before, out_ref = refs[:-1], refs[-1]
+    block = block_ref[:, 0 : gate_ref.shape[0]]
+    for columns in tiles(gate_ref.shape[1]):
+        made = jnp.dot(block, gate_ref[:, columns], preferred_element_type=F32)
+        out_ref[:, columns] = made + before[0][:, columns] if before else made
+
+
+def product(block, gate, before):
+    return pl.pallas_call(
+        product_kernel,
         name="product",
-        out_shape=tuple(out_shape),
-        in_specs=[VMEM] * (3 + len(sums)) + [HBM] * len(more),
-        out_specs=tuple([VMEM] * len(out_shape)),
-        scratch_shapes=scratch_shapes,
-        compiler_params=pltpu.CompilerParams(vmem_limit_bytes=6 << 20),
+        out_shape=pltpu.VMEM((block.shape[0], gate.shape[1]), F32),
+        in_specs=[VMEM] * (2 + len(before)),
+        out_specs=VMEM,
+        compiler_params=pltpu.CompilerParams(vmem_limit_bytes=2 << 20),
         cost_estimate=pl.CostEstimate(flops=10**8, bytes_accessed=1000, transcendentals=0),
-    )(block, gate, up, *sums, *more)
+    )(block, gate, *before)
 
 
 def routing(ids_ref, logits_ref, mine, rows):
@@ -427,80 +370,55 @@
     return (gate_sum / (1.0 + jnp.exp(-gate_sum)) * (up_sum * inverse)).astype(BF)
 
 
-def experts_kernel(count, sharing, last, cut, *refs):
+def experts_kernel(count, holders, sharing, last, *refs):
     part_refs, refs = refs[:count], refs[count:]
-    ids_ref, logits_ref, gate_ref, up_ref, gate_sum_ref, up_sum_ref, refs = *refs[:6], refs[6:]
-    down_refs, down_hbm, refs = refs[: count - 1], refs[count - 1], refs[count:]
-    out_refs, refs = refs[:count], refs[count:]
-    act, made, mix_ref, last_down, sem = refs
+    ids_ref, logits_ref, gate_ref, sum_ref, up_ref, down_ref, *out_refs = refs
+    *out_refs, spread, act, made = out_refs
     me = lax.axis_index("expert")
-    rows, hidden_units = act.shape
-    width = gate_ref.shape[0]
-    step = last_down.shape[0]
-
-    def work():
-        mix_ref[...] = jnp.broadcast_to(
-            routing(ids_ref, logits_ref, me // sharing, rows), mix_ref.shape
-        )
-        inverse = inverse_rms([ref[...] for ref in part_refs], width, count * width)
-        block = part_refs[last][:, 0:width]
-        at, _ = rows_at(last, count, width, True)
-        for columns in tiles(hidden_units):
-            gate_sum = gate_sum_ref[:, columns] + jnp.dot(
-                block, gate_ref[:, columns], preferred_element_type=F32
-            )
-            up_sum = up_sum_ref[:, columns] + jnp.dot(
-                block, up_ref[at, columns], preferred_element_type=F32
-            )
-            act[:, columns] = activate(gate_sum, up_sum, inverse)
-        for columns in tiles(count * width):
-            made[:, columns] = sum(
-                jnp.dot(
-                    act[:, c * step : (c + 1) * step], ref[:, columns], preferred_element_type=F32
-                )
-                for c, ref in enumerate(down_refs)
-            )
-
-    with_copy([pltpu.make_async_copy(down_hbm.at[cut()], last_down, sem)], work)
-    mix = mix_ref[:, 0:1]
+    rows, depth = spread.shape
+    width = depth // count
     for shift in range(count):
-        at = target(False, count, me, shift)
-        columns = pl.ds(pl.multiple_of(at * width, width), width)
-        total = made[:, columns] + jnp.dot(
-            act[:, hidden_units - step :], last_down[:, columns], preferred_element_type=F32
-        )
-        out_refs[shift][...] = (total * mix).astype(BF)
-
-
-def experts(last, parts, ids, logits, gate, up, sums, downs, down_last, count):
-    rows, hidden_units = sums[0].shape
-    width = gate.shape[0]
-    array, cut, shape = down_last
-    return pl.pallas_call(
-        functools.partial(experts_kernel, count, count // EXPERTS, last, cut),
+        at = source(part_refs, count, me, shift)
+        spread[:, pl.ds(pl.multiple_of(at * width, width), width)] = part_refs[shift][:, 0:width]
+    mix = routing(ids_ref, logits_ref, me // sharing, rows)
+    inverse = inverse_rms([ref[...] for ref in part_refs], width, depth)
+    block = part_refs[last][:, 0:width]
+    for columns in tiles(act.shape[1]):
+        gate_sum = sum_ref[:, columns] + jnp.dot(
+            block, gate_ref[:, columns], preferred_element_type=F32
+        )
+        up_sum = jnp.dot(spread[...], up_ref[:, columns], preferred_element_type=F32)
+        act[:, columns] = activate(gate_sum, up_sum, inverse)
+    for columns in tiles(depth):
+        made[:, columns] = mix * jnp.dot(
+            act[...], down_ref[:, columns], preferred_element_type=F32
+        )
+    own = rows // holders
+    mine = lax.axis_index("tensor")
+    for shift in range(holders):
+        at = target(False, holders, mine, shift)
+        chosen = sum(
+            jnp.where(at == i, made[i * own : (i + 1) * own, :], 0.0) for i in range(holders)
+        )
+        out_refs[shift][...] = chosen.astype(BF)
+
+
+def experts(last, parts, ids, logits, gate, gate_sum, up, down, count, holders):
+    rows, (hidden_units, depth) = gate_sum.shape[0], down.shape
+    return pl.pallas_call(
+        functools.partial(experts_kernel, count, holders, count // EXPERTS, last),
         name="experts",
-        out_shape=tuple([pltpu.VMEM((rows, width), BF)] * count),
-        in_specs=[VMEM] * (len(parts) + 6 + len(downs)) + [HBM],
-        out_specs=tuple([VMEM] * count),
+        out_shape=tuple([pltpu.VMEM((rows // holders, depth), BF)] * holders),
+        in_specs=[VMEM] * (len(parts) + 6),
+        out_specs=tuple([VMEM] * holders),
         scratch_shapes=[
+            pltpu.VMEM((rows, depth), BF),
             pltpu.VMEM((rows, hidden_units), BF),
-            pltpu.VMEM((rows, count * width), F32),
-            pltpu.VMEM((rows, LANES), F32),
-            pltpu.VMEM(shape, BF),
-            pltpu.SemaphoreType.DMA,
+            pltpu.VMEM((rows, depth), F32),
         ],
-        compiler_params=pltpu.CompilerParams(vmem_limit_bytes=7 << 20),
+        compiler_params=pltpu.CompilerParams(vmem_limit_bytes=EXPERTS_MIB << 20),
         cost_estimate=pl.CostEstimate(flops=10**8, bytes_accessed=1000, transcendentals=0),
-    )(
-        *parts,
-        ids,
-        logits,
-        gate,
-        up,
-        *sums,
-        *downs,
-        pltpu.with_memory_space_constraint(array, pltpu.HBM),
-    )
+    )(*parts, ids, logits, gate, gate_sum, up, down)
 
 
 def all_experts_kernel(count, sharing, *refs):
@@ -549,6 +467,30 @@
             at = target(False, other, me, shift)
             chosen = sum(jnp.where(at == i, blocks[i], 0.0) for i in range(other))
             out_refs[shift][...] = chosen.astype(BF)
+
+
+def token_sum_kernel(count, other, *refs):
+    part_refs, out_refs, total = refs[:count], refs[count:-1], refs[-1]
+    me = lax.axis_index("expert")
+    total[...] = sum(ref[...].astype(F32) for ref in part_refs)
+    width = total.shape[1] // other
+    for shift in range(other):
+        at = target(False, other, me, shift)
+        columns = pl.ds(pl.multiple_of(at * width, width), width)
+        out_refs[shift][...] = total[:, columns].astype(BF)
+
+
+def token_sum(parts, count, other):
+    rows, depth = parts[0].shape
+    return pl.pallas_call(
+        functools.partial(token_sum_kernel, count, other),
+        name="first_sum",
+        out_shape=tuple([pltpu.VMEM((rows, depth // other), BF)] * other),
+        in_specs=[VMEM] * count,
+        out_specs=tuple([VMEM] * other),
+        scratch_shapes=[pltpu.VMEM((rows, depth), F32)],
+        compiler_params=pltpu.CompilerParams(vmem_limit_bytes=2 << 20),
+    )(*parts)
 
 
 def last_sum_kernel(count, *refs):
@@ -608,7 +550,6 @@
     split = len(queries) == expert_count == CHUNKS
     gate, up, down = gate_weight_slabs[0], w_up[0], w_down[0]
     gate_rows = [[rows_of(gate, i, CHUNKS, True)] if split else [] for i in range(CHUNKS)]
-    down_rows = [[rows_of(down, i, CHUNKS, False)] if split else [] for i in range(CHUNKS)]
     head_shape = (slots, positions, 2, HD)
     heads = [
         (kv_prefill, (slice(None), slice(None), slice(None), pl.ds(g * HD, HD)), head_shape)
@@ -621,50 +562,55 @@
     if split:
         queries[0] = own
     caches = [cache.reshape(slots, 2 * positions, HD) for cache in caches]
-    part, *second_gates = attend(
+    part = attend(
         slot_of,
         lengths,
         queries,
         fresh,
         caches,
-        gate_rows[2][0] if split else None,
         expert_count,
     )
     parts = gather(part, "expert")
     wo_here, resid_here, gain_here, *third = load(
-        [whole(wo), whole(resid), whole(norm_gain), *gate_rows[1], *down_rows[0]], [part]
+        [whole(wo), whole(resid), whole(norm_gain), *gate_rows[2], *gate_rows[1]], [part]
     )
     projected = project(parts, wo_here, expert_count, total)
     partials = gather(projected, "tensor")
     attention, scaled = residual(partials, resid_here, gain_here, tensor_count)
     blocks = gather(scaled, "expert")
     if split:
-        g_0, g_3, g_2, g_1, d_0 = *first_gates, *second_gates, *third
-        *sums, d_1 = product(0, CHUNKS, blocks[0], g_0, up, (), down_rows[1][0])
-        *sums, d_2 = product(3, CHUNKS, blocks[3], g_3, up, sums, down_rows[2][0])
-        sums = product(2, CHUNKS, blocks[2], g_2, up, sums)
+        g_0, g_3, g_2, g_1 = *first_gates, *third
+        gate_sum = product(blocks[0], g_0, ())
+        gate_sum = product(blocks[3], g_3, (gate_sum,))
+        gate_sum = product(blocks[2], g_2, (gate_sum,))
         outgoing = experts(
             1,
             blocks,
             expert_ids.T,
             gate_logits.T,
             g_1,
+            gate_sum,
             up,
-            sums,
-            (d_0, d_1, d_2),
-            down_rows[3][0],
+            down,
             CHUNKS,
+            tensor_count,
+        )
+        token_parts = token_sum(
+            exchange(outgoing, "tensor"), tensor_count, expert_count
+        )
+        moe_out = last_sum(
+            exchange(token_parts, "expert"), expert_count, (total // tensor_count, width)
         )
     else:
         outgoing = all_experts(
             blocks, expert_ids.T, gate_logits.T, gate, up, down, expert_count
         )
-    column_parts = first_sum(
-        exchange(outgoing, "expert"), expert_count, tensor_count, total, width
-    )
-    moe_out = last_sum(
-        exchange(column_parts, "tensor"), tensor_count, (total // tensor_count, width)
-    )
+        column_parts = first_sum(
+            exchange(outgoing, "expert"), expert_count, tensor_count, total, width
+        )
+        moe_out = last_sum(
+            exchange(column_parts, "tensor"), tensor_count, (total // tensor_count, width)
+        )
     return (attention, moe_out)
 
 

time: 53.7 us -> 51.9 us (0.966); the launches traced: 53.5 us -> 50.9 us
  Pallas kernels: 21.8 us -> 18.7 us
  waiting for transfers between devices: 7.49 us -> 8.34 us
    pallas_call x5, Pallas kernels: 9.22 us -> 7.07 us  [the longest x1 5.1 us: experts(): pl.pallas_call(functools.partial(experts_kernel, count, holders, count //...]
    pallas_call x1, Pallas kernels: 2.76 us -> 1.71 us  [attend(): pl.pallas_call(functools.partial(attend_kernel, count, own_rows, kv_heads...]
    ppermute x12, waiting for transfers between devices: 3.2 us -> 4.14 us  [gather(): lax.ppermute(value, axis, [(i, (i + shift) % count) for i in range(count)])]
    ppermute x12, starting transfers between devices: 15.7 us -> 14.8 us  [gather(): lax.ppermute(value, axis, [(i, (i + shift) % count) for i in range(count)])]
  transfers between devices with their start and end apart: 18 -> 18, of which waited for: 7 -> 10; matrix products, arithmetic and copies ran while one was open for 1% -> 1% of each run, Pallas kernels for 26% -> 20%
where the time goes in v6:
time: 51.9 us; the launch traced here: 50.9 us
  starting transfers between devices  22.3 us (43%)
  Pallas kernels  18.7 us (36%)
  waiting for transfers between devices  8.34 us (16%)
  between operations  0.87 us (2%)
  local copies, waits for them, and re-layouts  0.67 us (1%)
    ppermute x12, starting transfers between devices, gather(): lax.ppermute(value, axis, [(i, (i + shift) % count) for i in range(count)])  14.8 us
    pallas_call x2, Pallas kernels, load(): pl.pallas_call(functools.partial(load_kernel, [cut for _, cut, _ in items...  8.4 us
    ppermute x6, starting transfers between devices, exchange(): lax.ppermute(values[shift], axis, [(i, (i + shift) % count) for i in rang...  7.53 us
    pallas_call x1, Pallas kernels, experts(): pl.pallas_call(functools.partial(experts_kernel, count, holders, count //...  5.1 us
    ppermute x6, waiting for transfers between devices, exchange(): lax.ppermute(values[shift], axis, [(i, (i + shift) % count) for i in rang...  4.21 us
    ppermute x12, waiting for transfers between devices, gather(): lax.ppermute(value, axis, [(i, (i + shift) % count) for i in range(count)])  4.14 us
    pallas_call x3, Pallas kernels, product(): pl.pallas_call(product_kernel, name='product', out_shape=pltpu.VMEM((bloc...  1.95 us
    pallas_call x1, Pallas kernels, attend(): pl.pallas_call(functools.partial(attend_kernel, count, own_rows, kv_heads...  1.71 us
  transfers between devices with their start and end apart: 18, of which 10 were waited for; matrix products, arithmetic and copies ran while one was open for 1% of the time, Pallas kernels for 20%

profile of v6, /device:TPU:1, one launch (start us, length us, event | category | flops | bytes accessed | tf_op | source)
XLA Modules:
  0.0 50.9 jit_solution(6540557864728254313)
XLA Ops:
  0.6 2.2 %collective-permute-start = (bf16[4,1024]{1,0:T(4,128)(2,1)}, bf16[4,1024]{1,0:T(4,128)(2,1)S(1)}, u32[]{:S(2)}, u32[]{:S(2)}) collective-permute-start(bf16[4,1024]{1,0:T(4,128)(2,1)} %refs_0_.3), channel_id=1, source_target_pairs={{0,4},{4,8},{8,12},{12,0},{1,5},{5,9},{9,13},{13,1},{2,6},{6,10},{... | collective-permute-start | bytes 24584 | tf_op jit(solution)/shard_map/ppermute | solution.py:38
  2.8 2.1 %collective-permute-start.2 = (bf16[4,1024]{1,0:T(4,128)(2,1)}, bf16[4,1024]{1,0:T(4,128)(2,1)S(1)}, u32[]{:S(2)}, u32[]{:S(2)}) collective-permute-start(bf16[4,1024]{1,0:T(4,128)(2,1)} %refs_0_.3), channel_id=1, source_target_pairs={{0,12},{4,0},{8,4},{12,8},{1,13},{5,1},{9,5},{13,9},{2,14},{6,2},{... | collective-permute-start | bytes 24584 | tf_op jit(solution)/shard_map/ppermute | solution.py:38
  5.3 4.1 %load.2 = (bf16[4,1024]{1,0:T(4,128)(2,1)S(1)}, bf16[4,2,256]{2,1,0:T(2,128)(2,1)S(1)}, bf16[16,128,2,128]{3,2,1,0:T(2,128)(2,1)S(1)}, bf16[16,128,2,128]{3,2,1,...) custom-call(bf16[4,1024]{1,0:T(4,128)(2,1)} %refs_0_.3, bf16[4,2,256]{2,1,0:T(2,128)(2,1)} %refs_1_.3, ...), custom_call_target="tpu_custom_call" | custom-call | flops 100000000 | bytes 1000 | tf_op jit(solution)/shard_map/load/pallas_call | solution.py:85
  9.5 1.7 %attend.1.refs_5_.refs_0_ = bf16[144,128]{1,0:T(8,128)(2,1)S(1)} custom-call(s32[16]{0:T(128)S(1)} %copy-done.2, s32[16]{0:T(128)S(1)} %copy-done.3, bf16[4,1024]{1,0:T(4,128)(2,1)S(1)} %get-tuple-element.23.refs_2_, bf16[4,1024]{1,0:T(4,128)(2,1)S(1)} %collective-permute-done.refs_3_, bf16[4,1024]{1,0:T(4,128)(2,1)S(1)} %collective-permute-done.1.refs_4_, ...), custom_call_target="tpu_custom_call" | custom-call | flops 100000000 | bytes 1000 | tf_op jit(solution)/shard_map/attend/pallas_call | solution.py:217
  11.2 1.1 %collective-permute-start.5 = (bf16[144,128]{1,0:T(8,128)(2,1)S(1)}, bf16[144,128]{1,0:T(8,128)(2,1)S(1)}, u32[]{:S(2)}, u32[]{:S(2)}) collective-permute-start(bf16[144,128]{1,0:T(8,128)(2,1)S(1)} %attend.1.refs_5_.refs_0_), channel_id=1, source_target_pairs={{0,12},{4,0},{8,4},{12,8},{1,13},{5,1},{9,5},{13,9},{2,14},{6,2},{... | collective-permute-start | bytes 110600 | tf_op jit(solution)/shard_map/ppermute | solution.py:38
  12.3 1.4 %collective-permute-start.4 = (bf16[144,128]{1,0:T(8,128)(2,1)S(1)}, bf16[144,128]{1,0:T(8,128)(2,1)S(1)}, u32[]{:S(2)}, u32[]{:S(2)}) collective-permute-start(bf16[144,128]{1,0:T(8,128)(2,1)S(1)} %attend.1.refs_5_.refs_0_), channel_id=1, source_target_pairs={{0,8},{4,12},{8,0},{12,4},{1,9},{5,13},{9,1},{13,5},{2,10},{6,14},... | collective-permute-start | bytes 110600 | tf_op jit(solution)/shard_map/ppermute | solution.py:38
  13.7 1.0 %collective-permute-start.3 = (bf16[144,128]{1,0:T(8,128)(2,1)S(1)}, bf16[144,128]{1,0:T(8,128)(2,1)S(1)}, u32[]{:S(2)}, u32[]{:S(2)}) collective-permute-start(bf16[144,128]{1,0:T(8,128)(2,1)S(1)} %attend.1.refs_5_.refs_0_), channel_id=1, source_target_pairs={{0,4},{4,8},{8,12},{12,0},{1,5},{5,9},{9,13},{13,1},{2,6},{6,10},{... | collective-permute-start | bytes 110600 | tf_op jit(solution)/shard_map/ppermute | solution.py:38
  14.7 4.3 %load.3 = (bf16[1024,1024]{1,0:T(8,128)(2,1)S(1)}, bf16[16,1024]{1,0:T(8,128)(2,1)S(1)}, bf16[1024]{0:T(1024)(128)(2,1)S(1)}, bf16[1024,2048]{1,0:T(8,128)(2,1)S(1)}, bf16[1024,2048]{1,0:T(8,128)(2,1)S(1)}) custom-call(bf16[1024,1024]{1,0:T(8,128)(2,1)} %refs_0_.5, bf16[16,1024]{1,0:T(8,128)(2,1)} %refs_1_.5, bf16[1024]{0:T(1024)(128)(2,1)} %refs_2_.3, ...), custom_call_target="tpu_custom_call" | custom-call | flops 100000000 | bytes 1000 | tf_op jit(solution)/shard_map/load/pallas_call | solution.py:85
  19.0 0.8 %project.1.refs_0_ = bf16[16,1024]{1,0:T(8,128)(2,1)S(1)} custom-call(bf16[144,128]{1,0:T(8,128)(2,1)S(1)} %attend.1.refs_5_.refs_0_, bf16[144,128]{1,0:T(8,128)(2,1)S(1)} %collective-permute-done.3.refs_1_, bf16[144,128]{1,0:T(8,128)(2,1)S(1)} %collective-permute-done.4.refs_2_, bf16[144,128]{1,0:T(8,128)(2,1)S(1)} %collective-permute-done.5.refs_3_, ...), custom_call_target="tpu_custom_call" | custom-call | flops 99999997952 | bytes 1000 | tf_op jit(solution)/shard_map/project/pallas_call | solution.py:267
  19.8 2.5 %collective-permute-start.8 = (bf16[16,1024]{1,0:T(8,128)(2,1)S(1)}, bf16[16,1024]{1,0:T(8,128)(2,1)S(1)}, u32[]{:S(2)}, u32[]{:S(2)}) collective-permute-start(bf16[16,1024]{1,0:T(8,128)(2,1)S(1)} %project.1.refs_0_), channel_id=1, source_target_pairs={{0,3},{1,0},{2,1},{3,2},{4,7},{5,4},{6,5},{7,6},{8,11},{9,8},{10,9... | collective-permute-start | bytes 98312 | tf_op jit(solution)/shard_map/ppermute | solution.py:38
  22.4 1.2 %collective-permute-start.7 = (bf16[16,1024]{1,0:T(8,128)(2,1)S(1)}, bf16[16,1024]{1,0:T(8,128)(2,1)S(1)}, u32[]{:S(2)}, u32[]{:S(2)}) collective-permute-start(bf16[16,1024]{1,0:T(8,128)(2,1)S(1)} %project.1.refs_0_), channel_id=1, source_target_pairs={{0,2},{1,3},{2,0},{3,1},{4,6},{5,7},{6,4},{7,5},{8,10},{9,11},{10,... | collective-permute-start | bytes 98312 | tf_op jit(solution)/shard_map/ppermute | solution.py:38
  24.0 1.3 %collective-permute-done.8.refs_3_ = bf16[16,1024]{1,0:T(8,128)(2,1)S(1)} collective-permute-done((bf16[16,1024]{1,0:T(8,128)(2,1)S(1)}, bf16[16,1024]{1,0:T(8,128)(2,1)S(1)}, u32[]{:S(2)}, u32[]{:S(2)}) %collective-permute-start.8) | collective-permute-done | bytes 32800 | tf_op jit(solution)/shard_map/ppermute | solution.py:38
  25.9 2.1 %collective-permute-start.11 = (bf16[16,1152]{1,0:T(8,128)(2,1)S(1)}, bf16[16,1152]{1,0:T(8,128)(2,1)S(1)}, u32[]{:S(2)}, u32[]{:S(2)}) collective-permute-start(bf16[16,1152]{1,0:T(8,128)(2,1)S(1)} %get-tuple-element.31.block_ref.refs_0_), channel_id=1, source_target_pairs={{0,12},{4,0},{8,4},{12,8},{1,13},{5,1},{9,5},{13,9},{2,14},{6,2},{... | collective-permute-start | bytes 110600 | tf_op jit(solution)/shard_map/ppermute | solution.py:38
  29.1 0.6 %product.4.refs_0_ = f32[16,2048]{1,0:T(8,128)S(1)} custom-call(bf16[16,1152]{1,0:T(8,128)(2,1)S(1)} %collective-permute-done.11.block_ref.refs_3_, bf16[1024,2048]{1,0:T(8,128)(2,1)S(1)} %get-tuple-element.34.gate_ref, f32[16,2048]{1,0:T(8,128)S(1)} %product.3.refs_0_), custom_call_target="tpu_custom_call" | custom-call | flops 100000000 | bytes 1000 | tf_op jit(solution)/shard_map/product/pallas_call | solution.py:336
  29.8 2.0 %collective-permute-done.10.block_ref.refs_2_ = bf16[16,1152]{1,0:T(8,128)(2,1)S(1)} collective-permute-done((bf16[16,1152]{1,0:T(8,128)(2,1)S(1)}, bf16[16,1152]{1,0:T(8,128)(2,1)S(1)}, u32[]{:S(2)}, u32[]{:S(2)}) %collective-permute-start.10) | collective-permute-done | bytes 36896 | tf_op jit(solution)/shard_map/ppermute | solution.py:38
  31.7 0.6 %product.5.refs_7_ = f32[16,2048]{1,0:T(8,128)S(1)} custom-call(bf16[16,1152]{1,0:T(8,128)(2,1)S(1)} %collective-permute-done.10.block_ref.refs_2_, bf16[1024,2048]{1,0:T(8,128)(2,1)S(1)} %get-tuple-element.33.gate_ref, f32[16,2048]{1,0:T(8,128)S(1)} %product.4.refs_0_), custom_call_target="tpu_custom_call" | custom-call | flops 100000000 | bytes 1000 | tf_op jit(solution)/shard_map/product/pallas_call | solution.py:336
  32.8 5.1 %experts.1 = (bf16[4,4096]{1,0:T(4,128)(2,1)S(1)}, bf16[4,4096]{1,0:T(4,128)(2,1)S(1)}, bf16[4,4096]{1,0:T(4,128)(2,1)S(1)}, bf16[4,4096]{1,0:T(4,128)(2,1)S(1)}) custom-call(bf16[16,1152]{1,0:T(8,128)(2,1)S(1)} %get-tuple-element.31.block_ref.refs_0_, bf16[16,1152]{1,0:T(8,128)(2,1)S(1)} %collective-permute-done.9.refs_1_, ...), custom_call_target="tpu_custom_call" | custom-call | flops 100000000 | bytes 1000 | tf_op jit(solution)/shard_map/experts/pallas_call | solution.py:408
  37.9 3.4 %collective-permute-start.12 = (bf16[4,4096]{1,0:T(4,128)(2,1)S(1)}, bf16[4,4096]{1,0:T(4,128)(2,1)S(1)}, u32[]{:S(2)}, u32[]{:S(2)}) collective-permute-start(bf16[4,4096]{1,0:T(4,128)(2,1)S(1)} %get-tuple-element.37), channel_id=1, source_target_pairs={{0,1},{1,2},{2,3},{3,0},{4,5},{5,6},{6,7},{7,4},{8,9},{9,10},{10,1... | collective-permute-start | bytes 98312 | tf_op jit(solution)/shard_map/ppermute | solution.py:49
  41.3 0.9 %collective-permute-start.13 = (bf16[4,4096]{1,0:T(4,128)(2,1)S(1)}, bf16[4,4096]{1,0:T(4,128)(2,1)S(1)}, u32[]{:S(2)}, u32[]{:S(2)}) collective-permute-start(bf16[4,4096]{1,0:T(4,128)(2,1)S(1)} %get-tuple-element.38), channel_id=1, source_target_pairs={{0,2},{1,3},{2,0},{3,1},{4,6},{5,7},{6,4},{7,5},{8,10},{9,11},{10,... | collective-permute-start | bytes 98312 | tf_op jit(solution)/shard_map/ppermute | solution.py:49
  42.3 2.3 %collective-permute-done.13.refs_2_ = bf16[4,4096]{1,0:T(4,128)(2,1)S(1)} collective-permute-done((bf16[4,4096]{1,0:T(4,128)(2,1)S(1)}, bf16[4,4096]{1,0:T(4,128)(2,1)S(1)}, u32[]{:S(2)}, u32[]{:S(2)}) %collective-permute-start.13) | collective-permute-done | bytes 32800 | tf_op jit(solution)/shard_map/ppermute | solution.py:49
  44.6 0.8 %collective-permute-done.14.refs_3_ = bf16[4,4096]{1,0:T(4,128)(2,1)S(1)} collective-permute-done((bf16[4,4096]{1,0:T(4,128)(2,1)S(1)}, bf16[4,4096]{1,0:T(4,128)(2,1)S(1)}, u32[]{:S(2)}, u32[]{:S(2)}) %collective-permute-start.14) | collective-permute-done | bytes 32800 | tf_op jit(solution)/shard_map/ppermute | solution.py:49
  45.6 1.3 %collective-permute-start.16 = (bf16[4,1024]{1,0:T(4,128)(2,1)S(1)}, bf16[4,1024]{1,0:T(4,128)(2,1)S(1)}, u32[]{:S(2)}, u32[]{:S(2)}) collective-permute-start(bf16[4,1024]{1,0:T(4,128)(2,1)S(1)} %get-tuple-element.42), channel_id=1, source_target_pairs={{0,8},{4,12},{8,0},{12,4},{1,9},{5,13},{9,1},{13,5},{2,10},{6,14},... | collective-permute-start | bytes 24584 | tf_op jit(solution)/shard_map/ppermute | solution.py:49
  46.9 1.9 %collective-permute-start.17 = (bf16[4,1024]{1,0:T(4,128)(2,1)S(1)}, bf16[4,1024]{1,0:T(4,128)(2,1)S(1)}, u32[]{:S(2)}, u32[]{:S(2)}) collective-permute-start(bf16[4,1024]{1,0:T(4,128)(2,1)S(1)} %get-tuple-element.43), channel_id=1, source_target_pairs={{0,12},{4,0},{8,4},{12,8},{1,13},{5,1},{9,5},{13,9},{2,14},{6,2},{... | collective-permute-start | bytes 24584 | tf_op jit(solution)/shard_map/ppermute | solution.py:49
  49.4 0.7 %collective-permute-done.15.refs_1_ = bf16[4,1024]{1,0:T(4,128)(2,1)S(1)} collective-permute-done((bf16[4,1024]{1,0:T(4,128)(2,1)S(1)}, bf16[4,1024]{1,0:T(4,128)(2,1)S(1)}, u32[]{:S(2)}, u32[]{:S(2)}) %collective-permute-start.15) | collective-permute-done | bytes 8224 | tf_op jit(solution)/shard_map/ppermute | solution.py:49
  (50 shorter events, 4.5 us)
Async XLA Ops:
  0.6 8.8 %collective-permute-start = (bf16[4,1024]{1,0:T(4,128)(2,1)}, bf16[4,1024]{1,0:T(4,128)(2,1)S(1)}, u32[]{:S(2)}, u32[]{:S(2)}) collective-permute-start(bf16[4,1024]{1,0:T(4,128)(2,1)} %refs_0_.3), channel_id=1, source_target_pairs={{0,4},{4,8},{8,12},{12,0},{1,5},{5,9},{9,13},{13,1},{2,6},{6,10},{... | collective-permute-start | bytes 24584 | tf_op jit(solution)/shard_map/ppermute | solution.py:38
  2.8 6.7 %collective-permute-start.2 = (bf16[4,1024]{1,0:T(4,128)(2,1)}, bf16[4,1024]{1,0:T(4,128)(2,1)S(1)}, u32[]{:S(2)}, u32[]{:S(2)}) collective-permute-start(bf16[4,1024]{1,0:T(4,128)(2,1)} %refs_0_.3), channel_id=1, source_target_pairs={{0,12},{4,0},{8,4},{12,8},{1,13},{5,1},{9,5},{13,9},{2,14},{6,2},{... | collective-permute-start | bytes 24584 | tf_op jit(solution)/shard_map/ppermute | solution.py:38
  4.9 4.6 %collective-permute-start.1 = (bf16[4,1024]{1,0:T(4,128)(2,1)}, bf16[4,1024]{1,0:T(4,128)(2,1)S(1)}, u32[]{:S(2)}, u32[]{:S(2)}) collective-permute-start(bf16[4,1024]{1,0:T(4,128)(2,1)} %refs_0_.3), channel_id=1, source_target_pairs={{0,8},{4,12},{8,0},{12,4},{1,9},{5,13},{9,1},{13,5},{2,10},{6,14},... | collective-permute-start | bytes 24584 | tf_op jit(solution)/shard_map/ppermute | solution.py:38
  11.2 7.8 %collective-permute-start.5 = (bf16[144,128]{1,0:T(8,128)(2,1)S(1)}, bf16[144,128]{1,0:T(8,128)(2,1)S(1)}, u32[]{:S(2)}, u32[]{:S(2)}) collective-permute-start(bf16[144,128]{1,0:T(8,128)(2,1)S(1)} %attend.1.refs_5_.refs_0_), channel_id=1, source_target_pairs={{0,12},{4,0},{8,4},{12,8},{1,13},{5,1},{9,5},{13,9},{2,14},{6,2},{... | collective-permute-start | bytes 110600 | tf_op jit(solution)/shard_map/ppermute | solution.py:38
  12.3 6.7 %collective-permute-start.4 = (bf16[144,128]{1,0:T(8,128)(2,1)S(1)}, bf16[144,128]{1,0:T(8,128)(2,1)S(1)}, u32[]{:S(2)}, u32[]{:S(2)}) collective-permute-start(bf16[144,128]{1,0:T(8,128)(2,1)S(1)} %attend.1.refs_5_.refs_0_), channel_id=1, source_target_pairs={{0,8},{4,12},{8,0},{12,4},{1,9},{5,13},{9,1},{13,5},{2,10},{6,14},... | collective-permute-start | bytes 110600 | tf_op jit(solution)/shard_map/ppermute | solution.py:38
  13.7 5.3 %collective-permute-start.3 = (bf16[144,128]{1,0:T(8,128)(2,1)S(1)}, bf16[144,128]{1,0:T(8,128)(2,1)S(1)}, u32[]{:S(2)}, u32[]{:S(2)}) collective-permute-start(bf16[144,128]{1,0:T(8,128)(2,1)S(1)} %attend.1.refs_5_.refs_0_), channel_id=1, source_target_pairs={{0,4},{4,8},{8,12},{12,0},{1,5},{5,9},{9,13},{13,1},{2,6},{6,10},{... | collective-permute-start | bytes 110600 | tf_op jit(solution)/shard_map/ppermute | solution.py:38
  14.7 18.0 %slice-start = ((s8[16777216]{0:T(1024)(128)(4,1)}), s8[4194304]{0:T(1024)(128)(4,1)S(1)}, s32[]{:S(2)}) async-start(s8[16777216]{0:T(1024)(128)(4,1)} %bitcast.7), calls=%async_computation | async-start | bytes 8388608
  14.7 18.0 %slice-start.4 = ((s8[16777216]{0:T(1024)(128)(4,1)}), s8[4194304]{0:T(1024)(128)(4,1)S(1)}, s32[]{:S(2)}) async-start(s8[16777216]{0:T(1024)(128)(4,1)} %bitcast.10), calls=%async_computation.4 | async-start | bytes 8388608
  19.0 13.7 %slice-start.1 = ((s8[16777216]{0:T(1024)(128)(4,1)}), s8[4194304]{0:T(1024)(128)(4,1)S(1)}, s32[]{:S(2)}) async-start(s8[16777216]{0:T(1024)(128)(4,1)} %bitcast.7), calls=%async_computation.1 | async-start | bytes 8388608
  19.0 13.7 %slice-start.2 = ((s8[16777216]{0:T(1024)(128)(4,1)}), s8[4194304]{0:T(1024)(128)(4,1)S(1)}, s32[]{:S(2)}) async-start(s8[16777216]{0:T(1024)(128)(4,1)} %bitcast.7), calls=%async_computation.2 | async-start | bytes 8388608
  19.0 13.7 %slice-start.3 = ((s8[16777216]{0:T(1024)(128)(4,1)}), s8[4194304]{0:T(1024)(128)(4,1)S(1)}, s32[]{:S(2)}) async-start(s8[16777216]{0:T(1024)(128)(4,1)} %bitcast.7), calls=%async_computation.3 | async-start | bytes 8388608
  19.0 13.7 %slice-start.5 = ((s8[16777216]{0:T(1024)(128)(4,1)}), s8[4194304]{0:T(1024)(128)(4,1)S(1)}, s32[]{:S(2)}) async-start(s8[16777216]{0:T(1024)(128)(4,1)} %bitcast.10), calls=%async_computation.5 | async-start | bytes 8388608
  19.8 5.5 %collective-permute-start.8 = (bf16[16,1024]{1,0:T(8,128)(2,1)S(1)}, bf16[16,1024]{1,0:T(8,128)(2,1)S(1)}, u32[]{:S(2)}, u32[]{:S(2)}) collective-permute-start(bf16[16,1024]{1,0:T(8,128)(2,1)S(1)} %project.1.refs_0_), channel_id=1, source_target_pairs={{0,3},{1,0},{2,1},{3,2},{4,7},{5,4},{6,5},{7,6},{8,11},{9,8},{10,9... | collective-permute-start | bytes 98312 | tf_op jit(solution)/shard_map/ppermute | solution.py:38
  22.4 3.4 %collective-permute-start.7 = (bf16[16,1024]{1,0:T(8,128)(2,1)S(1)}, bf16[16,1024]{1,0:T(8,128)(2,1)S(1)}, u32[]{:S(2)}, u32[]{:S(2)}) collective-permute-start(bf16[16,1024]{1,0:T(8,128)(2,1)S(1)} %project.1.refs_0_), channel_id=1, source_target_pairs={{0,2},{1,3},{2,0},{3,1},{4,6},{5,7},{6,4},{7,5},{8,10},{9,11},{10,... | collective-permute-start | bytes 98312 | tf_op jit(solution)/shard_map/ppermute | solution.py:38
  23.6 2.2 %collective-permute-start.6 = (bf16[16,1024]{1,0:T(8,128)(2,1)S(1)}, bf16[16,1024]{1,0:T(8,128)(2,1)S(1)}, u32[]{:S(2)}, u32[]{:S(2)}) collective-permute-start(bf16[16,1024]{1,0:T(8,128)(2,1)S(1)} %project.1.refs_0_), channel_id=1, source_target_pairs={{0,1},{1,2},{2,3},{3,0},{4,5},{5,6},{6,7},{7,4},{8,9},{9,10},{10,1... | collective-permute-start | bytes 98312 | tf_op jit(solution)/shard_map/ppermute | solution.py:38
  25.9 3.2 %collective-permute-start.11 = (bf16[16,1152]{1,0:T(8,128)(2,1)S(1)}, bf16[16,1152]{1,0:T(8,128)(2,1)S(1)}, u32[]{:S(2)}, u32[]{:S(2)}) collective-permute-start(bf16[16,1152]{1,0:T(8,128)(2,1)S(1)} %get-tuple-element.31.block_ref.refs_0_), channel_id=1, source_target_pairs={{0,12},{4,0},{8,4},{12,8},{1,13},{5,1},{9,5},{13,9},{2,14},{6,2},{... | collective-permute-start | bytes 110600 | tf_op jit(solution)/shard_map/ppermute | solution.py:38
  28.0 3.7 %collective-permute-start.10 = (bf16[16,1152]{1,0:T(8,128)(2,1)S(1)}, bf16[16,1152]{1,0:T(8,128)(2,1)S(1)}, u32[]{:S(2)}, u32[]{:S(2)}) collective-permute-start(bf16[16,1152]{1,0:T(8,128)(2,1)S(1)} %get-tuple-element.31.block_ref.refs_0_), channel_id=1, source_target_pairs={{0,8},{4,12},{8,0},{12,4},{1,9},{5,13},{9,1},{13,5},{2,10},{6,14},... | collective-permute-start | bytes 110600 | tf_op jit(solution)/shard_map/ppermute | solution.py:38
  28.0 4.7 %collective-permute-start.9 = (bf16[16,1152]{1,0:T(8,128)(2,1)S(1)}, bf16[16,1152]{1,0:T(8,128)(2,1)S(1)}, u32[]{:S(2)}, u32[]{:S(2)}) collective-permute-start(bf16[16,1152]{1,0:T(8,128)(2,1)S(1)} %get-tuple-element.31.block_ref.refs_0_), channel_id=1, source_target_pairs={{0,4},{4,8},{8,12},{12,0},{1,5},{5,9},{9,13},{13,1},{2,6},{6,10},{... | collective-permute-start | bytes 110600 | tf_op jit(solution)/shard_map/ppermute | solution.py:38
  37.9 4.4 %collective-permute-start.12 = (bf16[4,4096]{1,0:T(4,128)(2,1)S(1)}, bf16[4,4096]{1,0:T(4,128)(2,1)S(1)}, u32[]{:S(2)}, u32[]{:S(2)}) collective-permute-start(bf16[4,4096]{1,0:T(4,128)(2,1)S(1)} %get-tuple-element.37), channel_id=1, source_target_pairs={{0,1},{1,2},{2,3},{3,0},{4,5},{5,6},{6,7},{7,4},{8,9},{9,10},{10,1... | collective-permute-start | bytes 98312 | tf_op jit(solution)/shard_map/ppermute | solution.py:49
  41.3 3.4 %collective-permute-start.13 = (bf16[4,4096]{1,0:T(4,128)(2,1)S(1)}, bf16[4,4096]{1,0:T(4,128)(2,1)S(1)}, u32[]{:S(2)}, u32[]{:S(2)}) collective-permute-start(bf16[4,4096]{1,0:T(4,128)(2,1)S(1)} %get-tuple-element.38), channel_id=1, source_target_pairs={{0,2},{1,3},{2,0},{3,1},{4,6},{5,7},{6,4},{7,5},{8,10},{9,11},{10,... | collective-permute-start | bytes 98312 | tf_op jit(solution)/shard_map/ppermute | solution.py:49
  42.1 3.3 %collective-permute-start.14 = (bf16[4,4096]{1,0:T(4,128)(2,1)S(1)}, bf16[4,4096]{1,0:T(4,128)(2,1)S(1)}, u32[]{:S(2)}, u32[]{:S(2)}) collective-permute-start(bf16[4,4096]{1,0:T(4,128)(2,1)S(1)} %get-tuple-element.39), channel_id=1, source_target_pairs={{0,3},{1,0},{2,1},{3,2},{4,7},{5,4},{6,5},{7,6},{8,11},{9,8},{10,9... | collective-permute-start | bytes 98312 | tf_op jit(solution)/shard_map/ppermute | solution.py:49
  45.5 4.7 %collective-permute-start.15 = (bf16[4,1024]{1,0:T(4,128)(2,1)S(1)}, bf16[4,1024]{1,0:T(4,128)(2,1)S(1)}, u32[]{:S(2)}, u32[]{:S(2)}) collective-permute-start(bf16[4,1024]{1,0:T(4,128)(2,1)S(1)} %get-tuple-element.41), channel_id=1, source_target_pairs={{0,4},{4,8},{8,12},{12,0},{1,5},{5,9},{9,13},{13,1},{2,6},{6,10},{... | collective-permute-start | bytes 24584 | tf_op jit(solution)/shard_map/ppermute | solution.py:49
  45.6 4.6 %collective-permute-start.16 = (bf16[4,1024]{1,0:T(4,128)(2,1)S(1)}, bf16[4,1024]{1,0:T(4,128)(2,1)S(1)}, u32[]{:S(2)}, u32[]{:S(2)}) collective-permute-start(bf16[4,1024]{1,0:T(4,128)(2,1)S(1)} %get-tuple-element.42), channel_id=1, source_target_pairs={{0,8},{4,12},{8,0},{12,4},{1,9},{5,13},{9,1},{13,5},{2,10},{6,14},... | collective-permute-start | bytes 24584 | tf_op jit(solution)/shard_map/ppermute | solution.py:49
  46.9 3.4 %collective-permute-start.17 = (bf16[4,1024]{1,0:T(4,128)(2,1)S(1)}, bf16[4,1024]{1,0:T(4,128)(2,1)S(1)}, u32[]{:S(2)}, u32[]{:S(2)}) collective-permute-start(bf16[4,1024]{1,0:T(4,128)(2,1)S(1)} %get-tuple-element.43), channel_id=1, source_target_pairs={{0,12},{4,0},{8,4},{12,8},{1,13},{5,1},{9,5},{13,9},{2,14},{6,2},{... | collective-permute-start | bytes 24584 | tf_op jit(solution)/shard_map/ppermute | solution.py:49
  (6 other events, 43.2 us)
